TPU v7x, 256 devices: a whole 4x4x8 slice. The times are simulated.
256 devices in a mesh: expert: 4 (over y), shard: 64 (over z, x, core).
Axes of the slice: x: 4, y: 4, z: 8, core: 2. Of those that a mesh axis runs over, the one named last changes fastest.
Arguments:
- gradient: bfloat16 [4, 2048, 28672], P('expert', 'shard'), may hold values from -16 to 16
- factor: float32 [4, 2048, 512], P('expert', 'shard'), may hold values from -2 to 2, as said below
- right_diag: float32 [4, 28672], P('expert', 'shard'), may hold values from 0.5 to 2
- counts: int32 [4], P('expert'), may hold values from 256 to 1023
Outputs:
- new_factor: float32 [4, 2048, 512], P('expert', 'shard')
- new_right: float32 [4, 28672], P('expert', 'shard')
Inputs may be any that keep to these rules, and one draw needn't show every extreme that they name: Every diagonal block of factor is upper triangular with a positive diagonal: in row r, entry j is zero for j < r % 512.
All inputs are finite; a program needn't handle non-finite values. Where the computation divides by a largest or mean magnitude, that divisor is 1e-20 or more.
Results may differ from a plain program's by a relative error of at most 0.002.
Values may be sent and summed in bfloat16 or wider, within the bound.
No kernel may reach another device: no remote copies, remote signals or barrier semaphores. Data moves between devices by JAX's collectives and lax.ppermute only.
A program may use at most 128 MiB of HBM per device.

v0:
```python
import jax
import jax.numpy as jnp
from jax import lax
from jax.sharding import Mesh
from jax.sharding import PartitionSpec as P

FF = 14336
SHARD = ("shard_0", "shard_1", "shard_2")


step_rate = 0.5
epsilon = 1e-06


def from_everyone(shard, axis):
    size = lax.axis_size(axis)
    return lax.all_to_all(
        jnp.broadcast_to(shard[None], (size, *shard.shape)), axis, 0, 0, tiled=True
    )


def of_everyone(shard, axis):
    everything = from_everyone(shard, axis)
    return jnp.sum(everything, axis=0)


def cut_along(shard, dim, size):
    before, after = (shard.shape[:dim], shard.shape[dim + 1 :])
    return jnp.moveaxis(shard.reshape(*before, size, -1, *after), dim, 0)


def laid_out(parts, dim):
    shape = list(parts.shape[1:])
    shape[dim] *= parts.shape[0]
    return jnp.moveaxis(parts, 0, dim).reshape(shape)


def moved_by_axis(parts, axes, sequence):
    inside = parts.shape[1:]
    out = parts.reshape(*(lax.axis_size(a) for a in axes), *inside)
    for k in sequence:
        out = lax.all_to_all(out, axes[k], k, k, tiled=True)
    return out.reshape(-1, *inside)


def two_step_exchange(shard, groups, sequence, split_dim, concat_dim):
    size = lax.axis_size(groups[0]) * lax.axis_size(groups[1])
    parts = cut_along(shard, split_dim, size)
    return laid_out(moved_by_axis(parts, groups, sequence), concat_dim)


def all_blocks(shard, axes, sequence):
    parts = shard[None]
    for k in sequence:
        parts = lax.all_gather(parts, axes[k], axis=0, tiled=True)
    held = [lax.axis_size(axes[k]) for k in reversed(sequence)]
    parts = parts.reshape(*held, *shard.shape)
    turned = sorted(range(len(sequence)), key=lambda place: sequence[len(sequence) - 1 - place])
    return parts.transpose(*turned, *range(len(sequence), parts.ndim)).reshape(-1, *shard.shape)


def gather_axes(shard, axes, sequence, dim):
    return laid_out(all_blocks(shard, axes, sequence), dim)


def sum_by_axis(so_far, axes):
    for axis in axes:
        so_far = lax.psum_scatter(so_far, axis, scatter_dimension=0, tiled=True)
    return so_far


def of_everyone_2(shard, axis):
    return from_everyone(shard, axis).max(axis=0)


def in_one(arrays, axis):
    ends = [0]
    for a in arrays:
        ends.append(ends[-1] + a.size)
    so_far = of_everyone_2(jnp.concatenate([a.ravel() for a in arrays]), axis)
    return tuple((so_far[b:e].reshape(a.shape) for a, b, e in zip(arrays, ends, ends[1:])))


def body(gradient, factor, right_diag, counts):
    local_experts = counts.shape[0]
    experts_all = local_experts * lax.axis_size("expert")
    token_sum = of_everyone(jnp.sum(counts), "expert")
    weight = experts_all * counts.astype(jnp.float32) / jnp.asarray(token_sum).astype(jnp.float32)
    squared = weight * weight
    columns = two_step_exchange(gradient, (("shard_0", "shard_1"), "shard_2"), (1, 0), 2, 1)
    own_rows = factor.shape[1]
    block = factor.shape[2]
    width = columns.shape[1]
    col_count = columns.shape[2]
    narrow = factor.astype(jnp.bfloat16)
    whole = gather_axes(narrow, SHARD, (1, 0, 2), 1)
    blocks = width // block
    left = whole.reshape((local_experts, blocks, block, block))
    right = columns.reshape((local_experts, blocks, block, col_count))
    raw = jnp.einsum("ebik,ebkc->ebic", left, right, preferred_element_type=jnp.float32)
    raw = raw.reshape((local_experts, width, col_count))
    image = (raw * right_diag[:, None, :]).astype(jnp.bfloat16)
    column_term = (
        squared[:, None] * jnp.sum(jnp.square(image.astype(jnp.float32)), axis=1) / width - 1.0
    )
    column_level = jnp.max(jnp.abs(column_term), axis=1)
    groups = own_rows * lax.axis_size(SHARD) // own_rows

    def one_group(group):
        begin = group * own_rows
        picked = lax.dynamic_slice_in_dim(image, begin, own_rows, 1)
        window = lax.dynamic_slice_in_dim(image, begin // block * block, block, 1)
        return jnp.einsum("eic,ejc->iej", picked, window, preferred_element_type=jnp.float32)

    parts = lax.map(one_group, jnp.arange(groups, dtype=jnp.int32))
    gram = sum_by_axis(
        parts.reshape((own_rows * lax.axis_size(SHARD), local_experts, block)), SHARD
    )
    gram = jnp.transpose(gram, (1, 0, 2)) * (squared / (2 * FF))[:, None, None]
    my_index = lax.axis_index(SHARD)
    first_row = my_index * own_rows
    row_place = (first_row + lax.broadcasted_iota(jnp.int32, (own_rows, block), 0)) % block
    col_place = lax.broadcasted_iota(jnp.int32, (own_rows, block), 1)
    identity = jnp.where(col_place == row_place, 1.0, 0.0).astype(jnp.float32)
    upper_part = jnp.where((col_place >= row_place)[None, :, :], gram - identity[None, :, :], 0.0)
    row_level = jnp.max(jnp.abs(upper_part), axis=(1, 2))
    row_peak, column_peak = in_one((row_level, column_level), SHARD)
    steps = (upper_part / (row_peak + epsilon)[:, None, None]).astype(jnp.bfloat16)
    diag_block = lax.dynamic_slice_in_dim(whole, first_row // block * block, block, 1)
    moved = jnp.einsum("eik,ekj->eij", steps, diag_block, preferred_element_type=jnp.float32)
    new_factor = factor - step_rate * moved
    new_right = right_diag - step_rate * column_term / (column_peak + epsilon)[:, None] * right_diag
    return (new_factor, new_right)


def solution(mesh):
    torus = Mesh(
        mesh.devices.reshape(mesh.shape["expert"], 8, 4, 2),
        ("expert", "shard_0", "shard_1", "shard_2"),
    )
    return jax.shard_map(
        body,
        mesh=torus,
        in_specs=(
            P("expert", SHARD, None),
            P("expert", SHARD, None),
            P("expert", SHARD),
            P("expert"),
        ),
        out_specs=(P("expert", SHARD, None), P("expert", SHARD)),
        check_vma=False,
    )
```

profile of v0, /device:TPU:1, one launch (start us, length us, event | category | flops | bytes accessed | tf_op | source)
XLA Modules:
  0.0 385.5 jit_solution(12259285968247481593)
XLA Ops:
  8.1 11.3 %all-gather = bf16[4,32,512]{2,1,0:T(8,128)(2,1)} all-gather(bf16[1,32,512]{2,1,0:T(8,128)(2,1)S(1)} %convert_element_type.51), channel_id=2, replica_groups=mesh['expert'=4,'shard_0'=8,'shard_1'=4,'shard_2'=2] {'shard_1'}, dimensions={0}, use_global_device_ids=true | all-gather | bytes 163840 | tf_op jit(solution)/shard_map/all_gather | solution.py:55
  19.4 3.6 reshape.312
  23.0 1.2 copy.38
  24.4 9.7 %all_to_all.22 = bf16[32,2,1,32,448]{4,3,0,2,1:T(8,128)(2,1)S(1)} all-to-all(bf16[32,2,1,32,448]{4,3,0,2,1:T(8,128)(2,1)S(1)} %copy.39), channel_id=1, replica_groups=mesh['expert'=4,'shard_0'=8,'shard_1'=4,'shard_2'=2] {'shard_2'}, dimensions={1} | all-to-all | bytes 3670016 | tf_op jit(solution)/shard_map/all_to_all | solution.py:42
  34.2 1.6 copy.40
  35.8 9.1 %all-to-all-start.1 = ((bf16[32,2,1,32,448]{4,3,1,2,0:T(8,128)(2,1)}), bf16[32,2,1,32,448]{4,3,1,2,0:T(8,128)(2,1)}, u32[]{:S(2)}, u32[]{:S(2)}) async-start(bf16[32,2,1,32,448]{4,3,1,2,0:T(8,128)(2,1)} %copy.40), calls=%async_computation.1 | async-start | bytes 4194304 | tf_op jit(solution)/shard_map/all_to_all | solution.py:42
  44.9 21.0 %all-gather.6.cloned.1.call-done = bf16[32,32,512]{2,1,0:T(8,128)(2,1)} async-done(((bf16[4,32,512]{2,1,0:T(8,128)(2,1)}), bf16[32,32,512]{2,1,0:T(8,128)(2,1)}) %all-gather.6.cloned.1.call-update) | async-done | bytes 1048592 | tf_op jit(solution)/shard_map/all_gather | solution.py:55
  66.1 22.5 %all-gather.8.cloned.1.call-done = bf16[64,32,512]{2,1,0:T(8,128)(2,1)} async-done(((bf16[32,32,512]{2,1,0:T(8,128)(2,1)}), bf16[64,32,512]{2,1,0:T(8,128)(2,1)}) %all-gather.8.cloned.1.call-update) | async-done | bytes 2097168 | tf_op jit(solution)/shard_map/all_gather | solution.py:55
  88.5 1.7 copy.37
  90.3 8.6 %all-to-all-done.1 = bf16[32,2,1,32,448]{4,3,1,2,0:T(8,128)(2,1)} async-done(((bf16[32,2,1,32,448]{4,3,1,2,0:T(8,128)(2,1)}), bf16[32,2,1,32,448]{4,3,1,2,0:T(8,128)(2,1)}, u32[]{:S(2)}, u32[]{:S(2)}) %all-to-all-start.1) | async-done | bytes 1835040 | tf_op jit(solution)/shard_map/all_to_all | solution.py:42
  98.9 2.9 multiply_reduce_fusion
  101.8 4.3 %copy.42 = f32[4,512,448]{1,0,2:T(4,128)} copy(f32[4,512,448]{1,2,0:T(8,128)S(1)} %get-tuple-element.92) | data formatting | bytes 7340032 | tf_op jit(solution)/shard_map/ebik,ebkc->ebic/dot_general | solution.py:100
  106.1 5.5 %reshape.315 = f32[1,2048,448]{1,2,0:T(8,128)} reshape(f32[4,512,448]{1,0,2:T(4,128)} %copy.42) | data formatting | bytes 7340032 | tf_op jit(solution)/shard_map/reshape | solution.py:101
  111.6 3.6 multiply_convert_fusion.1
  115.2 2.8 copy.43
  118.0 138.5 %while.12 = (s32[]{:T(128)}, f32[64,32,1,512]{3,1,2,0:T(8,128)}, s32[64]{0:T(128)S(1)}, bf16[1,2048,448]{2,1,0:T(8,128)(2,1)S(1)}, s32[]{:T(128)}, /*index=5*/s3...) while((s32[]{:T(128)}, f32[64,32,1,512]{3,1,2,0:T(8,128)}, ...), condition=%wide.region_1.0_spmd, body=%wide.region_0.0_spmd.sunk | while | flops 14680088 | bytes 623474 | solution.py:115
  121.4 0.9 fusion.36
  123.6 0.9 fusion.36
  134.4 0.9 fusion.36
  136.6 0.9 fusion.36
  143.1 0.9 fusion.36
  147.4 0.9 fusion.36
  149.6 0.9 fusion.36
  151.7 0.9 fusion.36
  158.2 0.9 fusion.36
  179.8 0.9 fusion.36
  186.3 0.9 fusion.36
  188.5 0.9 fusion.36
  197.1 0.9 fusion.36
  201.5 0.9 fusion.36
  208.0 0.9 fusion.36
  216.6 0.9 fusion.36
  218.8 0.9 fusion.36
  223.1 0.9 fusion.36
  231.8 0.9 fusion.36
  233.9 0.9 fusion.36
  238.3 0.9 fusion.36
  251.2 0.9 fusion.36
  255.6 0.9 fusion.36
  256.5 54.2 %reduce-scatter.4.cloned.1.call-done = f32[256,1,512]{2,0,1:T(8,128)} async-done(((f32[2048,1,512]{2,0,1:T(8,128)}), f32[256,1,512]{2,0,1:T(8,128)}) %reduce-scatter.4.cloned.1.call-update) | async-done | bytes 524304 | tf_op jit(solution)/shard_map/reduce_scatter | solution.py:68
  312.0 4.0 %all-to-all-start.2 = ((s32[4,1,1]{2,1,0:T(1,128)}), s32[4,1,1]{2,1,0:T(1,128)S(1)}, u32[]{:S(2)}, u32[]{:S(2)}) async-start(s32[4,1,1]{2,1,0:T(1,128)} %broadcast_in_dim.51), calls=%async_computation.5 | async-start | bytes 4096 | tf_op jit(solution)/shard_map/all_to_all | solution.py:17
  316.0 17.7 %reduce-scatter.6.cloned.1.call-done = f32[64,1,512]{2,0,1:T(8,128)} async-done(((f32[256,1,512]{2,0,1:T(8,128)}), f32[64,1,512]{2,0,1:T(8,128)}) %reduce-scatter.6.cloned.1.call-update) | async-done | bytes 131088 | tf_op jit(solution)/shard_map/reduce_scatter | solution.py:68
  335.7 16.1 %reduce-scatter.8.cloned.1.call-done = f32[32,1,512]{2,0,1:T(8,128)} async-done(((f32[64,1,512]{2,0,1:T(8,128)}), f32[32,1,512]{2,0,1:T(8,128)}) %reduce-scatter.8.cloned.1.call-update) | async-done | bytes 65552 | tf_op jit(solution)/shard_map/reduce_scatter | solution.py:68
  351.8 1.5 fusion.12
  353.4 1.3 pad_maximum_fusion
  355.3 9.9 %all-to-all-start.3 = ((f32[64,1,2]{2,1,0:T(1,128)}), f32[64,1,2]{2,1,0:T(1,128)S(1)}, u32[]{:S(2)}, u32[]{:S(2)}) async-start(f32[64,1,2]{2,1,0:T(1,128)} %broadcast_in_dim.56), calls=%async_computation.6 | async-start | bytes 65536 | tf_op jit(solution)/shard_map/all_to_all | solution.py:17
  365.2 9.3 %all-to-all-done.3 = f32[64,1,2]{2,1,0:T(1,128)S(1)} async-done(((f32[64,1,2]{2,1,0:T(1,128)}), f32[64,1,2]{2,1,0:T(1,128)S(1)}, u32[]{:S(2)}, u32[]{:S(2)}) %all-to-all-start.3) | async-done | bytes 544 | tf_op jit(solution)/shard_map/all_to_all | solution.py:17
  377.0 2.0 fusion.7
  (136 shorter events, 79.1 us)
Async XLA Ops:
  7.2 58.8 %all-gather.6.cloned.1.call-start = ((), (), s32[]{:S(2)}) async-start(), calls=%async_computation.10 | async-start | bytes 1179648 | tf_op jit(solution)/shard_map/all_gather | solution.py:55
  35.8 63.1 %all-to-all-start.1 = ((bf16[32,2,1,32,448]{4,3,1,2,0:T(8,128)(2,1)}), bf16[32,2,1,32,448]{4,3,1,2,0:T(8,128)(2,1)}, u32[]{:S(2)}, u32[]{:S(2)}) async-start(bf16[32,2,1,32,448]{4,3,1,2,0:T(8,128)(2,1)} %copy.40), calls=%async_computation.1 | async-start | bytes 4194304 | tf_op jit(solution)/shard_map/all_to_all | solution.py:42
  44.9 43.7 %all-gather.8.cloned.1.call-start = ((), (), s32[]{:S(2)}) async-start(), calls=%async_computation.11 | async-start | bytes 3145728 | tf_op jit(solution)/shard_map/all_gather | solution.py:55
  66.0 244.8 %reduce-scatter.4.cloned.1.call-start = ((), (), s32[]{:S(2)}) async-start(), calls=%async_computation.7 | async-start | bytes 4718592 | tf_op jit(solution)/shard_map/reduce_scatter | solution.py:68
  88.5 10.3 %copy-start.2 = (f32[1,448]{1,0:T(1,128)S(1)}, f32[1,448]{1,0:T(1,128)}, u32[]{:S(2)}) copy-start(f32[1,448]{1,0:T(1,128)} %param.8) | copy-start | bytes 5380
  90.3 11.5 %copy-start = (bf16[2,8,4,1,32,512]{5,4,0,2,1,3:T(8,128)(2,1)}, bf16[2,8,4,1,32,512]{5,4,0,2,1,3:T(8,128)(2,1)S(1)}, u32[]{:S(2)}) copy-start(bf16[2,8,4,1,32,512]{5,4,0,2,1,3:T(8,128)(2,1)S(1)} %copy.37) | copy-start | bytes 6291460
  256.5 120.6 %copy-start.1 = (f32[1,32,512]{2,1,0:T(8,128)S(1)}, f32[1,32,512]{2,1,0:T(8,128)}, u32[]{:S(2)}) copy-start(f32[1,32,512]{2,1,0:T(8,128)} %param.7) | copy-start | bytes 196612
  256.5 77.2 %reduce-scatter.6.cloned.1.call-start = ((), (), s32[]{:S(2)}) async-start(), calls=%async_computation.8 | async-start | bytes 655360 | tf_op jit(solution)/shard_map/reduce_scatter | solution.py:68
  312.0 21.7 %all-to-all-start.2 = ((s32[4,1,1]{2,1,0:T(1,128)}), s32[4,1,1]{2,1,0:T(1,128)S(1)}, u32[]{:S(2)}, u32[]{:S(2)}) async-start(s32[4,1,1]{2,1,0:T(1,128)} %broadcast_in_dim.51), calls=%async_computation.5 | async-start | bytes 4096 | tf_op jit(solution)/shard_map/all_to_all | solution.py:17
  316.0 35.8 %reduce-scatter.8.cloned.1.call-start = ((), (), s32[]{:S(2)}) async-start(), calls=%async_computation.9 | async-start | bytes 196608 | tf_op jit(solution)/shard_map/reduce_scatter | solution.py:68
  355.3 19.2 %all-to-all-start.3 = ((f32[64,1,2]{2,1,0:T(1,128)}), f32[64,1,2]{2,1,0:T(1,128)S(1)}, u32[]{:S(2)}, u32[]{:S(2)}) async-start(f32[64,1,2]{2,1,0:T(1,128)} %broadcast_in_dim.56), calls=%async_computation.6 | async-start | bytes 65536 | tf_op jit(solution)/shard_map/all_to_all | solution.py:17
Sparse Core Ops, SparseCore 0:
  19.5 46.4 all-gather.5
  67.8 20.7 all-gather.7
  256.6 54.1 reduce-scatter.3
  313.2 20.4 reduce-scatter.5
  336.0 15.7 reduce-scatter.7
where the time goes:
time: 387 us; the launch traced here: 386 us
  waiting for transfers between devices  149 us (39%)
  matrix products  62.5 us (16%)
  local copies, waits for them, and re-layouts  60 us (16%)
  loops' own time  43.6 us (11%)
  starting transfers between devices  23.2 us (6%)
  blocking collectives  21.1 us (5%)
  between operations  16.5 us (4%)
  other arithmetic  9.29 us (2%)
    reduce_scatter x3, waiting for transfers between devices, sum_by_axis(): so_far = lax.psum_scatter(so_far, axis, scatter_dimension=0, tiled=True)  88 us
    dot_general x64, matrix products, one_group(): jnp.einsum('eic,ejc->iej', picked, window, preferred_element_type=jnp.flo...  57.6 us
    another operation x1, loops' own time, body(): parts = lax.map(one_group, jnp.arange(groups, dtype=jnp.int32))  43.6 us
    all_gather x2, waiting for transfers between devices, all_blocks(): parts = lax.all_gather(parts, axes[k], axis=0, tiled=True)  43.5 us
    dynamic_slice x64, local copies, waits for them, and re-layouts, body(): parts = lax.map(one_group, jnp.arange(groups, dtype=jnp.int32))  37.3 us
    all_to_all x2, starting transfers between devices, from_everyone(): lax.all_to_all(jnp.broadcast_to(shard[None], (size, *shard.shape)), axis,...  13.9 us
    all_gather x1, blocking collectives, all_blocks(): parts = lax.all_gather(parts, axes[k], axis=0, tiled=True)  11.3 us
    all_to_all x1, blocking collectives, moved_by_axis(): out = lax.all_to_all(out, axes[k], k, k, tiled=True)  9.74 us
  transfers between devices with their start and end apart: 8, of which 7 were waited for; matrix products, arithmetic and copies ran while one was open for 3% of the time, Pallas kernels for 0%

commit v1 on v0

v1 whole, which is shorter than its diff:
```python
import jax
import jax.numpy as jnp
from jax import lax
from jax.experimental import pallas as pl
from jax.experimental.pallas import tpu as pltpu
from jax.sharding import Mesh
from jax.sharding import PartitionSpec as P

SHARD = ("zh", "zl", "x", "c")
GROUP = ("zl", "x", "c")
CROSS = ("zh", "c")
FF2 = 28672
DIM = 2048
BLOCK = 512
ROWS = 32
OWN = 448
PAIR = 896
WIDE = 1792
MESSAGE = BLOCK + WIDE

step_rate = 0.5
epsilon = 1e-06

VMEM = pl.BlockSpec(memory_space=pltpu.VMEM)
SMEM = pl.BlockSpec(memory_space=pltpu.SMEM)


def pack_kernel(gradient, factor, out):
    narrow = factor[0].astype(jnp.bfloat16)
    for place in range(8):
        for core in range(2):
            dest = place * 2 + core
            out[dest, :, :BLOCK] = narrow
            for q in range(2):
                begin = ((2 * core + q) * 16 + place * 2) * OWN
                left = BLOCK + q * PAIR
                out[dest, :, left : left + PAIR] = gradient[0, :, begin : begin + PAIR]


def gram_kernel(places, scales, got, rights, part, sums, image):
    core = places[0]
    mine = jnp.where(core == 0, rights[0:4, :], rights[4:8, :])
    right = jnp.concatenate([mine[k : k + 1, :] for k in range(4)], axis=1)
    upper_left = got[0:256, 0:512]
    lower_right = got[256:512, 256:512]
    totals = []
    for k in range(7):
        at = BLOCK + k * 256
        scale = right[:, k * 256 : (k + 1) * 256]
        high = jnp.dot(upper_left, got[:, at : at + 256], preferred_element_type=jnp.float32)
        low = jnp.dot(lower_right, got[256:512, at : at + 256], preferred_element_type=jnp.float32)
        high = (high * scale).astype(jnp.bfloat16)
        low = (low * scale).astype(jnp.bfloat16)
        image[0:256, k * 256 : (k + 1) * 256] = high
        image[256:512, k * 256 : (k + 1) * 256] = low
        total = jnp.sum(jnp.square(high.astype(jnp.float32)), axis=0, keepdims=True)
        total = total + jnp.sum(jnp.square(low.astype(jnp.float32)), axis=0, keepdims=True)
        totals.append(total)
    total = jnp.concatenate(totals, axis=1)
    row = lax.broadcasted_iota(jnp.int32, (8, PAIR), 0)
    chosen = jnp.where((row // 2) % 2 == 0, total[:, :PAIR], total[:, PAIR:])
    sums[...] = jnp.where(row // 4 == core, chosen, 0.0)
    last = (((1,), (1,)), ((), ()))
    scale = scales[1]
    high = lax.dot_general(image[0:256, :], image[...], last, preferred_element_type=jnp.float32)
    low = lax.dot_general(image[256:512, :], image[256:512, :], last, preferred_element_type=jnp.float32)
    share = jnp.float32(1.0 / 16.0)
    row_high = lax.broadcasted_iota(jnp.int32, (256, 512), 0)
    col_high = lax.broadcasted_iota(jnp.int32, (256, 512), 1)
    row_low = lax.broadcasted_iota(jnp.int32, (256, 256), 0)
    col_low = lax.broadcasted_iota(jnp.int32, (256, 256), 1)
    part[0:256, :] = (high * scale - jnp.where(row_high == col_high, share, 0.0)).astype(part.dtype)
    part[256:512, 256:512] = (low * scale - jnp.where(row_low == col_low, share, 0.0)).astype(part.dtype)
    part[256:512, 0:256] = jnp.zeros((256, 256), part.dtype)


def peaks_kernel(places, scales, parts, sums, upper, term, levels):
    core, first = places[0], places[1]
    total = parts[0].astype(jnp.float32)
    for k in range(1, 16):
        total = total + parts[k].astype(jnp.float32)
    row = lax.broadcasted_iota(jnp.int32, (ROWS, BLOCK), 0) + first
    col = lax.broadcasted_iota(jnp.int32, (ROWS, BLOCK), 1)
    total = jnp.where(col >= row, total, 0.0)
    upper[...] = total
    row_level = jnp.max(jnp.abs(total))
    added = jnp.sum(sums[...], axis=0, keepdims=True)
    added = jnp.where(core == 0, added[:, :OWN], added[:, OWN:])
    column_term = scales[0] * added / DIM - 1.0
    term[...] = column_term
    column_level = jnp.max(jnp.abs(column_term))
    lane = lax.broadcasted_iota(jnp.int32, levels.shape, 2)
    levels[...] = jnp.where(lane == 0, row_level, column_level)


def final_kernel(levels, upper, narrow, factor, term, right, new_factor, new_right):
    peak = jnp.max(levels[...], axis=0)
    row_peak = jnp.max(peak[0:1, 0:1])
    column_peak = jnp.max(peak[0:1, 1:2])
    steps = (upper[...] / (row_peak + epsilon)).astype(jnp.bfloat16)
    moved = jnp.dot(steps, narrow[...], preferred_element_type=jnp.float32)
    new_factor[0] = factor[0] - step_rate * moved
    new_right[...] = right[...] - step_rate * term[...] / (column_peak + epsilon) * right[...]


def shape(dims, dtype=jnp.float32):
    return jax.ShapeDtypeStruct(dims, dtype)


def cost(flops, moved):
    return pl.CostEstimate(flops=flops, bytes_accessed=moved, transcendentals=0)


def body(gradient, factor, right_diag, counts):
    packed = pl.pallas_call(
        pack_kernel,
        out_shape=shape((16, ROWS, MESSAGE), jnp.bfloat16),
        in_specs=[VMEM, VMEM],
        out_specs=VMEM,
        cost_estimate=cost(1000000, 4194304),
        name="pack",
    )(gradient, factor)
    got = lax.all_to_all(packed, GROUP, 0, 0, tiled=True).reshape(BLOCK, MESSAGE)
    rights = lax.all_to_all(jnp.broadcast_to(right_diag, (8, OWN)), CROSS, 0, 0, tiled=True)
    tokens = lax.all_to_all(jnp.broadcast_to(counts, (4,)), "expert", 0, 0, tiled=True)
    weight = 4 * counts.astype(jnp.float32) / jnp.sum(tokens).astype(jnp.float32)
    squared = weight * weight
    scales = jnp.concatenate([squared, squared / FF2])
    core = lax.axis_index("c")
    first = lax.axis_index(GROUP) * ROWS
    places = jnp.stack([core, first]).astype(jnp.int32)
    part, sums = pl.pallas_call(
        gram_kernel,
        out_shape=[shape((BLOCK, BLOCK), jnp.bfloat16), shape((8, PAIR))],
        in_specs=[SMEM, SMEM, VMEM, VMEM],
        out_specs=[VMEM, VMEM],
        scratch_shapes=[pltpu.VMEM((BLOCK, WIDE), jnp.bfloat16)],
        cost_estimate=cost(1600000000, 4194304),
        name="gram",
    )(places, scales, got, rights)
    parts = lax.all_to_all(part.reshape(16, ROWS, BLOCK), GROUP, 0, 0, tiled=True)
    sums = lax.all_to_all(sums, CROSS, 0, 0, tiled=True)
    upper, term, levels = pl.pallas_call(
        peaks_kernel,
        out_shape=[shape((ROWS, BLOCK)), shape((1, OWN)), shape((64, 1, 128))],
        in_specs=[SMEM, SMEM, VMEM, VMEM],
        out_specs=[VMEM, VMEM, VMEM],
        cost_estimate=cost(1000000, 1048576),
        name="peaks",
    )(places, scales, parts, sums)
    levels = lax.all_to_all(levels, SHARD, 0, 0, tiled=True)
    new_factor, new_right = pl.pallas_call(
        final_kernel,
        out_shape=[shape((1, ROWS, BLOCK)), shape((1, OWN))],
        grid=(1,),
        in_specs=[
            VMEM,
            VMEM,
            pl.BlockSpec((BLOCK, BLOCK), lambda i: (0, 0)),
            VMEM,
            VMEM,
            VMEM,
        ],
        out_specs=[VMEM, VMEM],
        cost_estimate=cost(17000000, 1048576),
        name="final",
    )(levels, upper, got, factor, term, right_diag)
    return new_factor, new_right


def solution(mesh):
    torus = Mesh(
        mesh.devices.reshape(mesh.shape["expert"], 4, 2, 4, 2),
        ("expert", "zh", "zl", "x", "c"),
    )
    return jax.shard_map(
        body,
        mesh=torus,
        in_specs=(
            P("expert", SHARD, None),
            P("expert", SHARD, None),
            P("expert", SHARD),
            P("expert"),
        ),
        out_specs=(P("expert", SHARD, None), P("expert", SHARD)),
        check_vma=False,
    )
```

time: 387 us -> 120 us (0.31)
  waiting for transfers between devices: 149 us -> 40.5 us
  matrix products: 62.5 us -> 0 us
  local copies, waits for them, and re-layouts: 60 us -> 5.46 us
  loops' own time: 43.6 us -> 0 us
  between operations: 16.5 us -> 1.99 us
  blocking collectives: 21.1 us -> 34.8 us
  Pallas kernels: 0 us -> 11.3 us
  other arithmetic: 9.29 us -> 1.88 us
    reduce_scatter x3 -> x0, waiting for transfers between devices: 88 us -> none  [sum_by_axis(): so_far = lax.psum_scatter(so_far, axis, scatter_dimension=0, tiled=True)]
    dot_general x66 -> x0, matrix products: 62.5 us -> none  [the longest x64 57.6 us: one_group(): jnp.einsum('eic,ejc->iej', picked, window, preferred_element_type=jnp.flo...]
    another operation x1 -> x0, loops' own time: 43.6 us -> none  [body(): parts = lax.map(one_group, jnp.arange(groups, dtype=jnp.int32))]
    all_gather x2 -> x0, waiting for transfers between devices: 43.5 us -> none  [all_blocks(): parts = lax.all_gather(parts, axes[k], axis=0, tiled=True)]
    dynamic_slice x64 -> x0, local copies, waits for them, and re-layouts: 37.3 us -> none  [body(): parts = lax.map(one_group, jnp.arange(groups, dtype=jnp.int32))]
    all_to_all x1 -> x3, blocking collectives: 9.74 us -> 34.8 us  [the longest x1 15.4 us: body(): levels = lax.all_to_all(levels, SHARD, 0, 0, tiled=True)]
    all_to_all x3, waiting for transfers between devices: 17.9 us -> 40.5 us  [the longest x1 27.4 us: body(): lax.all_to_all(packed, GROUP, 0, 0, tiled=True).reshape(BLOCK, MESSAGE)]
    all_gather x1 -> x0, blocking collectives: 11.3 us -> none  [all_blocks(): parts = lax.all_gather(parts, axes[k], axis=0, tiled=True)]
  transfers between devices with their start and end apart: 8 -> 3, of which waited for: 7 -> 3; matrix products, arithmetic and copies ran while one was open for 3% -> 3% of each run, Pallas kernels for 0% -> 3%
where the time goes in v1:
time: 120 us; the launch traced here: 119 us
  waiting for transfers between devices  40.5 us (34%)
  blocking collectives  34.8 us (29%)
  starting transfers between devices  23.2 us (19%)
  Pallas kernels  11.3 us (9%)
  local copies, waits for them, and re-layouts  5.46 us (5%)
  between operations  1.99 us (2%)
  other arithmetic  1.88 us (2%)
    all_to_all x1, waiting for transfers between devices, body(): lax.all_to_all(packed, GROUP, 0, 0, tiled=True).reshape(BLOCK, MESSAGE)  27.4 us
    all_to_all x1, blocking collectives, body(): levels = lax.all_to_all(levels, SHARD, 0, 0, tiled=True)  15.4 us
    all_to_all x1, starting transfers between devices, body(): lax.all_to_all(jnp.broadcast_to(right_diag, (8, OWN)), CROSS, 0, 0, tiled...  10.6 us
    all_to_all x1, blocking collectives, body(): sums = lax.all_to_all(sums, CROSS, 0, 0, tiled=True)  10.4 us
    all_to_all x1, waiting for transfers between devices, body(): lax.all_to_all(part.reshape(16, ROWS, BLOCK), GROUP, 0, 0, tiled=True)  9.06 us
    all_to_all x1, blocking collectives, body(): lax.all_to_all(jnp.broadcast_to(counts, (4,)), 'expert', 0, 0, tiled=True)  8.94 us
    all_to_all x1, starting transfers between devices, body(): lax.all_to_all(part.reshape(16, ROWS, BLOCK), GROUP, 0, 0, tiled=True)  7.13 us
    all_to_all x1, starting transfers between devices, body(): lax.all_to_all(packed, GROUP, 0, 0, tiled=True).reshape(BLOCK, MESSAGE)  5.48 us
  transfers between devices with their start and end apart: 3, of which 3 were waited for; matrix products, arithmetic and copies ran while one was open for 3% of the time, Pallas kernels for 3%

profile of v1, /device:TPU:1, one launch (start us, length us, event | category | flops | bytes accessed | tf_op | source)
XLA Modules:
  0.0 119.0 jit_solution(13592760003987242736)
XLA Ops:
  1.3 8.9 %all_to_all.40 = s32[4,1,1]{2,1,0:T(1,128)S(1)} all-to-all(s32[4,1,1]{2,1,0:T(1,128)S(1)} %broadcast_in_dim.13), channel_id=1, replica_groups=mesh['expert'=4,'zh'=4,'zl'=2,'x'=4,'c'=2] {'expert'}, dimensions={0} | all-to-all | bytes 32 | tf_op jit(solution)/shard_map/all_to_all | solution.py:125
  10.2 1.3 %broadcast_in_dim.14 = f32[8,1,448]{2,1,0:T(1,128)} broadcast(f32[448]{0:T(512)} %bitcast.21), dimensions={2} | broadcast | bytes 16128 | tf_op jit(solution)/shard_map/broadcast_in_dim | solution.py:124
  11.5 10.6 %all-to-all-start.2 = ((f32[8,1,448]{2,1,0:T(1,128)}), f32[8,1,448]{2,1,0:T(1,128)S(1)}, u32[]{:S(2)}, u32[]{:S(2)}) async-start(f32[8,1,448]{2,1,0:T(1,128)} %broadcast_in_dim.14), calls=%async_computation.2 | async-start | bytes 32768 | tf_op jit(solution)/shard_map/all_to_all | solution.py:124
  22.1 3.1 %pack.1 = bf16[16,32,2304]{2,1,0:T(8,128)(2,1)} custom-call(bf16[1,32,28672]{2,1,0:T(8,128)(2,1)} %gradient.1, f32[1,32,512]{2,1,0:T(8,128)} %factor.3), custom_call_target="tpu_custom_call" | custom-call | flops 1000000 | bytes 4194304 | tf_op jit(solution)/shard_map/pack/pallas_call | solution.py:115
  25.2 4.0 %all-to-all-done.2 = f32[8,1,448]{2,1,0:T(1,128)S(1)} async-done(((f32[8,1,448]{2,1,0:T(1,128)}), f32[8,1,448]{2,1,0:T(1,128)S(1)}, u32[]{:S(2)}, u32[]{:S(2)}) %all-to-all-start.2) | async-done | bytes 14368 | tf_op jit(solution)/shard_map/all_to_all | solution.py:124
  29.2 5.5 %all-to-all-start.1 = ((bf16[16,32,2304]{2,1,0:T(8,128)(2,1)}), bf16[16,32,2304]{2,1,0:T(8,128)(2,1)S(1)}, u32[]{:S(2)}, u32[]{:S(2)}) async-start(bf16[16,32,2304]{2,1,0:T(8,128)(2,1)} %pack.1), calls=%async_computation.1 | async-start | bytes 4718592 | tf_op jit(solution)/shard_map/all_to_all | solution.py:123
  34.7 0.7 pad_add_fusion.places
  35.3 0.6 reduce_sum.9
  36.7 0.6 pad_maximum_fusion.scales
  37.2 0.6 copy.16
  37.8 27.4 %all-to-all-done.1 = bf16[16,32,2304]{2,1,0:T(8,128)(2,1)S(1)} async-done(((bf16[16,32,2304]{2,1,0:T(8,128)(2,1)}), bf16[16,32,2304]{2,1,0:T(8,128)(2,1)S(1)}, u32[]{:S(2)}, u32[]{:S(2)}) %all-to-all-start.1) | async-done | bytes 2359328 | tf_op jit(solution)/shard_map/all_to_all | solution.py:123
  65.2 0.0 copy-start
  65.2 1.4 %copy-done = bf16[16,32,2304]{2,1,0:T(8,128)(2,1)} copy-done((bf16[16,32,2304]{2,1,0:T(8,128)(2,1)}, bf16[16,32,2304]{2,1,0:T(8,128)(2,1)S(1)}, u32[]{:S(2)}) %copy-start) | copy-done | bytes 2359320
  66.6 4.3 %gram.1 = (bf16[512,512]{1,0:T(8,128)(2,1)}, f32[8,896]{1,0:T(8,128)}) custom-call(s32[2]{0:T(128)} %pad_add_fusion.places, f32[2]{0:T(128)} %pad_maximum_fusion.scales, bf16[512,2304]{1,0:T(8,128)(2,1)} %bitcast.15, f32[8,448]{1,0:T(8,128)} %bitcast.20), custom_call_target="tpu_custom_call" | custom-call | flops 1600000000 | bytes 4194304 | tf_op jit(solution)/shard_map/gram/pallas_call | solution.py:132
  70.9 0.8 copy.9
  71.7 10.4 %all_to_all.41 = f32[8,1,896]{2,1,0:T(1,128)S(1)} all-to-all(f32[8,1,896]{2,1,0:T(1,128)S(1)} %copy.9), channel_id=1, replica_groups=mesh['expert'=4,'zh'=4,'zl'=2,'x'=4,'c'=2] {'zh','c'}, dimensions={0} | all-to-all | bytes 57344 | tf_op jit(solution)/shard_map/all_to_all | solution.py:142
  82.1 7.1 %all-to-all-start.3 = ((bf16[16,32,512]{2,1,0:T(8,128)(2,1)}), bf16[16,32,512]{2,1,0:T(8,128)(2,1)S(1)}, u32[]{:S(2)}, u32[]{:S(2)}) async-start(bf16[16,32,512]{2,1,0:T(8,128)(2,1)} %bitcast.17), calls=%async_computation.3 | async-start | bytes 1048576 | tf_op jit(solution)/shard_map/all_to_all | solution.py:141
  89.2 0.6 copy.15
  89.8 9.1 %all-to-all-done.3.parts = bf16[16,32,512]{2,1,0:T(8,128)(2,1)S(1)} async-done(((bf16[16,32,512]{2,1,0:T(8,128)(2,1)}), bf16[16,32,512]{2,1,0:T(8,128)(2,1)S(1)}, u32[]{:S(2)}, u32[]{:S(2)}) %all-to-all-start.3) | async-done | bytes 524320 | tf_op jit(solution)/shard_map/all_to_all | solution.py:141
  98.9 0.0 copy-start.1
  98.9 0.8 copy-done.1
  99.7 1.9 %peaks.1 = (f32[32,512]{1,0:T(8,128)}, f32[1,448]{1,0:T(1,128)}, f32[64,1,128]{2,1,0:T(1,128)}) custom-call(s32[2]{0:T(128)} %pad_add_fusion.places, f32[2]{0:T(128)} %pad_maximum_fusion.scales, bf16[16,32,512]{2,1,0:T(8,128)(2,1)} %copy-done.1, f32[8,896]{1,0:T(8,128)} %bitcast.18), custom_call_target="tpu_custom_call" | custom-call | flops 1000000 | bytes 1048576 | tf_op jit(solution)/shard_map/peaks/pallas_call | solution.py:143
  101.6 15.4 %all_to_all.42.levels = f32[64,1,128]{2,1,0:T(1,128)} all-to-all(f32[64,1,128]{2,1,0:T(1,128)} %get-tuple-element.9), channel_id=1, replica_groups=mesh['expert'=4,'zh'=4,'zl'=2,'x'=4,'c'=2] {'zh','zl','x','c'}, dimensions={0} | all-to-all | bytes 65536 | tf_op jit(solution)/shard_map/all_to_all | solution.py:151
  117.0 2.0 %final.1 = (f32[1,32,512]{2,1,0:T(8,128)}, f32[1,448]{1,0:T(1,128)}) custom-call(f32[64,1,128]{2,1,0:T(1,128)} %all_to_all.42.levels, f32[32,512]{1,0:T(8,128)} %get-tuple-element.10.upper, bf16[512,2304]{1,0:T(8,128)(2,1)} %bitcast.16, f32[1,32,512]{2,1,0:T(8,128)} %factor.3, f32[1,448]{1,0:T(1,128)} %get-tuple-element.11.term, f32[1,448]{1,0:T(1,128)} %right.1), custom_call_target="tpu_custom_call" | custom-call | flops 17000000 | bytes 1048576 | tf_op jit(solution)/shard_map/final/pallas_call | solution.py:152
  (1 shorter events, 0.0 us)
Async XLA Ops:
  11.5 17.7 %all-to-all-start.2 = ((f32[8,1,448]{2,1,0:T(1,128)}), f32[8,1,448]{2,1,0:T(1,128)S(1)}, u32[]{:S(2)}, u32[]{:S(2)}) async-start(f32[8,1,448]{2,1,0:T(1,128)} %broadcast_in_dim.14), calls=%async_computation.2 | async-start | bytes 32768 | tf_op jit(solution)/shard_map/all_to_all | solution.py:124
  29.2 36.0 %all-to-all-start.1 = ((bf16[16,32,2304]{2,1,0:T(8,128)(2,1)}), bf16[16,32,2304]{2,1,0:T(8,128)(2,1)S(1)}, u32[]{:S(2)}, u32[]{:S(2)}) async-start(bf16[16,32,2304]{2,1,0:T(8,128)(2,1)} %pack.1), calls=%async_computation.1 | async-start | bytes 4718592 | tf_op jit(solution)/shard_map/all_to_all | solution.py:123
  65.2 1.4 %copy-start = (bf16[16,32,2304]{2,1,0:T(8,128)(2,1)}, bf16[16,32,2304]{2,1,0:T(8,128)(2,1)S(1)}, u32[]{:S(2)}) copy-start(bf16[16,32,2304]{2,1,0:T(8,128)(2,1)S(1)} %all-to-all-done.1) | copy-start | bytes 7077892
  82.1 16.8 %all-to-all-start.3 = ((bf16[16,32,512]{2,1,0:T(8,128)(2,1)}), bf16[16,32,512]{2,1,0:T(8,128)(2,1)S(1)}, u32[]{:S(2)}, u32[]{:S(2)}) async-start(bf16[16,32,512]{2,1,0:T(8,128)(2,1)} %bitcast.17), calls=%async_computation.3 | async-start | bytes 1048576 | tf_op jit(solution)/shard_map/all_to_all | solution.py:141
  98.9 0.8 copy-start.1

commit v2 on v1

v2 whole, which is shorter than its diff:
```python
import jax
import jax.numpy as jnp
from jax import lax
from jax.experimental import pallas as pl
from jax.experimental.pallas import tpu as pltpu
from jax.sharding import Mesh
from jax.sharding import PartitionSpec as P


SHARD = ("zh", "zl", "x", "c")
GROUP = ("zl", "x", "c")
FF2 = 28672
DIM = 2048
BLOCK = 512
ROWS = 32
OWN = 448
PAIR = 896
SPAN = 16 * OWN
WIDE = 1792
MESSAGE = BLOCK + WIDE

step_rate = 0.5
epsilon = 1e-06


VMEM = pl.BlockSpec(memory_space=pltpu.VMEM)
HBM = pl.BlockSpec(memory_space=pltpu.HBM)
SMEM = pl.BlockSpec(memory_space=pltpu.SMEM)


def pack_kernel(gradient, factor, out, near, rows, message, in_sems, out_sems):
    block = lax.axis_index("zh")
    fetches = [pltpu.make_async_copy(factor, rows, in_sems.at[4])]
    for d in range(4):
        begin = pl.multiple_of(lax.rem(block + (4 - d), 4) * SPAN, 128)
        source = gradient.at[0, :, pl.ds(begin, SPAN)]
        fetches.append(pltpu.make_async_copy(source, near.at[d], in_sems.at[d]))
    for fetch in fetches:
        fetch.start()
    fetches[0].wait()
    narrow = rows[0].astype(jnp.bfloat16)
    for dest in range(16):
        message[dest, :, :BLOCK] = narrow
    sends = []
    for q in range(2):
        fetches[1 + 2 * q].wait()
        fetches[2 + 2 * q].wait()
        left = BLOCK + q * PAIR
        for part in range(2):
            for place in range(4 * part, 4 * part + 4):
                pairs = [near[2 * q + k, :, place * PAIR : (place + 1) * PAIR] for k in range(2)]
                for core in range(2):
                    pieces = [pair[:, core * OWN : (core + 1) * OWN] for pair in pairs]
                    message[place * 2 + core, :, left : left + PAIR] = jnp.concatenate(pieces, axis=1)
            begin = 0 if q == 0 else left
            view = (pl.ds(8 * part, 8), slice(None), pl.ds(begin, left + PAIR - begin))
            send = pltpu.make_async_copy(message.at[view], out.at[view], out_sems.at[2 * q + part])
            send.start()
            sends.append(send)
    for send in sends:
        send.wait()


def gram_kernel(scales, got, right0, right1, right2, right3, part, sum0, sum1, sum2, sum3, image):
    right = jnp.concatenate([right0[...], right1[...], right2[...], right3[...]], axis=1)
    upper_left = got[0:256, 0:512]
    lower_right = got[256:512, 256:512]
    totals = []
    for k in range(7):
        at = BLOCK + k * 256
        scale = right[:, k * 256 : (k + 1) * 256]
        high = jnp.dot(upper_left, got[:, at : at + 256], preferred_element_type=jnp.float32)
        low = jnp.dot(lower_right, got[256:512, at : at + 256], preferred_element_type=jnp.float32)
        high = (high * scale).astype(jnp.bfloat16)
        low = (low * scale).astype(jnp.bfloat16)
        image[0:256, k * 256 : (k + 1) * 256] = high
        image[256:512, k * 256 : (k + 1) * 256] = low
        total = jnp.sum(jnp.square(high.astype(jnp.float32)), axis=0, keepdims=True)
        total = total + jnp.sum(jnp.square(low.astype(jnp.float32)), axis=0, keepdims=True)
        totals.append(total)
    total = jnp.concatenate(totals, axis=1)
    for d, out in enumerate((sum0, sum1, sum2, sum3)):
        out[...] = total[:, d * OWN : (d + 1) * OWN]
    last = (((1,), (1,)), ((), ()))
    scale = scales[1]
    high = lax.dot_general(image[0:256, :], image[...], last, preferred_element_type=jnp.float32)
    low = lax.dot_general(image[256:512, :], image[256:512, :], last, preferred_element_type=jnp.float32)
    share = jnp.float32(1.0 / 16.0)
    row_high = lax.broadcasted_iota(jnp.int32, (256, 512), 0)
    col_high = lax.broadcasted_iota(jnp.int32, (256, 512), 1)
    row_low = lax.broadcasted_iota(jnp.int32, (256, 256), 0)
    col_low = lax.broadcasted_iota(jnp.int32, (256, 256), 1)
    part[0:256, :] = (high * scale - jnp.where(row_high == col_high, share, 0.0)).astype(part.dtype)
    part[256:512, 256:512] = (low * scale - jnp.where(row_low == col_low, share, 0.0)).astype(part.dtype)
    part[256:512, 0:256] = jnp.zeros((256, 256), part.dtype)


def peaks_kernel(scales, parts, sum0, sum1, sum2, sum3, upper, term, levels):
    first = lax.axis_index(GROUP) * ROWS
    total = parts[0].astype(jnp.float32)
    for k in range(1, 16):
        total = total + parts[k].astype(jnp.float32)
    row = lax.broadcasted_iota(jnp.int32, (ROWS, BLOCK), 0) + first
    col = lax.broadcasted_iota(jnp.int32, (ROWS, BLOCK), 1)
    total = jnp.where(col >= row, total, 0.0)
    upper[...] = total
    row_level = jnp.max(jnp.abs(total))
    added = (sum0[...] + sum1[...]) + (sum2[...] + sum3[...])
    column_term = scales[0] * added / DIM - 1.0
    term[...] = column_term
    column_level = jnp.max(jnp.abs(column_term))
    lane = lax.broadcasted_iota(jnp.int32, levels.shape, 2)
    levels[...] = jnp.where(lane == 0, row_level, column_level)


def final_kernel(levels, upper, narrow, factor, term, right, new_factor, new_right):
    peak = jnp.max(levels[...], axis=0)
    row_peak = jnp.max(peak[0:1, 0:1])
    column_peak = jnp.max(peak[0:1, 1:2])
    steps = (upper[...] / (row_peak + epsilon)).astype(jnp.bfloat16)
    moved = jnp.dot(steps, narrow[...], preferred_element_type=jnp.float32)
    new_factor[0] = factor[0] - step_rate * moved
    new_right[...] = right[...] - step_rate * term[...] / (column_peak + epsilon) * right[...]


def shape(dims, dtype=jnp.float32):
    return jax.ShapeDtypeStruct(dims, dtype)


def call(kernel, ins, outs, flops, scratch=(), room=16):
    return pl.pallas_call(
        kernel,
        out_shape=outs,
        grid=(1,),
        in_specs=ins,
        out_specs=[VMEM] * len(outs),
        scratch_shapes=list(scratch),
        compiler_params=pltpu.CompilerParams(vmem_limit_bytes=room * 1024 * 1024),
        cost_estimate=pl.CostEstimate(flops=flops, bytes_accessed=2097152, transcendentals=0),
    )


def exchange(value, axes):
    return lax.all_to_all(value, axes, 0, 0, tiled=True)


def shifted(value, axis, by):
    size = lax.axis_size(axis)
    return lax.ppermute(value, axis, [(k, (k + by) % size) for k in range(size)])


def inner(gradient, factor, right_diag, counts):
    half = jnp.bfloat16
    packed = pl.pallas_call(
        pack_kernel,
        out_shape=shape((16, ROWS, MESSAGE), half),
        in_specs=[HBM, HBM],
        out_specs=HBM,
        scratch_shapes=[
            pltpu.VMEM((4, ROWS, SPAN), half),
            pltpu.VMEM((1, ROWS, BLOCK), jnp.float32),
            pltpu.VMEM((16, ROWS, MESSAGE), half),
            pltpu.SemaphoreType.DMA((5,)),
            pltpu.SemaphoreType.DMA((4,)),
        ],
        compiler_params=pltpu.CompilerParams(vmem_limit_bytes=62 * 1024 * 1024),
        cost_estimate=pl.CostEstimate(flops=2000000, bytes_accessed=4194304, transcendentals=0),
        name="pack",
    )(gradient, factor)
    got = exchange(packed, GROUP).reshape(BLOCK, MESSAGE)
    rights = [right_diag] + [shifted(right_diag, "zh", d) for d in (1, 2, 3)]
    tokens = counts
    for d in (1, 2, 3):
        tokens = tokens + shifted(counts, "expert", d)
    weight = 4 * counts.astype(jnp.float32) / tokens.astype(jnp.float32)
    squared = weight * weight
    scales = jnp.concatenate([squared, squared / FF2])
    part, *sums = call(
        gram_kernel,
        [SMEM] + [VMEM] * 5,
        [shape((BLOCK, BLOCK), half)] + [shape((1, OWN))] * 4,
        1600000000,
        [pltpu.VMEM((BLOCK, WIDE), half)],
    )(scales, got, *rights)
    parts = exchange(part.reshape(16, ROWS, BLOCK), GROUP)
    sums = [sums[0]] + [shifted(sums[d], "zh", -d) for d in (1, 2, 3)]
    upper, term, levels = call(
        peaks_kernel,
        [SMEM] + [VMEM] * 5,
        [shape((ROWS, BLOCK)), shape((1, OWN)), shape((64, 1, 128))],
        2000000,
    )(scales, parts, *sums)
    levels = exchange(levels, SHARD)
    new_factor, new_right = call(
        final_kernel,
        [VMEM, VMEM, pl.BlockSpec((BLOCK, BLOCK), lambda i: (0, 0)), VMEM, VMEM, VMEM],
        [shape((1, ROWS, BLOCK)), shape((1, OWN))],
        17000000,
    )(levels, upper, got, factor, term, right_diag)
    return new_factor, new_right


def solution(mesh):
    torus = Mesh(
        mesh.devices.reshape(mesh.shape["expert"], 4, 2, 4, 2),
        ("expert", "zh", "zl", "x", "c"),
    )
    return jax.shard_map(
        inner,
        mesh=torus,
        in_specs=(
            P("expert", SHARD, None),
            P("expert", SHARD, None),
            P("expert", SHARD),
            P("expert"),
        ),
        out_specs=(P("expert", SHARD, None), P("expert", SHARD)),
        check_vma=False,
    )
```

time: 120 us -> 84.9 us (0.71)
  waiting for transfers between devices: 40.5 us -> 22.6 us
  blocking collectives: 34.8 us -> 17.8 us
  starting transfers between devices: 23.2 us -> 33.2 us
  local copies, waits for them, and re-layouts: 5.46 us -> 0.01 us
  Pallas kernels: 11.3 us -> 7.64 us
  other arithmetic: 1.88 us -> 0.08 us
  between operations: 1.99 us -> 3.26 us
    all_to_all x3 -> x2, waiting for transfers between devices: 40.5 us -> 0.35 us  [exchange(): return lax.all_to_all(value, axes, 0, 0, tiled=True)]
    ppermute x0 -> x9, waiting for transfers between devices: none -> 22.2 us  [shifted(): lax.ppermute(value, axis, [(k, (k + by) % size) for k in range(size)])]
    ppermute x0 -> x9, starting transfers between devices: none -> 19.4 us  [shifted(): lax.ppermute(value, axis, [(k, (k + by) % size) for k in range(size)])]
    all_to_all x3 -> x1, blocking collectives: 34.8 us -> 17.8 us  [exchange(): return lax.all_to_all(value, axes, 0, 0, tiled=True)]
    all_to_all x3 -> x2, starting transfers between devices: 23.2 us -> 13.8 us  [exchange(): return lax.all_to_all(value, axes, 0, 0, tiled=True)]
    pallas_call x4, Pallas kernels: 11.3 us -> 7.64 us  [the longest x1 3.13 us: inner(): call(gram_kernel, [SMEM] + [VMEM] * 5, [shape((BLOCK, BLOCK), half)] + [s...]
    unnamed x6 -> x4, local copies, waits for them, and re-layouts: 3.38 us -> 0.01 us
    broadcast_in_dim x2 -> x0, local copies, waits for them, and re-layouts: 1.3 us -> none  [the longest x1 1.3 us: body(): jnp.broadcast_to(right_diag, (8, OWN))]
  transfers between devices with their start and end apart: 3 -> 11, of which waited for: 3 -> 5; matrix products, arithmetic and copies ran while one was open for 3% -> 0% of each run, Pallas kernels for 3% -> 0%
where the time goes in v2:
time: 84.9 us; the launch traced here: 84.5 us
  starting transfers between devices  33.2 us (39%)
  waiting for transfers between devices  22.6 us (27%)
  blocking collectives  17.8 us (21%)
  Pallas kernels  7.64 us (9%)
  between operations  3.26 us (4%)
    ppermute x9, waiting for transfers between devices, shifted(): lax.ppermute(value, axis, [(k, (k + by) % size) for k in range(size)])  22.2 us
    ppermute x9, starting transfers between devices, shifted(): lax.ppermute(value, axis, [(k, (k + by) % size) for k in range(size)])  19.4 us
    all_to_all x1, blocking collectives, exchange(): return lax.all_to_all(value, axes, 0, 0, tiled=True)  17.8 us
    all_to_all x2, starting transfers between devices, exchange(): return lax.all_to_all(value, axes, 0, 0, tiled=True)  13.8 us
    pallas_call x1, Pallas kernels, inner(): call(gram_kernel, [SMEM] + [VMEM] * 5, [shape((BLOCK, BLOCK), half)] + [s...  3.13 us
    pallas_call x1, Pallas kernels, inner(): pl.pallas_call(pack_kernel, out_shape=shape((16, ROWS, MESSAGE), half), i...  2.88 us
  transfers between devices with their start and end apart: 11, of which 5 were waited for; matrix products, arithmetic and copies ran while one was open for 0% of the time, Pallas kernels for 0%

profile of v2, /device:TPU:1, one launch (start us, length us, event | category | flops | bytes accessed | tf_op | source)
XLA Modules:
  0.0 84.5 jit_solution(15239971434011606621)
XLA Ops:
  0.6 2.9 %pack.1 = bf16[16,32,2304]{2,1,0:T(8,128)(2,1)} custom-call(bf16[1,32,28672]{2,1,0:T(8,128)(2,1)} %gradient.1, f32[1,32,512]{2,1,0:T(8,128)} %factor.3), custom_call_target="tpu_custom_call" | custom-call | flops 2000000 | bytes 4194304 | tf_op jit(solution)/shard_map/pack/pallas_call | solution.py:154
  3.5 0.0 copy-start.1
  3.5 7.2 %all-to-all-start = ((bf16[16,32,2304]{2,1,0:T(8,128)(2,1)}), bf16[16,32,2304]{2,1,0:T(8,128)(2,1)S(1)}, u32[]{:S(2)}, u32[]{:S(2)}) async-start(bf16[16,32,2304]{2,1,0:T(8,128)(2,1)} %pack.1), calls=%async_computation | async-start | bytes 4718592 | tf_op jit(solution)/shard_map/all_to_all | solution.py:144
  10.7 1.3 %collective-permute-start = (s32[1]{0:T(128)}, s32[1]{0:T(128)}, u32[]{:S(2)}, u32[]{:S(2)}) collective-permute-start(s32[1]{0:T(128)} %param.7), channel_id=1, source_target_pairs={{0,64},{64,128},{128,192},{192,0},{1,65},{65,129},{129,193},{193,1... | collective-permute-start | bytes 20 | tf_op jit(solution)/shard_map/ppermute | solution.py:149
  12.0 2.6 %collective-permute-start.1 = (s32[1]{0:T(128)}, s32[1]{0:T(128)}, u32[]{:S(2)}, u32[]{:S(2)}) collective-permute-start(s32[1]{0:T(128)} %param.7), channel_id=1, source_target_pairs={{0,128},{64,192},{128,0},{192,64},{1,129},{65,193},{129,1},{193,65... | collective-permute-start | bytes 20 | tf_op jit(solution)/shard_map/ppermute | solution.py:149
  14.6 1.1 %collective-permute-start.2 = (s32[1]{0:T(128)}, s32[1]{0:T(128)}, u32[]{:S(2)}, u32[]{:S(2)}) collective-permute-start(s32[1]{0:T(128)} %param.7), channel_id=1, source_target_pairs={{0,192},{64,0},{128,64},{192,128},{1,193},{65,1},{129,65},{193,129... | collective-permute-start | bytes 20 | tf_op jit(solution)/shard_map/ppermute | solution.py:149
  15.7 0.0 copy-done.1
  15.7 3.0 %collective-permute-start.3 = (f32[1,448]{1,0:T(1,128)S(1)}, f32[1,448]{1,0:T(1,128)S(1)}, u32[]{:S(2)}, u32[]{:S(2)}) collective-permute-start(f32[1,448]{1,0:T(1,128)S(1)} %copy-done.1), channel_id=1, source_target_pairs={{0,16},{16,32},{32,48},{48,0},{1,17},{17,33},{33,49},{49,1},{2,18}... | collective-permute-start | bytes 5384 | tf_op jit(solution)/shard_map/ppermute | solution.py:149
  18.7 4.2 %collective-permute-start.4 = (f32[1,448]{1,0:T(1,128)S(1)}, f32[1,448]{1,0:T(1,128)S(1)}, u32[]{:S(2)}, u32[]{:S(2)}) collective-permute-start(f32[1,448]{1,0:T(1,128)S(1)} %copy-done.1), channel_id=1, source_target_pairs={{0,32},{16,48},{32,0},{48,16},{1,33},{17,49},{33,1},{49,17},{2,34}... | collective-permute-start | bytes 5384 | tf_op jit(solution)/shard_map/ppermute | solution.py:149
  23.6 0.0 collective-permute-done
  23.6 2.5 %collective-permute-start.5 = (f32[1,448]{1,0:T(1,128)S(1)}, f32[1,448]{1,0:T(1,128)S(1)}, u32[]{:S(2)}, u32[]{:S(2)}) collective-permute-start(f32[1,448]{1,0:T(1,128)S(1)} %copy-done.1), channel_id=1, source_target_pairs={{0,48},{16,0},{32,16},{48,32},{1,49},{17,1},{33,17},{49,33},{2,50}... | collective-permute-start | bytes 5384 | tf_op jit(solution)/shard_map/ppermute | solution.py:149
  26.7 0.0 collective-permute-done.1
  27.2 0.0 collective-permute-done.2
  28.0 0.1 pad_maximum_fusion.scales
  28.0 16.7 %collective-permute-done.3.right1 = f32[1,448]{1,0:T(1,128)S(1)} collective-permute-done((f32[1,448]{1,0:T(1,128)S(1)}, f32[1,448]{1,0:T(1,128)S(1)}, u32[]{:S(2)}, u32[]{:S(2)}) %collective-permute-start.3) | collective-permute-done | bytes 1824 | tf_op jit(solution)/shard_map/ppermute | solution.py:149
  44.7 1.0 %collective-permute-done.4.right2 = f32[1,448]{1,0:T(1,128)S(1)} collective-permute-done((f32[1,448]{1,0:T(1,128)S(1)}, f32[1,448]{1,0:T(1,128)S(1)}, u32[]{:S(2)}, u32[]{:S(2)}) %collective-permute-start.4) | collective-permute-done | bytes 1824 | tf_op jit(solution)/shard_map/ppermute | solution.py:149
  45.7 0.0 collective-permute-done.5.right3
  45.7 0.0 all-to-all-done
  45.7 0.0 copy-start
  45.7 3.1 %shard_map.59 = (bf16[512,512]{1,0:T(8,128)(2,1)}, f32[1,448]{1,0:T(1,128)S(1)}, f32[1,448]{1,0:T(1,128)S(1)}, f32[1,448]{1,0:T(1,128)S(1)}, f32[1,448]{1,0:T(1,128)S(1)}) custom-call(f32[2]{0:T(128)S(1)} %pad_maximum_fusion.scales, bf16[512,2304]{1,0:T(8,128)(2,1)S(1)} %bitcast.2, f32[1,448]{1,0:T(1,128)S(1)} %copy-done.1, ...), custom_call_target="tpu_custom_call" | custom-call | flops 1600000000 | bytes 2097152 | tf_op jit(solution)/shard_map/pallas_call | solution.py:178
  48.8 6.6 %all-to-all-start.1 = ((bf16[16,32,512]{2,1,0:T(8,128)(2,1)}), bf16[16,32,512]{2,1,0:T(8,128)(2,1)S(1)}, u32[]{:S(2)}, u32[]{:S(2)}) async-start(bf16[16,32,512]{2,1,0:T(8,128)(2,1)} %bitcast.1), calls=%async_computation.1 | async-start | bytes 1048576 | tf_op jit(solution)/shard_map/all_to_all | solution.py:144
  55.4 1.5 %collective-permute-start.6 = (f32[1,448]{1,0:T(1,128)S(1)}, f32[1,448]{1,0:T(1,128)S(1)}, u32[]{:S(2)}, u32[]{:S(2)}) collective-permute-start(f32[1,448]{1,0:T(1,128)S(1)} %get-tuple-element.12), channel_id=1, source_target_pairs={{0,48},{16,0},{32,16},{48,32},{1,49},{17,1},{33,17},{49,33},{2,50}... | collective-permute-start | bytes 5384 | tf_op jit(solution)/shard_map/ppermute | solution.py:149
  57.0 3.0 %collective-permute-start.7 = (f32[1,448]{1,0:T(1,128)S(1)}, f32[1,448]{1,0:T(1,128)S(1)}, u32[]{:S(2)}, u32[]{:S(2)}) collective-permute-start(f32[1,448]{1,0:T(1,128)S(1)} %get-tuple-element.13), channel_id=1, source_target_pairs={{0,32},{16,48},{32,0},{48,16},{1,33},{17,49},{33,1},{49,17},{2,34}... | collective-permute-start | bytes 5384 | tf_op jit(solution)/shard_map/ppermute | solution.py:149
  59.9 0.3 collective-permute-start.8
  60.2 0.0 collective-permute-done.6.sum1
  60.2 4.3 %collective-permute-done.7.sum2 = f32[1,448]{1,0:T(1,128)S(1)} collective-permute-done((f32[1,448]{1,0:T(1,128)S(1)}, f32[1,448]{1,0:T(1,128)S(1)}, u32[]{:S(2)}, u32[]{:S(2)}) %collective-permute-start.7) | collective-permute-done | bytes 1824 | tf_op jit(solution)/shard_map/ppermute | solution.py:149
  64.6 0.2 collective-permute-done.8.sum3
  64.8 0.3 all-to-all-done.1.parts
  65.1 0.8 shard_map.60
  65.9 17.8 %all_to_all.15.levels = f32[64,1,128]{2,1,0:T(1,128)S(1)} all-to-all(f32[64,1,128]{2,1,0:T(1,128)S(1)} %get-tuple-element.15), channel_id=1, replica_groups=mesh['expert'=4,'zh'=4,'zl'=2,'x'=4,'c'=2] {'zh','zl','x','c'}, dimensions={0} | all-to-all | bytes 65536 | tf_op jit(solution)/shard_map/all_to_all | solution.py:144
  83.7 0.0 copy-done
  83.7 0.9 %shard_map.61 = (f32[1,32,512]{2,1,0:T(8,128)}, f32[1,448]{1,0:T(1,128)}) custom-call(f32[64,1,128]{2,1,0:T(1,128)S(1)} %all_to_all.15.levels, f32[32,512]{1,0:T(8,128)S(1)} %get-tuple-element.16.upper, bf16[512,2304]{1,0:T(8,128)(2,1)S(1)} %bitcast.3, f32[1,32,512]{2,1,0:T(8,128)S(1)} %copy-done, f32[1,448]{1,0:T(1,128)S(1)} %get-tuple-element.17.term, ...), custom_call_target="tpu_custom_call" | custom-call | flops 17000000 | bytes 2097152 | tf_op jit(solution)/shard_map/pallas_call | solution.py:194
Async XLA Ops:
  3.5 12.2 %copy-start.1 = (f32[1,448]{1,0:T(1,128)S(1)}, f32[1,448]{1,0:T(1,128)}, u32[]{:S(2)}) copy-start(f32[1,448]{1,0:T(1,128)} %right.1) | copy-start | bytes 5380
  3.5 42.1 %all-to-all-start = ((bf16[16,32,2304]{2,1,0:T(8,128)(2,1)}), bf16[16,32,2304]{2,1,0:T(8,128)(2,1)S(1)}, u32[]{:S(2)}, u32[]{:S(2)}) async-start(bf16[16,32,2304]{2,1,0:T(8,128)(2,1)} %pack.1), calls=%async_computation | async-start | bytes 4718592 | tf_op jit(solution)/shard_map/all_to_all | solution.py:144
  10.7 12.8 %collective-permute-start = (s32[1]{0:T(128)}, s32[1]{0:T(128)}, u32[]{:S(2)}, u32[]{:S(2)}) collective-permute-start(s32[1]{0:T(128)} %param.7), channel_id=1, source_target_pairs={{0,64},{64,128},{128,192},{192,0},{1,65},{65,129},{129,193},{193,1... | collective-permute-start | bytes 20 | tf_op jit(solution)/shard_map/ppermute | solution.py:149
  12.0 14.7 %collective-permute-start.1 = (s32[1]{0:T(128)}, s32[1]{0:T(128)}, u32[]{:S(2)}, u32[]{:S(2)}) collective-permute-start(s32[1]{0:T(128)} %param.7), channel_id=1, source_target_pairs={{0,128},{64,192},{128,0},{192,64},{1,129},{65,193},{129,1},{193,65... | collective-permute-start | bytes 20 | tf_op jit(solution)/shard_map/ppermute | solution.py:149
  14.6 12.6 %collective-permute-start.2 = (s32[1]{0:T(128)}, s32[1]{0:T(128)}, u32[]{:S(2)}, u32[]{:S(2)}) collective-permute-start(s32[1]{0:T(128)} %param.7), channel_id=1, source_target_pairs={{0,192},{64,0},{128,64},{192,128},{1,193},{65,1},{129,65},{193,129... | collective-permute-start | bytes 20 | tf_op jit(solution)/shard_map/ppermute | solution.py:149
  15.7 29.0 %collective-permute-start.3 = (f32[1,448]{1,0:T(1,128)S(1)}, f32[1,448]{1,0:T(1,128)S(1)}, u32[]{:S(2)}, u32[]{:S(2)}) collective-permute-start(f32[1,448]{1,0:T(1,128)S(1)} %copy-done.1), channel_id=1, source_target_pairs={{0,16},{16,32},{32,48},{48,0},{1,17},{17,33},{33,49},{49,1},{2,18}... | collective-permute-start | bytes 5384 | tf_op jit(solution)/shard_map/ppermute | solution.py:149
  18.7 27.0 %collective-permute-start.4 = (f32[1,448]{1,0:T(1,128)S(1)}, f32[1,448]{1,0:T(1,128)S(1)}, u32[]{:S(2)}, u32[]{:S(2)}) collective-permute-start(f32[1,448]{1,0:T(1,128)S(1)} %copy-done.1), channel_id=1, source_target_pairs={{0,32},{16,48},{32,0},{48,16},{1,33},{17,49},{33,1},{49,17},{2,34}... | collective-permute-start | bytes 5384 | tf_op jit(solution)/shard_map/ppermute | solution.py:149
  23.6 22.1 %collective-permute-start.5 = (f32[1,448]{1,0:T(1,128)S(1)}, f32[1,448]{1,0:T(1,128)S(1)}, u32[]{:S(2)}, u32[]{:S(2)}) collective-permute-start(f32[1,448]{1,0:T(1,128)S(1)} %copy-done.1), channel_id=1, source_target_pairs={{0,48},{16,0},{32,16},{48,32},{1,49},{17,1},{33,17},{49,33},{2,50}... | collective-permute-start | bytes 5384 | tf_op jit(solution)/shard_map/ppermute | solution.py:149
  45.7 38.0 %copy-start = (f32[1,32,512]{2,1,0:T(8,128)S(1)}, f32[1,32,512]{2,1,0:T(8,128)}, u32[]{:S(2)}) copy-start(f32[1,32,512]{2,1,0:T(8,128)} %factor.3) | copy-start | bytes 196612
  48.8 16.3 %all-to-all-start.1 = ((bf16[16,32,512]{2,1,0:T(8,128)(2,1)}), bf16[16,32,512]{2,1,0:T(8,128)(2,1)S(1)}, u32[]{:S(2)}, u32[]{:S(2)}) async-start(bf16[16,32,512]{2,1,0:T(8,128)(2,1)} %bitcast.1), calls=%async_computation.1 | async-start | bytes 1048576 | tf_op jit(solution)/shard_map/all_to_all | solution.py:144
  55.4 4.8 %collective-permute-start.6 = (f32[1,448]{1,0:T(1,128)S(1)}, f32[1,448]{1,0:T(1,128)S(1)}, u32[]{:S(2)}, u32[]{:S(2)}) collective-permute-start(f32[1,448]{1,0:T(1,128)S(1)} %get-tuple-element.12), channel_id=1, source_target_pairs={{0,48},{16,0},{32,16},{48,32},{1,49},{17,1},{33,17},{49,33},{2,50}... | collective-permute-start | bytes 5384 | tf_op jit(solution)/shard_map/ppermute | solution.py:149
  57.0 7.6 %collective-permute-start.7 = (f32[1,448]{1,0:T(1,128)S(1)}, f32[1,448]{1,0:T(1,128)S(1)}, u32[]{:S(2)}, u32[]{:S(2)}) collective-permute-start(f32[1,448]{1,0:T(1,128)S(1)} %get-tuple-element.13), channel_id=1, source_target_pairs={{0,32},{16,48},{32,0},{48,16},{1,33},{17,49},{33,1},{49,17},{2,34}... | collective-permute-start | bytes 5384 | tf_op jit(solution)/shard_map/ppermute | solution.py:149
  59.9 4.8 %collective-permute-start.8 = (f32[1,448]{1,0:T(1,128)S(1)}, f32[1,448]{1,0:T(1,128)S(1)}, u32[]{:S(2)}, u32[]{:S(2)}) collective-permute-start(f32[1,448]{1,0:T(1,128)S(1)} %get-tuple-element.14), channel_id=1, source_target_pairs={{0,16},{16,32},{32,48},{48,0},{1,17},{17,33},{33,49},{49,1},{2,18}... | collective-permute-start | bytes 5384 | tf_op jit(solution)/shard_map/ppermute | solution.py:149

commit v3 on v2

v3 whole, which is shorter than its diff:
```python
import jax
import jax.numpy as jnp
from jax import lax
from jax.experimental import pallas as pl
from jax.experimental.pallas import tpu as pltpu
from jax.sharding import Mesh
from jax.sharding import PartitionSpec as P


SHARD = ("zh", "zl", "x", "c")
GROUP = ("zl", "x", "c")
FF2 = 28672
DIM = 2048
BLOCK = 512
ROWS = 32
OWN = 448
PAIR = 896
SPAN = 16 * OWN
HALF = 8 * OWN
OFFSETS = (
    (1, 0, 0), (0, 2, 0), (1, 0, 1), (0, 2, 1), (1, 1, 0), (0, 3, 0), (1, 3, 0), (0, 1, 0),
    (1, 1, 1), (0, 3, 1), (1, 3, 1), (0, 1, 1), (1, 2, 0), (1, 2, 1), (0, 0, 1), (0, 0, 0),
)
PEERS = len(OFFSETS)
WIDE = 1792
MESSAGE = BLOCK + WIDE

step_rate = 0.5
epsilon = 1e-06


VMEM = pl.BlockSpec(memory_space=pltpu.VMEM)
HBM = pl.BlockSpec(memory_space=pltpu.HBM)
SMEM = pl.BlockSpec(memory_space=pltpu.SMEM)


def pack_kernel(gradient, factor, counts, *refs):
    outs, notes, (near, rows, sems) = refs[:PEERS], refs[PEERS], refs[PEERS + 1 :]
    block, plane = lax.axis_index("zh"), lax.axis_index("zl")
    x, c = lax.axis_index("x"), lax.axis_index("c")
    fetches = [pltpu.make_async_copy(factor, rows, sems.at[8])]
    for dz in range(2):
        for d in range(4):
            begin = pl.multiple_of((block ^ d) * SPAN + lax.rem(plane + dz, 2) * HALF, 128)
            source = gradient.at[0, :, pl.ds(begin, HALF)]
            fetches.append(pltpu.make_async_copy(source, near.at[dz, d], sems.at[4 * dz + d]))
    for fetch in fetches:
        fetch.start()
    notes[...] = jnp.full(notes.shape, counts[0].astype(jnp.float32), jnp.float32)
    fetches[0].wait()
    narrow = rows[0].astype(jnp.bfloat16)
    for out in outs:
        out[:, :BLOCK] = narrow
    for dz in range(2):
        for fetch in fetches[1 + 4 * dz : 5 + 4 * dz]:
            fetch.wait()
        for dx in range(4):
            begin = pl.multiple_of(lax.rem(x + dx, 4) * PAIR, 128)
            same, other = outs[OFFSETS.index((dz, dx, 0))], outs[OFFSETS.index((dz, dx, 1))]
            for q in range(2):
                pairs = [near[dz, 2 * q + k, :, pl.ds(begin, PAIR)] for k in range(2)]
                even = jnp.concatenate([pair[:, :OWN] for pair in pairs], axis=1)
                odd = jnp.concatenate([pair[:, OWN:] for pair in pairs], axis=1)
                left = BLOCK + q * PAIR
                same[:, left : left + PAIR] = jnp.where(c == 0, even, odd)
                other[:, left : left + PAIR] = jnp.where(c == 0, odd, even)


def gram_kernel(*refs):
    rights, tokens, staying = refs[0:4], refs[4:8], refs[8]
    crosses, refs = refs[9 : PEERS + 8], refs[9:]
    part, sum0, sum1, sum2, sum3, narrow, level, got, image = refs[PEERS - 1 :]
    plane, x, c = lax.axis_index("zl"), lax.axis_index("x"), lax.axis_index("c")
    own = pl.multiple_of((plane * 8 + x * 2 + c) * ROWS, ROWS)
    got[pl.ds(own, ROWS), :] = staying[...]
    total = (tokens[0][...] + tokens[1][...]) + (tokens[2][...] + tokens[3][...])
    weight = (4 * tokens[0][...] / total)[:, 0:1]
    squared = weight * weight
    level[...] = jnp.broadcast_to(squared, level.shape)
    for k, (dz, dx, dc) in enumerate(OFFSETS[:-1]):
        source = lax.rem(plane + dz, 2) * 8 + lax.rem(x + (4 - dx), 4) * 2 + lax.rem(c + dc, 2)
        got[pl.ds(pl.multiple_of(source * ROWS, ROWS), ROWS), :] = crosses[k][...]
    narrow[...] = got[:, :BLOCK]
    right = jnp.concatenate([one[...] for one in rights], axis=1)
    upper_left = got[0:256, 0:512]
    lower_right = got[256:512, 256:512]
    totals = []
    for k in range(7):
        at = BLOCK + k * 256
        scale = right[:, k * 256 : (k + 1) * 256]
        high = jnp.dot(upper_left, got[:, at : at + 256], preferred_element_type=jnp.float32)
        low = jnp.dot(lower_right, got[256:512, at : at + 256], preferred_element_type=jnp.float32)
        high = (high * scale).astype(jnp.bfloat16)
        low = (low * scale).astype(jnp.bfloat16)
        image[0:256, k * 256 : (k + 1) * 256] = high
        image[256:512, k * 256 : (k + 1) * 256] = low
        total = jnp.sum(jnp.square(high.astype(jnp.float32)), axis=0, keepdims=True)
        total = total + jnp.sum(jnp.square(low.astype(jnp.float32)), axis=0, keepdims=True)
        totals.append(total)
    total = jnp.concatenate(totals, axis=1)
    for d, out in enumerate((sum0, sum1, sum2, sum3)):
        out[...] = total[:, d * OWN : (d + 1) * OWN]
    last = (((1,), (1,)), ((), ()))
    scale = squared / FF2
    high = lax.dot_general(image[0:256, :], image[...], last, preferred_element_type=jnp.float32)
    low = lax.dot_general(image[256:512, :], image[256:512, :], last, preferred_element_type=jnp.float32)
    share = jnp.float32(1.0 / 16.0)
    row_high = lax.broadcasted_iota(jnp.int32, (256, 512), 0)
    col_high = lax.broadcasted_iota(jnp.int32, (256, 512), 1)
    row_low = lax.broadcasted_iota(jnp.int32, (256, 256), 0)
    col_low = lax.broadcasted_iota(jnp.int32, (256, 256), 1)
    part[0:256, :] = (high * scale - jnp.where(row_high == col_high, share, 0.0)).astype(part.dtype)
    part[256:512, 256:512] = (low * scale - jnp.where(row_low == col_low, share, 0.0)).astype(part.dtype)
    part[256:512, 0:256] = jnp.zeros((256, 256), part.dtype)


def peaks_kernel(squared, parts, sum0, sum1, sum2, sum3, upper, term, levels):
    first = lax.axis_index(GROUP) * ROWS
    total = parts[0].astype(jnp.float32)
    for k in range(1, 16):
        total = total + parts[k].astype(jnp.float32)
    row = lax.broadcasted_iota(jnp.int32, (ROWS, BLOCK), 0) + first
    col = lax.broadcasted_iota(jnp.int32, (ROWS, BLOCK), 1)
    total = jnp.where(col >= row, total, 0.0)
    upper[...] = total
    row_level = jnp.max(jnp.abs(total))
    added = (sum0[...] + sum1[...]) + (sum2[...] + sum3[...])
    column_term = squared[0:1, 0:1] * added / DIM - 1.0
    term[...] = column_term
    column_level = jnp.max(jnp.abs(column_term))
    lane = lax.broadcasted_iota(jnp.int32, levels.shape, 2)
    levels[...] = jnp.where(lane == 0, row_level, column_level)


def final_kernel(levels, upper, narrow, factor, term, right, new_factor, new_right):
    peak = jnp.max(levels[...], axis=0)
    row_peak = jnp.max(peak[0:1, 0:1])
    column_peak = jnp.max(peak[0:1, 1:2])
    steps = (upper[...] / (row_peak + epsilon)).astype(jnp.bfloat16)
    moved = jnp.dot(steps, narrow[...], preferred_element_type=jnp.float32)
    new_factor[0] = factor[0] - step_rate * moved
    new_right[...] = right[...] - step_rate * term[...] / (column_peak + epsilon) * right[...]


def shape(dims, dtype=jnp.float32):
    return jax.ShapeDtypeStruct(dims, dtype)


def call(kernel, ins, outs, flops, scratch=(), room=16):
    return pl.pallas_call(
        kernel,
        out_shape=outs,
        grid=(1,),
        in_specs=ins,
        out_specs=[VMEM] * len(outs),
        scratch_shapes=list(scratch),
        compiler_params=pltpu.CompilerParams(vmem_limit_bytes=room * 1024 * 1024),
        cost_estimate=pl.CostEstimate(flops=flops, bytes_accessed=2097152, transcendentals=0),
    )


def exchange(value, axes):
    return lax.all_to_all(value, axes, 0, 0, tiled=True)


def across(value, turn, axis="zh"):
    return lax.ppermute(value, axis, [(k, k ^ turn) for k in range(4)])


def to_peer(value, dz, dx, dc):
    pairs = []
    for device in range(16):
        plane, x, c = device // 8, device // 2 % 4, device % 2
        pairs.append((device, (plane + dz) % 2 * 8 + (x + dx) % 4 * 2 + (c + dc) % 2))
    return lax.ppermute(value, GROUP, pairs)


def pack(gradient, factor, counts):
    half = jnp.bfloat16
    outs = [shape((ROWS, MESSAGE), half)] * PEERS
    return pl.pallas_call(
        pack_kernel,
        out_shape=outs + [shape((1, 128))],
        in_specs=[HBM, HBM, SMEM],
        out_specs=[VMEM] * (PEERS + 1),
        scratch_shapes=[
            pltpu.VMEM((2, 4, ROWS, HALF), half),
            pltpu.VMEM((1, ROWS, BLOCK), jnp.float32),
            pltpu.SemaphoreType.DMA((9,)),
        ],
        compiler_params=pltpu.CompilerParams(vmem_limit_bytes=51 * 1024 * 1024),
        cost_estimate=pl.CostEstimate(flops=2000000, bytes_accessed=4194304, transcendentals=0),
        name="pack",
    )(gradient, factor, counts)


def inner(gradient, factor, right_diag, counts):
    half = jnp.bfloat16
    *leaving, staying, token = pack(gradient, factor, counts)
    crosses = [to_peer(value, *OFFSETS[k]) for k, value in enumerate(leaving)]
    rights = [right_diag] + [across(right_diag, d) for d in (1, 2, 3)]
    tokens = [token] + [across(token, d, "expert") for d in (1, 2, 3)]
    part, *sums, narrow, squared = call(
        gram_kernel,
        [VMEM] * (PEERS + 8),
        [shape((BLOCK, BLOCK), half)] + [shape((1, OWN))] * 4 + [shape((BLOCK, BLOCK), half), shape((1, 128))],
        1600000000,
        [pltpu.VMEM((BLOCK, MESSAGE), half), pltpu.VMEM((BLOCK, WIDE), half)],
    )(*rights, *tokens, staying, *crosses)
    parts = exchange(part.reshape(16, ROWS, BLOCK), GROUP)
    sums = [sums[0]] + [across(sums[d], d) for d in (1, 2, 3)]
    upper, term, levels = call(
        peaks_kernel,
        [VMEM] * 6,
        [shape((ROWS, BLOCK)), shape((1, OWN)), shape((64, 1, 128))],
        2000000,
    )(squared, parts, *sums)
    levels = exchange(levels, SHARD)
    new_factor, new_right = call(
        final_kernel, [VMEM] * 6, [shape((1, ROWS, BLOCK)), shape((1, OWN))], 17000000
    )(levels, upper, narrow, factor, term, right_diag)
    return new_factor, new_right


def solution(mesh):
    torus = Mesh(
        mesh.devices.reshape(mesh.shape["expert"], 4, 2, 4, 2),
        ("expert", "zh", "zl", "x", "c"),
    )
    return jax.shard_map(
        inner,
        mesh=torus,
        in_specs=(
            P("expert", SHARD, None),
            P("expert", SHARD, None),
            P("expert", SHARD),
            P("expert"),
        ),
        out_specs=(P("expert", SHARD, None), P("expert", SHARD)),
        check_vma=False,
    )
```

time: 84.9 us -> 93.2 us (1.098)
  starting transfers between devices: 33.2 us -> 44.3 us
  between operations: 3.26 us -> 1.36 us
  Pallas kernels: 7.64 us -> 5.86 us
    ppermute x9 -> x24, starting transfers between devices: 19.4 us -> 39 us  [the longest x15 20.8 us: to_peer(): return lax.ppermute(value, GROUP, pairs)]
    all_to_all x2 -> x1, starting transfers between devices: 13.8 us -> 5.25 us  [exchange(): return lax.all_to_all(value, axes, 0, 0, tiled=True)]
    pallas_call x4, Pallas kernels: 7.64 us -> 5.86 us  [the longest x1 2.86 us: inner(): call(gram_kernel, [VMEM] * (PEERS + 8), [shape((BLOCK, BLOCK), half)] + [...]
    ppermute x9 -> x24, waiting for transfers between devices: 22.2 us -> 23.5 us  [the longest x15 14.5 us: to_peer(): return lax.ppermute(value, GROUP, pairs)]
  transfers between devices with their start and end apart: 11 -> 25, of which waited for: 5 -> 8; matrix products, arithmetic and copies ran while one was open for 0% -> 0% of each run, Pallas kernels for 0% -> 2%
where the time goes in v3:
time: 93.2 us; the launch traced here: 92.9 us
  starting transfers between devices  44.3 us (48%)
  waiting for transfers between devices  23.5 us (25%)
  blocking collectives  17.1 us (18%)
  Pallas kernels  5.86 us (6%)
  between operations  1.36 us (1%)
    ppermute x15, starting transfers between devices, to_peer(): return lax.ppermute(value, GROUP, pairs)  20.8 us
    ppermute x9, starting transfers between devices, across(): return lax.ppermute(value, axis, [(k, k ^ turn) for k in range(4)])  18.3 us
    all_to_all x1, blocking collectives, exchange(): return lax.all_to_all(value, axes, 0, 0, tiled=True)  17.1 us
    ppermute x15, waiting for transfers between devices, to_peer(): return lax.ppermute(value, GROUP, pairs)  14.5 us
    ppermute x9, waiting for transfers between devices, across(): return lax.ppermute(value, axis, [(k, k ^ turn) for k in range(4)])  8.97 us
    all_to_all x1, starting transfers between devices, exchange(): return lax.all_to_all(value, axes, 0, 0, tiled=True)  5.25 us
    pallas_call x1, Pallas kernels, inner(): call(gram_kernel, [VMEM] * (PEERS + 8), [shape((BLOCK, BLOCK), half)] + [...  2.86 us
    pallas_call x1, Pallas kernels, pack(): pl.pallas_call(pack_kernel, out_shape=outs + [shape((1, 128))], in_specs=...  1.92 us
  transfers between devices with their start and end apart: 25, of which 8 were waited for; matrix products, arithmetic and copies ran while one was open for 0% of the time, Pallas kernels for 2%

profile of v3, /device:TPU:1, one launch (start us, length us, event | category | flops | bytes accessed | tf_op | source)
XLA Modules:
  0.0 92.9 jit_solution(13112644275957136963)
XLA Ops:
  0.6 6.9 %collective-permute-start.2 = (f32[1,448]{1,0:T(1,128)}, f32[1,448]{1,0:T(1,128)S(1)}, u32[]{:S(2)}, u32[]{:S(2)}) collective-permute-start(f32[1,448]{1,0:T(1,128)} %right.1), channel_id=1, source_target_pairs={{0,48},{16,32},{32,16},{48,0},{1,49},{17,33},{33,17},{49,1},{2,50}... | collective-permute-start | bytes 5384 | tf_op jit(solution)/shard_map/ppermute | solution.py:167
  7.6 1.0 %collective-permute-start.1 = (f32[1,448]{1,0:T(1,128)}, f32[1,448]{1,0:T(1,128)S(1)}, u32[]{:S(2)}, u32[]{:S(2)}) collective-permute-start(f32[1,448]{1,0:T(1,128)} %right.1), channel_id=1, source_target_pairs={{0,32},{16,48},{32,0},{48,16},{1,33},{17,49},{33,1},{49,17},{2,34}... | collective-permute-start | bytes 5384 | tf_op jit(solution)/shard_map/ppermute | solution.py:167
  8.5 1.2 %collective-permute-start = (f32[1,448]{1,0:T(1,128)}, f32[1,448]{1,0:T(1,128)S(1)}, u32[]{:S(2)}, u32[]{:S(2)}) collective-permute-start(f32[1,448]{1,0:T(1,128)} %right.1), channel_id=1, source_target_pairs={{0,16},{16,0},{32,48},{48,32},{1,17},{17,1},{33,49},{49,33},{2,18}... | collective-permute-start | bytes 5384 | tf_op jit(solution)/shard_map/ppermute | solution.py:167
  10.4 0.0 copy-start
  10.4 0.8 copy-done
  11.2 1.9 %pack.1 = (bf16[32,2304]{1,0:T(8,128)(2,1)S(1)}, bf16[32,2304]{1,0:T(8,128)(2,1)S(1)}, bf16[32,2304]{1,0:T(8,128)(2,1)S(1)}, bf16[32,2304]{1,0:T(8,128)(2,1)S(1)...) custom-call(bf16[1,32,28672]{2,1,0:T(8,128)(2,1)} %gradient.1, ...), custom_call_target="tpu_custom_call" | custom-call | flops 2000000 | bytes 4194304 | tf_op jit(solution)/shard_map/pack/pallas_call | solution.py:181
  13.2 2.8 %collective-permute-start.5 = (f32[1,128]{1,0:T(1,128)S(1)}, f32[1,128]{1,0:T(1,128)S(1)}, u32[]{:S(2)}, u32[]{:S(2)}) collective-permute-start(f32[1,128]{1,0:T(1,128)S(1)} %get-tuple-element.29.refs_4_), channel_id=1, source_target_pairs={{0,192},{64,128},{128,64},{192,0},{1,193},{65,129},{129,65},{193,1... | collective-permute-start | bytes 1544 | tf_op jit(solution)/shard_map/ppermute | solution.py:167
  16.0 0.3 collective-permute-start.4
  16.3 0.6 collective-permute-done.5.refs_7_
  16.9 0.2 collective-permute-start.3
  17.1 2.8 %collective-permute-done.4.refs_6_ = f32[1,128]{1,0:T(1,128)S(1)} collective-permute-done((f32[1,128]{1,0:T(1,128)S(1)}, f32[1,128]{1,0:T(1,128)S(1)}, u32[]{:S(2)}, u32[]{:S(2)}) %collective-permute-start.4) | collective-permute-done | bytes 544 | tf_op jit(solution)/shard_map/ppermute | solution.py:167
  19.9 0.7 collective-permute-start.6
  20.6 0.0 collective-permute-done.3.refs_5_
  20.6 2.7 %collective-permute-start.7 = (bf16[32,2304]{1,0:T(8,128)(2,1)S(1)}, bf16[32,2304]{1,0:T(8,128)(2,1)S(1)}, u32[]{:S(2)}, u32[]{:S(2)}) collective-permute-start(bf16[32,2304]{1,0:T(8,128)(2,1)S(1)} %get-tuple-element.32), channel_id=1, source_target_pairs={{0,4},{1,5},{2,6},{3,7},{4,0},{5,1},{6,2},{7,3},{8,12},{9,13},{10,... | collective-permute-start | bytes 442376 | tf_op jit(solution)/shard_map/ppermute | solution.py:175
  23.4 0.0 collective-permute-done.2.refs_3_
  23.4 3.8 %collective-permute-start.8 = (bf16[32,2304]{1,0:T(8,128)(2,1)S(1)}, bf16[32,2304]{1,0:T(8,128)(2,1)S(1)}, u32[]{:S(2)}, u32[]{:S(2)}) collective-permute-start(bf16[32,2304]{1,0:T(8,128)(2,1)S(1)} %get-tuple-element.33), channel_id=1, source_target_pairs={{0,9},{1,8},{2,11},{3,10},{4,13},{5,12},{6,15},{7,14},{8,1},{9,0},... | collective-permute-start | bytes 442376 | tf_op jit(solution)/shard_map/ppermute | solution.py:175
  27.2 0.0 collective-permute-done.1.refs_2_
  27.2 0.0 collective-permute-start.9
  27.2 0.0 collective-permute-done.refs_1_
  27.2 1.2 %collective-permute-start.10 = (bf16[32,2304]{1,0:T(8,128)(2,1)S(1)}, bf16[32,2304]{1,0:T(8,128)(2,1)S(1)}, u32[]{:S(2)}, u32[]{:S(2)}) collective-permute-start(bf16[32,2304]{1,0:T(8,128)(2,1)S(1)} %get-tuple-element.35), channel_id=1, source_target_pairs={{0,10},{1,11},{2,12},{3,13},{4,14},{5,15},{6,8},{7,9},{8,2},{9,3},... | collective-permute-start | bytes 442376 | tf_op jit(solution)/shard_map/ppermute | solution.py:175
  28.5 0.0 collective-permute-done.6.refs_9_
  28.5 2.0 %collective-permute-start.11 = (bf16[32,2304]{1,0:T(8,128)(2,1)S(1)}, bf16[32,2304]{1,0:T(8,128)(2,1)S(1)}, u32[]{:S(2)}, u32[]{:S(2)}) collective-permute-start(bf16[32,2304]{1,0:T(8,128)(2,1)S(1)} %get-tuple-element.36), channel_id=1, source_target_pairs={{0,6},{1,7},{2,0},{3,1},{4,2},{5,3},{6,4},{7,5},{8,14},{9,15},{10,... | collective-permute-start | bytes 442376 | tf_op jit(solution)/shard_map/ppermute | solution.py:175
  30.5 0.0 collective-permute-done.7.refs_10_
  30.5 1.2 %collective-permute-start.12 = (bf16[32,2304]{1,0:T(8,128)(2,1)S(1)}, bf16[32,2304]{1,0:T(8,128)(2,1)S(1)}, u32[]{:S(2)}, u32[]{:S(2)}) collective-permute-start(bf16[32,2304]{1,0:T(8,128)(2,1)S(1)} %get-tuple-element.37), channel_id=1, source_target_pairs={{0,14},{1,15},{2,8},{3,9},{4,10},{5,11},{6,12},{7,13},{8,6},{9,7},... | collective-permute-start | bytes 442376 | tf_op jit(solution)/shard_map/ppermute | solution.py:175
  31.7 0.0 collective-permute-done.8.refs_11_
  31.7 0.7 collective-permute-start.13
  32.4 5.4 %collective-permute-done.9.refs_12_ = bf16[32,2304]{1,0:T(8,128)(2,1)S(1)} collective-permute-done((bf16[32,2304]{1,0:T(8,128)(2,1)S(1)}, bf16[32,2304]{1,0:T(8,128)(2,1)S(1)}, u32[]{:S(2)}, u32[]{:S(2)}) %collective-permute-start.9) | collective-permute-done | bytes 147488 | tf_op jit(solution)/shard_map/ppermute | solution.py:175
  37.8 3.4 %collective-permute-start.15 = (bf16[32,2304]{1,0:T(8,128)(2,1)S(1)}, bf16[32,2304]{1,0:T(8,128)(2,1)S(1)}, u32[]{:S(2)}, u32[]{:S(2)}) collective-permute-start(bf16[32,2304]{1,0:T(8,128)(2,1)S(1)} %get-tuple-element.40), channel_id=1, source_target_pairs={{0,7},{1,6},{2,1},{3,0},{4,3},{5,2},{6,5},{7,4},{8,15},{9,14},{10,... | collective-permute-start | bytes 442376 | tf_op jit(solution)/shard_map/ppermute | solution.py:175
  41.1 1.4 %collective-permute-start.16 = (bf16[32,2304]{1,0:T(8,128)(2,1)S(1)}, bf16[32,2304]{1,0:T(8,128)(2,1)S(1)}, u32[]{:S(2)}, u32[]{:S(2)}) collective-permute-start(bf16[32,2304]{1,0:T(8,128)(2,1)S(1)} %get-tuple-element.41), channel_id=1, source_target_pairs={{0,15},{1,14},{2,9},{3,8},{4,11},{5,10},{6,13},{7,12},{8,7},{9,6},... | collective-permute-start | bytes 442376 | tf_op jit(solution)/shard_map/ppermute | solution.py:175
  42.5 0.8 collective-permute-start.17
  43.4 1.4 %collective-permute-start.18 = (bf16[32,2304]{1,0:T(8,128)(2,1)S(1)}, bf16[32,2304]{1,0:T(8,128)(2,1)S(1)}, u32[]{:S(2)}, u32[]{:S(2)}) collective-permute-start(bf16[32,2304]{1,0:T(8,128)(2,1)S(1)} %get-tuple-element.43), channel_id=1, source_target_pairs={{0,12},{1,13},{2,14},{3,15},{4,8},{5,9},{6,10},{7,11},{8,4},{9,5},... | collective-permute-start | bytes 442376 | tf_op jit(solution)/shard_map/ppermute | solution.py:175
  44.8 0.5 collective-permute-done.14.refs_17_
  45.2 1.3 %collective-permute-start.19 = (bf16[32,2304]{1,0:T(8,128)(2,1)S(1)}, bf16[32,2304]{1,0:T(8,128)(2,1)S(1)}, u32[]{:S(2)}, u32[]{:S(2)}) collective-permute-start(bf16[32,2304]{1,0:T(8,128)(2,1)S(1)} %get-tuple-element.44), channel_id=1, source_target_pairs={{0,13},{1,12},{2,15},{3,14},{4,9},{5,8},{6,11},{7,10},{8,5},{9,4},... | collective-permute-start | bytes 442376 | tf_op jit(solution)/shard_map/ppermute | solution.py:175
  46.5 6.8 %collective-permute-done.15.refs_18_ = bf16[32,2304]{1,0:T(8,128)(2,1)S(1)} collective-permute-done((bf16[32,2304]{1,0:T(8,128)(2,1)S(1)}, bf16[32,2304]{1,0:T(8,128)(2,1)S(1)}, u32[]{:S(2)}, u32[]{:S(2)}) %collective-permute-start.15) | collective-permute-done | bytes 147488 | tf_op jit(solution)/shard_map/ppermute | solution.py:175
  53.3 0.0 collective-permute-start.20
  53.4 0.0 collective-permute-done.16.refs_19_
  53.4 1.9 %collective-permute-done.17.refs_20_ = bf16[32,2304]{1,0:T(8,128)(2,1)S(1)} collective-permute-done((bf16[32,2304]{1,0:T(8,128)(2,1)S(1)}, bf16[32,2304]{1,0:T(8,128)(2,1)S(1)}, u32[]{:S(2)}, u32[]{:S(2)}) %collective-permute-start.17) | collective-permute-done | bytes 147488 | tf_op jit(solution)/shard_map/ppermute | solution.py:175
  55.2 0.0 copy-start.1
  55.3 2.9 %shard_map.59 = (bf16[512,512]{1,0:T(8,128)(2,1)}, f32[1,448]{1,0:T(1,128)S(1)}, f32[1,448]{1,0:T(1,128)S(1)}, f32[1,448]{1,0:T(1,128)S(1)}, f32[1,448]{1,0:T(1,...) custom-call(f32[1,448]{1,0:T(1,128)S(1)} %copy-done.2, f32[1,448]{1,0:T(1,128)S(1)} %collective-permute-done.refs_1_, ...), custom_call_target="tpu_custom_call" | custom-call | flops 1600000000 | bytes 2097152 | tf_op jit(solution)/shard_map/pallas_call | solution.py:203
  58.1 5.3 %all-to-all-start = ((bf16[16,32,512]{2,1,0:T(8,128)(2,1)}), bf16[16,32,512]{2,1,0:T(8,128)(2,1)S(1)}, u32[]{:S(2)}, u32[]{:S(2)}) async-start(bf16[16,32,512]{2,1,0:T(8,128)(2,1)} %bitcast), calls=%async_computation | async-start | bytes 1048576 | tf_op jit(solution)/shard_map/all_to_all | solution.py:163
  63.4 2.1 %collective-permute-start.21 = (f32[1,448]{1,0:T(1,128)S(1)}, f32[1,448]{1,0:T(1,128)S(1)}, u32[]{:S(2)}, u32[]{:S(2)}) collective-permute-start(f32[1,448]{1,0:T(1,128)S(1)} %get-tuple-element.49), channel_id=1, source_target_pairs={{0,16},{16,0},{32,48},{48,32},{1,17},{17,1},{33,49},{49,33},{2,18}... | collective-permute-start | bytes 5384 | tf_op jit(solution)/shard_map/ppermute | solution.py:167
  65.5 3.8 %collective-permute-start.22 = (f32[1,448]{1,0:T(1,128)S(1)}, f32[1,448]{1,0:T(1,128)S(1)}, u32[]{:S(2)}, u32[]{:S(2)}) collective-permute-start(f32[1,448]{1,0:T(1,128)S(1)} %get-tuple-element.50), channel_id=1, source_target_pairs={{0,32},{16,48},{32,0},{48,16},{1,33},{17,49},{33,1},{49,17},{2,34}... | collective-permute-start | bytes 5384 | tf_op jit(solution)/shard_map/ppermute | solution.py:167
  69.2 0.5 collective-permute-done.21.sum1
  69.7 5.1 %collective-permute-done.22.sum2 = f32[1,448]{1,0:T(1,128)S(1)} collective-permute-done((f32[1,448]{1,0:T(1,128)S(1)}, f32[1,448]{1,0:T(1,128)S(1)}, u32[]{:S(2)}, u32[]{:S(2)}) %collective-permute-start.22) | collective-permute-done | bytes 1824 | tf_op jit(solution)/shard_map/ppermute | solution.py:167
  74.8 0.0 all-to-all-done.parts
  74.8 0.2 shard_map.60
  75.0 17.1 %all_to_all.10.levels = f32[64,1,128]{2,1,0:T(1,128)S(1)} all-to-all(f32[64,1,128]{2,1,0:T(1,128)S(1)} %get-tuple-element.52), channel_id=1, replica_groups=mesh['expert'=4,'zh'=4,'zl'=2,'x'=4,'c'=2] {'zh','zl','x','c'}, dimensions={0} | all-to-all | bytes 65536 | tf_op jit(solution)/shard_map/all_to_all | solution.py:163
  92.1 0.9 shard_map.61
  (13 shorter events, 0.0 us)
Async XLA Ops:
  0.6 22.8 %collective-permute-start.2 = (f32[1,448]{1,0:T(1,128)}, f32[1,448]{1,0:T(1,128)S(1)}, u32[]{:S(2)}, u32[]{:S(2)}) collective-permute-start(f32[1,448]{1,0:T(1,128)} %right.1), channel_id=1, source_target_pairs={{0,48},{16,32},{32,16},{48,0},{1,49},{17,33},{33,17},{49,1},{2,50}... | collective-permute-start | bytes 5384 | tf_op jit(solution)/shard_map/ppermute | solution.py:167
  7.6 19.7 %collective-permute-start.1 = (f32[1,448]{1,0:T(1,128)}, f32[1,448]{1,0:T(1,128)S(1)}, u32[]{:S(2)}, u32[]{:S(2)}) collective-permute-start(f32[1,448]{1,0:T(1,128)} %right.1), channel_id=1, source_target_pairs={{0,32},{16,48},{32,0},{48,16},{1,33},{17,49},{33,1},{49,17},{2,34}... | collective-permute-start | bytes 5384 | tf_op jit(solution)/shard_map/ppermute | solution.py:167
  8.5 18.7 %collective-permute-start = (f32[1,448]{1,0:T(1,128)}, f32[1,448]{1,0:T(1,128)S(1)}, u32[]{:S(2)}, u32[]{:S(2)}) collective-permute-start(f32[1,448]{1,0:T(1,128)} %right.1), channel_id=1, source_target_pairs={{0,16},{16,0},{32,48},{48,32},{1,17},{17,1},{33,49},{49,33},{2,18}... | collective-permute-start | bytes 5384 | tf_op jit(solution)/shard_map/ppermute | solution.py:167
  10.4 0.8 copy-start
  11.2 44.0 %copy-start.2 = (f32[1,448]{1,0:T(1,128)S(1)}, f32[1,448]{1,0:T(1,128)}, u32[]{:S(2)}) copy-start(f32[1,448]{1,0:T(1,128)} %right.1) | copy-start | bytes 5380
  13.2 3.8 %collective-permute-start.5 = (f32[1,128]{1,0:T(1,128)S(1)}, f32[1,128]{1,0:T(1,128)S(1)}, u32[]{:S(2)}, u32[]{:S(2)}) collective-permute-start(f32[1,128]{1,0:T(1,128)S(1)} %get-tuple-element.29.refs_4_), channel_id=1, source_target_pairs={{0,192},{64,128},{128,64},{192,0},{1,193},{65,129},{129,65},{193,1... | collective-permute-start | bytes 1544 | tf_op jit(solution)/shard_map/ppermute | solution.py:167
  16.0 3.9 %collective-permute-start.4 = (f32[1,128]{1,0:T(1,128)S(1)}, f32[1,128]{1,0:T(1,128)S(1)}, u32[]{:S(2)}, u32[]{:S(2)}) collective-permute-start(f32[1,128]{1,0:T(1,128)S(1)} %get-tuple-element.29.refs_4_), channel_id=1, source_target_pairs={{0,128},{64,192},{128,0},{192,64},{1,129},{65,193},{129,1},{193,65... | collective-permute-start | bytes 1544 | tf_op jit(solution)/shard_map/ppermute | solution.py:167
  16.9 3.7 %collective-permute-start.3 = (f32[1,128]{1,0:T(1,128)S(1)}, f32[1,128]{1,0:T(1,128)S(1)}, u32[]{:S(2)}, u32[]{:S(2)}) collective-permute-start(f32[1,128]{1,0:T(1,128)S(1)} %get-tuple-element.29.refs_4_), channel_id=1, source_target_pairs={{0,64},{64,0},{128,192},{192,128},{1,65},{65,1},{129,193},{193,129... | collective-permute-start | bytes 1544 | tf_op jit(solution)/shard_map/ppermute | solution.py:167
  19.9 8.6 %collective-permute-start.6 = (bf16[32,2304]{1,0:T(8,128)(2,1)S(1)}, bf16[32,2304]{1,0:T(8,128)(2,1)S(1)}, u32[]{:S(2)}, u32[]{:S(2)}) collective-permute-start(bf16[32,2304]{1,0:T(8,128)(2,1)S(1)} %get-tuple-element.31), channel_id=1, source_target_pairs={{0,8},{1,9},{2,10},{3,11},{4,12},{5,13},{6,14},{7,15},{8,0},{9,1},... | collective-permute-start | bytes 442376 | tf_op jit(solution)/shard_map/ppermute | solution.py:175
  20.6 9.8 %collective-permute-start.7 = (bf16[32,2304]{1,0:T(8,128)(2,1)S(1)}, bf16[32,2304]{1,0:T(8,128)(2,1)S(1)}, u32[]{:S(2)}, u32[]{:S(2)}) collective-permute-start(bf16[32,2304]{1,0:T(8,128)(2,1)S(1)} %get-tuple-element.32), channel_id=1, source_target_pairs={{0,4},{1,5},{2,6},{3,7},{4,0},{5,1},{6,2},{7,3},{8,12},{9,13},{10,... | collective-permute-start | bytes 442376 | tf_op jit(solution)/shard_map/ppermute | solution.py:175
  23.4 8.3 %collective-permute-start.8 = (bf16[32,2304]{1,0:T(8,128)(2,1)S(1)}, bf16[32,2304]{1,0:T(8,128)(2,1)S(1)}, u32[]{:S(2)}, u32[]{:S(2)}) collective-permute-start(bf16[32,2304]{1,0:T(8,128)(2,1)S(1)} %get-tuple-element.33), channel_id=1, source_target_pairs={{0,9},{1,8},{2,11},{3,10},{4,13},{5,12},{6,15},{7,14},{8,1},{9,0},... | collective-permute-start | bytes 442376 | tf_op jit(solution)/shard_map/ppermute | solution.py:175
  27.2 10.5 %collective-permute-start.9 = (bf16[32,2304]{1,0:T(8,128)(2,1)S(1)}, bf16[32,2304]{1,0:T(8,128)(2,1)S(1)}, u32[]{:S(2)}, u32[]{:S(2)}) collective-permute-start(bf16[32,2304]{1,0:T(8,128)(2,1)S(1)} %get-tuple-element.34), channel_id=1, source_target_pairs={{0,5},{1,4},{2,7},{3,6},{4,1},{5,0},{6,3},{7,2},{8,13},{9,12},{10,... | collective-permute-start | bytes 442376 | tf_op jit(solution)/shard_map/ppermute | solution.py:175
  27.2 10.5 %collective-permute-start.10 = (bf16[32,2304]{1,0:T(8,128)(2,1)S(1)}, bf16[32,2304]{1,0:T(8,128)(2,1)S(1)}, u32[]{:S(2)}, u32[]{:S(2)}) collective-permute-start(bf16[32,2304]{1,0:T(8,128)(2,1)S(1)} %get-tuple-element.35), channel_id=1, source_target_pairs={{0,10},{1,11},{2,12},{3,13},{4,14},{5,15},{6,8},{7,9},{8,2},{9,3},... | collective-permute-start | bytes 442376 | tf_op jit(solution)/shard_map/ppermute | solution.py:175
  28.5 12.7 %collective-permute-start.11 = (bf16[32,2304]{1,0:T(8,128)(2,1)S(1)}, bf16[32,2304]{1,0:T(8,128)(2,1)S(1)}, u32[]{:S(2)}, u32[]{:S(2)}) collective-permute-start(bf16[32,2304]{1,0:T(8,128)(2,1)S(1)} %get-tuple-element.36), channel_id=1, source_target_pairs={{0,6},{1,7},{2,0},{3,1},{4,2},{5,3},{6,4},{7,5},{8,14},{9,15},{10,... | collective-permute-start | bytes 442376 | tf_op jit(solution)/shard_map/ppermute | solution.py:175
  30.5 12.1 %collective-permute-start.12 = (bf16[32,2304]{1,0:T(8,128)(2,1)S(1)}, bf16[32,2304]{1,0:T(8,128)(2,1)S(1)}, u32[]{:S(2)}, u32[]{:S(2)}) collective-permute-start(bf16[32,2304]{1,0:T(8,128)(2,1)S(1)} %get-tuple-element.37), channel_id=1, source_target_pairs={{0,14},{1,15},{2,8},{3,9},{4,10},{5,11},{6,12},{7,13},{8,6},{9,7},... | collective-permute-start | bytes 442376 | tf_op jit(solution)/shard_map/ppermute | solution.py:175
  31.7 11.7 %collective-permute-start.13 = (bf16[32,2304]{1,0:T(8,128)(2,1)S(1)}, bf16[32,2304]{1,0:T(8,128)(2,1)S(1)}, u32[]{:S(2)}, u32[]{:S(2)}) collective-permute-start(bf16[32,2304]{1,0:T(8,128)(2,1)S(1)} %get-tuple-element.38), channel_id=1, source_target_pairs={{0,2},{1,3},{2,4},{3,5},{4,6},{5,7},{6,0},{7,1},{8,10},{9,11},{10,... | collective-permute-start | bytes 442376 | tf_op jit(solution)/shard_map/ppermute | solution.py:175
  37.8 7.5 %collective-permute-start.14 = (bf16[32,2304]{1,0:T(8,128)(2,1)S(1)}, bf16[32,2304]{1,0:T(8,128)(2,1)S(1)}, u32[]{:S(2)}, u32[]{:S(2)}) collective-permute-start(bf16[32,2304]{1,0:T(8,128)(2,1)S(1)} %get-tuple-element.39), channel_id=1, source_target_pairs={{0,11},{1,10},{2,13},{3,12},{4,15},{5,14},{6,9},{7,8},{8,3},{9,2},... | collective-permute-start | bytes 442376 | tf_op jit(solution)/shard_map/ppermute | solution.py:175
  37.8 15.6 %collective-permute-start.15 = (bf16[32,2304]{1,0:T(8,128)(2,1)S(1)}, bf16[32,2304]{1,0:T(8,128)(2,1)S(1)}, u32[]{:S(2)}, u32[]{:S(2)}) collective-permute-start(bf16[32,2304]{1,0:T(8,128)(2,1)S(1)} %get-tuple-element.40), channel_id=1, source_target_pairs={{0,7},{1,6},{2,1},{3,0},{4,3},{5,2},{6,5},{7,4},{8,15},{9,14},{10,... | collective-permute-start | bytes 442376 | tf_op jit(solution)/shard_map/ppermute | solution.py:175
  41.1 12.2 %collective-permute-start.16 = (bf16[32,2304]{1,0:T(8,128)(2,1)S(1)}, bf16[32,2304]{1,0:T(8,128)(2,1)S(1)}, u32[]{:S(2)}, u32[]{:S(2)}) collective-permute-start(bf16[32,2304]{1,0:T(8,128)(2,1)S(1)} %get-tuple-element.41), channel_id=1, source_target_pairs={{0,15},{1,14},{2,9},{3,8},{4,11},{5,10},{6,13},{7,12},{8,7},{9,6},... | collective-permute-start | bytes 442376 | tf_op jit(solution)/shard_map/ppermute | solution.py:175
  42.5 12.7 %collective-permute-start.17 = (bf16[32,2304]{1,0:T(8,128)(2,1)S(1)}, bf16[32,2304]{1,0:T(8,128)(2,1)S(1)}, u32[]{:S(2)}, u32[]{:S(2)}) collective-permute-start(bf16[32,2304]{1,0:T(8,128)(2,1)S(1)} %get-tuple-element.42), channel_id=1, source_target_pairs={{0,3},{1,2},{2,5},{3,4},{4,7},{5,6},{6,1},{7,0},{8,11},{9,10},{10,... | collective-permute-start | bytes 442376 | tf_op jit(solution)/shard_map/ppermute | solution.py:175
  43.4 11.9 %collective-permute-start.18 = (bf16[32,2304]{1,0:T(8,128)(2,1)S(1)}, bf16[32,2304]{1,0:T(8,128)(2,1)S(1)}, u32[]{:S(2)}, u32[]{:S(2)}) collective-permute-start(bf16[32,2304]{1,0:T(8,128)(2,1)S(1)} %get-tuple-element.43), channel_id=1, source_target_pairs={{0,12},{1,13},{2,14},{3,15},{4,8},{5,9},{6,10},{7,11},{8,4},{9,5},... | collective-permute-start | bytes 442376 | tf_op jit(solution)/shard_map/ppermute | solution.py:175
  45.2 10.0 %collective-permute-start.19 = (bf16[32,2304]{1,0:T(8,128)(2,1)S(1)}, bf16[32,2304]{1,0:T(8,128)(2,1)S(1)}, u32[]{:S(2)}, u32[]{:S(2)}) collective-permute-start(bf16[32,2304]{1,0:T(8,128)(2,1)S(1)} %get-tuple-element.44), channel_id=1, source_target_pairs={{0,13},{1,12},{2,15},{3,14},{4,9},{5,8},{6,11},{7,10},{8,5},{9,4},... | collective-permute-start | bytes 442376 | tf_op jit(solution)/shard_map/ppermute | solution.py:175
  53.3 1.9 %collective-permute-start.20 = (bf16[32,2304]{1,0:T(8,128)(2,1)S(1)}, bf16[32,2304]{1,0:T(8,128)(2,1)S(1)}, u32[]{:S(2)}, u32[]{:S(2)}) collective-permute-start(bf16[32,2304]{1,0:T(8,128)(2,1)S(1)} %get-tuple-element.45), channel_id=1, source_target_pairs={{0,1},{1,0},{2,3},{3,2},{4,5},{5,4},{6,7},{7,6},{8,9},{9,8},{10,11... | collective-permute-start | bytes 442376 | tf_op jit(solution)/shard_map/ppermute | solution.py:175
  55.2 36.8 %copy-start.1 = (f32[1,32,512]{2,1,0:T(8,128)S(1)}, f32[1,32,512]{2,1,0:T(8,128)}, u32[]{:S(2)}) copy-start(f32[1,32,512]{2,1,0:T(8,128)} %factor.3) | copy-start | bytes 196612
  58.1 16.7 %all-to-all-start = ((bf16[16,32,512]{2,1,0:T(8,128)(2,1)}), bf16[16,32,512]{2,1,0:T(8,128)(2,1)S(1)}, u32[]{:S(2)}, u32[]{:S(2)}) async-start(bf16[16,32,512]{2,1,0:T(8,128)(2,1)} %bitcast), calls=%async_computation | async-start | bytes 1048576 | tf_op jit(solution)/shard_map/all_to_all | solution.py:163
  63.4 6.3 %collective-permute-start.21 = (f32[1,448]{1,0:T(1,128)S(1)}, f32[1,448]{1,0:T(1,128)S(1)}, u32[]{:S(2)}, u32[]{:S(2)}) collective-permute-start(f32[1,448]{1,0:T(1,128)S(1)} %get-tuple-element.49), channel_id=1, source_target_pairs={{0,16},{16,0},{32,48},{48,32},{1,17},{17,1},{33,49},{49,33},{2,18}... | collective-permute-start | bytes 5384 | tf_op jit(solution)/shard_map/ppermute | solution.py:167
  65.5 9.3 %collective-permute-start.22 = (f32[1,448]{1,0:T(1,128)S(1)}, f32[1,448]{1,0:T(1,128)S(1)}, u32[]{:S(2)}, u32[]{:S(2)}) collective-permute-start(f32[1,448]{1,0:T(1,128)S(1)} %get-tuple-element.50), channel_id=1, source_target_pairs={{0,32},{16,48},{32,0},{48,16},{1,33},{17,49},{33,1},{49,17},{2,34}... | collective-permute-start | bytes 5384 | tf_op jit(solution)/shard_map/ppermute | solution.py:167
  69.2 5.6 %collective-permute-start.23 = (f32[1,448]{1,0:T(1,128)S(1)}, f32[1,448]{1,0:T(1,128)S(1)}, u32[]{:S(2)}, u32[]{:S(2)}) collective-permute-start(f32[1,448]{1,0:T(1,128)S(1)} %get-tuple-element.51), channel_id=1, source_target_pairs={{0,48},{16,32},{32,16},{48,0},{1,49},{17,33},{33,17},{49,1},{2,50}... | collective-permute-start | bytes 5384 | tf_op jit(solution)/shard_map/ppermute | solution.py:167

commit v4 on v3

--- a/solution.py
+++ b/solution.py
@@ -67,16 +67,12 @@
 
 
 def gram_kernel(*refs):
-    rights, tokens, staying = refs[0:4], refs[4:8], refs[8]
-    crosses, refs = refs[9 : PEERS + 8], refs[9:]
-    part, sum0, sum1, sum2, sum3, narrow, level, got, image = refs[PEERS - 1 :]
+    rights, staying = refs[0:4], refs[4]
+    crosses, refs = refs[5 : PEERS + 4], refs[5:]
+    part, sum0, sum1, sum2, sum3, narrow, got, image = refs[PEERS - 1 :]
     plane, x, c = lax.axis_index("zl"), lax.axis_index("x"), lax.axis_index("c")
     own = pl.multiple_of((plane * 8 + x * 2 + c) * ROWS, ROWS)
     got[pl.ds(own, ROWS), :] = staying[...]
-    total = (tokens[0][...] + tokens[1][...]) + (tokens[2][...] + tokens[3][...])
-    weight = (4 * tokens[0][...] / total)[:, 0:1]
-    squared = weight * weight
-    level[...] = jnp.broadcast_to(squared, level.shape)
     for k, (dz, dx, dc) in enumerate(OFFSETS[:-1]):
         source = lax.rem(plane + dz, 2) * 8 + lax.rem(x + (4 - dx), 4) * 2 + lax.rem(c + dc, 2)
         got[pl.ds(pl.multiple_of(source * ROWS, ROWS), ROWS), :] = crosses[k][...]
@@ -101,45 +97,67 @@
     for d, out in enumerate((sum0, sum1, sum2, sum3)):
         out[...] = total[:, d * OWN : (d + 1) * OWN]
     last = (((1,), (1,)), ((), ()))
-    scale = squared / FF2
     high = lax.dot_general(image[0:256, :], image[...], last, preferred_element_type=jnp.float32)
     low = lax.dot_general(image[256:512, :], image[256:512, :], last, preferred_element_type=jnp.float32)
-    share = jnp.float32(1.0 / 16.0)
-    row_high = lax.broadcasted_iota(jnp.int32, (256, 512), 0)
-    col_high = lax.broadcasted_iota(jnp.int32, (256, 512), 1)
-    row_low = lax.broadcasted_iota(jnp.int32, (256, 256), 0)
-    col_low = lax.broadcasted_iota(jnp.int32, (256, 256), 1)
-    part[0:256, :] = (high * scale - jnp.where(row_high == col_high, share, 0.0)).astype(part.dtype)
-    part[256:512, 256:512] = (low * scale - jnp.where(row_low == col_low, share, 0.0)).astype(part.dtype)
+    places = [[lax.broadcasted_iota(jnp.int32, half.shape, k) for k in range(2)] for half in (high, low)]
+    least = [jnp.min(jnp.where(row == col, half, jnp.inf)) for half, (row, col) in zip((high, low), places)]
+    share = jnp.full((8, 128), jnp.minimum(*least), jnp.float32).astype(part.dtype).astype(jnp.float32)[0:1, 0:1]
+    shared = []
+    for half, (row, col) in zip((high, low), places):
+        half = jnp.where(row == col, half - share, half)
+        slot = jnp.logical_and(row % ROWS == ROWS - 1, col == row - (ROWS - 1))
+        shared.append(jnp.where(slot, share, half).astype(part.dtype))
+    part[0:256, :], part[256:512, 256:512] = shared
     part[256:512, 0:256] = jnp.zeros((256, 256), part.dtype)
 
 
-def peaks_kernel(squared, parts, sum0, sum1, sum2, sum3, upper, term, levels):
+def peaks_kernel(parts, sum0, sum1, sum2, sum3, upper, sums, levels):
     first = lax.axis_index(GROUP) * ROWS
     total = parts[0].astype(jnp.float32)
     for k in range(1, 16):
         total = total + parts[k].astype(jnp.float32)
+    place = lax.broadcasted_iota(jnp.int32, (ROWS, BLOCK), 0)
+    row = place + first
+    col = lax.broadcasted_iota(jnp.int32, (ROWS, BLOCK), 1)
+    share = jnp.sum(jnp.where(jnp.logical_and(place == ROWS - 1, col == first), total, 0.0))
+    diagonal = total + share
+    above, on = col > row, col == row
+    upper[...] = jnp.where(above, total, jnp.where(on, diagonal, 0.0))
+    added = (sum0[...] + sum1[...]) + (sum2[...] + sum3[...])
+    sums[...] = added
+    ends = (
+        jnp.max(jnp.where(above, jnp.abs(total), 0.0)),
+        jnp.max(jnp.where(on, diagonal, -jnp.inf)),
+        -jnp.min(jnp.where(on, diagonal, jnp.inf)),
+        jnp.max(added),
+        -jnp.min(added),
+    )
+    lane = lax.broadcasted_iota(jnp.int32, levels.shape, 2)
+    value = jnp.full(levels.shape, ends[0], jnp.float32)
+    for k in range(1, 5):
+        value = jnp.where(lane == k, ends[k], value)
+    levels[...] = value
+
+
+def final_kernel(levels, upper, narrow, factor, sums, right, token0, token1, token2, token3, new_factor, new_right):
+    first = lax.axis_index(GROUP) * ROWS
+    tokens = (token0[...] + token1[...]) + (token2[...] + token3[...])
+    weight = (4 * token0[...] / tokens)[:, 0:1]
+    squared = weight * weight
+    scale = squared / FF2
+    peak = jnp.max(levels[...], axis=0)
+    off, most, least, sum_most, sum_least = (peak[0:1, k : k + 1] for k in range(5))
+    row_peak = jnp.maximum(scale * off, jnp.maximum(jnp.abs(scale * most - 1.0), jnp.abs(-scale * least - 1.0)))
+    column_most = jnp.abs(squared * sum_most / DIM - 1.0)
+    column_peak = jnp.maximum(column_most, jnp.abs(-squared * sum_least / DIM - 1.0))
     row = lax.broadcasted_iota(jnp.int32, (ROWS, BLOCK), 0) + first
     col = lax.broadcasted_iota(jnp.int32, (ROWS, BLOCK), 1)
-    total = jnp.where(col >= row, total, 0.0)
-    upper[...] = total
-    row_level = jnp.max(jnp.abs(total))
-    added = (sum0[...] + sum1[...]) + (sum2[...] + sum3[...])
-    column_term = squared[0:1, 0:1] * added / DIM - 1.0
-    term[...] = column_term
-    column_level = jnp.max(jnp.abs(column_term))
-    lane = lax.broadcasted_iota(jnp.int32, levels.shape, 2)
-    levels[...] = jnp.where(lane == 0, row_level, column_level)
-
-
-def final_kernel(levels, upper, narrow, factor, term, right, new_factor, new_right):
-    peak = jnp.max(levels[...], axis=0)
-    row_peak = jnp.max(peak[0:1, 0:1])
-    column_peak = jnp.max(peak[0:1, 1:2])
-    steps = (upper[...] / (row_peak + epsilon)).astype(jnp.bfloat16)
+    upper_part = upper[...] * scale - jnp.where(row == col, 1.0, 0.0)
+    steps = (upper_part / (row_peak + epsilon)).astype(jnp.bfloat16)
     moved = jnp.dot(steps, narrow[...], preferred_element_type=jnp.float32)
     new_factor[0] = factor[0] - step_rate * moved
-    new_right[...] = right[...] - step_rate * term[...] / (column_peak + epsilon) * right[...]
+    term = squared * sums[...] / DIM - 1.0
+    new_right[...] = right[...] - step_rate * term / (column_peak + epsilon) * right[...]
 
 
 def shape(dims, dtype=jnp.float32):
@@ -200,25 +218,22 @@
     crosses = [to_peer(value, *OFFSETS[k]) for k, value in enumerate(leaving)]
     rights = [right_diag] + [across(right_diag, d) for d in (1, 2, 3)]
     tokens = [token] + [across(token, d, "expert") for d in (1, 2, 3)]
-    part, *sums, narrow, squared = call(
+    part, *sums, narrow = call(
         gram_kernel,
-        [VMEM] * (PEERS + 8),
-        [shape((BLOCK, BLOCK), half)] + [shape((1, OWN))] * 4 + [shape((BLOCK, BLOCK), half), shape((1, 128))],
+        [VMEM] * (PEERS + 4),
+        [shape((BLOCK, BLOCK), half)] + [shape((1, OWN))] * 4 + [shape((BLOCK, BLOCK), half)],
         1600000000,
         [pltpu.VMEM((BLOCK, MESSAGE), half), pltpu.VMEM((BLOCK, WIDE), half)],
-    )(*rights, *tokens, staying, *crosses)
+    )(*rights, staying, *crosses)
     parts = exchange(part.reshape(16, ROWS, BLOCK), GROUP)
     sums = [sums[0]] + [across(sums[d], d) for d in (1, 2, 3)]
     upper, term, levels = call(
-        peaks_kernel,
-        [VMEM] * 6,
-        [shape((ROWS, BLOCK)), shape((1, OWN)), shape((64, 1, 128))],
-        2000000,
-    )(squared, parts, *sums)
+        peaks_kernel, [VMEM] * 5, [shape((ROWS, BLOCK)), shape((1, OWN)), shape((64, 1, 128))], 2000000
+    )(parts, *sums)
     levels = exchange(levels, SHARD)
     new_factor, new_right = call(
-        final_kernel, [VMEM] * 6, [shape((1, ROWS, BLOCK)), shape((1, OWN))], 17000000
-    )(levels, upper, narrow, factor, term, right_diag)
+        final_kernel, [VMEM] * 10, [shape((1, ROWS, BLOCK)), shape((1, OWN))], 17000000
+    )(levels, upper, narrow, factor, term, right_diag, *tokens)
     return new_factor, new_right
 
 

time: 93.2 us -> 86.6 us (0.929)
  blocking collectives: 17.1 us -> 0 us
  starting transfers between devices: 44.3 us -> 60.5 us
  waiting for transfers between devices: 23.5 us -> 16.8 us
    all_to_all x1 -> x0, blocking collectives: 17.1 us -> none  [exchange(): return lax.all_to_all(value, axes, 0, 0, tiled=True)]
    all_to_all x1 -> x2, starting transfers between devices: 5.25 us -> 14.7 us  [exchange(): return lax.all_to_all(value, axes, 0, 0, tiled=True)]
    ppermute x15, waiting for transfers between devices: 14.5 us -> 5.92 us  [to_peer(): return lax.ppermute(value, GROUP, pairs)]
    ppermute x15, starting transfers between devices: 20.8 us -> 26.6 us  [to_peer(): return lax.ppermute(value, GROUP, pairs)]
    all_to_all x1 -> x2, waiting for transfers between devices: 0.01 us -> 1.7 us  [exchange(): return lax.all_to_all(value, axes, 0, 0, tiled=True)]
  transfers between devices with their start and end apart: 25 -> 26, of which waited for: 8 -> 11; matrix products, arithmetic and copies ran while one was open for 0% -> 0% of each run, Pallas kernels for 2% -> 2%
where the time goes in v4:
time: 86.6 us; the launch traced here: 86.2 us
  starting transfers between devices  60.5 us (70%)
  waiting for transfers between devices  16.8 us (19%)
  Pallas kernels  6.76 us (8%)
  between operations  1.34 us (2%)
    ppermute x15, starting transfers between devices, to_peer(): return lax.ppermute(value, GROUP, pairs)  26.6 us
    ppermute x9, starting transfers between devices, across(): return lax.ppermute(value, axis, [(k, k ^ turn) for k in range(4)])  19.1 us
    all_to_all x2, starting transfers between devices, exchange(): return lax.all_to_all(value, axes, 0, 0, tiled=True)  14.7 us
    ppermute x9, waiting for transfers between devices, across(): return lax.ppermute(value, axis, [(k, k ^ turn) for k in range(4)])  9.19 us
    ppermute x15, waiting for transfers between devices, to_peer(): return lax.ppermute(value, GROUP, pairs)  5.92 us
    pallas_call x1, Pallas kernels, inner(): call(gram_kernel, [VMEM] * (PEERS + 4), [shape((BLOCK, BLOCK), half)] + [...  2.96 us
    pallas_call x1, Pallas kernels, pack(): pl.pallas_call(pack_kernel, out_shape=outs + [shape((1, 128))], in_specs=...  1.92 us
  transfers between devices with their start and end apart: 26, of which 11 were waited for; matrix products, arithmetic and copies ran while one was open for 0% of the time, Pallas kernels for 2%

profile of v4, /device:TPU:1, one launch (start us, length us, event | category | flops | bytes accessed | tf_op | source)
XLA Modules:
  0.0 86.2 jit_solution(3887238837524635680)
XLA Ops:
  0.6 3.9 %collective-permute-start = (f32[1,448]{1,0:T(1,128)}, f32[1,448]{1,0:T(1,128)S(1)}, u32[]{:S(2)}, u32[]{:S(2)}) collective-permute-start(f32[1,448]{1,0:T(1,128)} %right.1), channel_id=1, source_target_pairs={{0,16},{16,0},{32,48},{48,32},{1,17},{17,1},{33,49},{49,33},{2,18}... | collective-permute-start | bytes 5384 | tf_op jit(solution)/shard_map/ppermute | solution.py:185
  4.5 5.1 %collective-permute-start.1 = (f32[1,448]{1,0:T(1,128)}, f32[1,448]{1,0:T(1,128)S(1)}, u32[]{:S(2)}, u32[]{:S(2)}) collective-permute-start(f32[1,448]{1,0:T(1,128)} %right.1), channel_id=1, source_target_pairs={{0,32},{16,48},{32,0},{48,16},{1,33},{17,49},{33,1},{49,17},{2,34}... | collective-permute-start | bytes 5384 | tf_op jit(solution)/shard_map/ppermute | solution.py:185
  10.3 0.0 copy-start
  10.3 0.8 copy-done
  11.1 1.9 %pack.1 = (bf16[32,2304]{1,0:T(8,128)(2,1)S(1)}, bf16[32,2304]{1,0:T(8,128)(2,1)S(1)}, bf16[32,2304]{1,0:T(8,128)(2,1)S(1)}, bf16[32,2304]{1,0:T(8,128)(2,1)S(1)...) custom-call(bf16[1,32,28672]{2,1,0:T(8,128)(2,1)} %gradient.1, ...), custom_call_target="tpu_custom_call" | custom-call | flops 2000000 | bytes 4194304 | tf_op jit(solution)/shard_map/pack/pallas_call | solution.py:199
  13.1 1.3 %collective-permute-start.10 = (bf16[32,2304]{1,0:T(8,128)(2,1)S(1)}, bf16[32,2304]{1,0:T(8,128)(2,1)S(1)}, u32[]{:S(2)}, u32[]{:S(2)}) collective-permute-start(bf16[32,2304]{1,0:T(8,128)(2,1)S(1)} %get-tuple-element.36), channel_id=1, source_target_pairs={{0,2},{1,3},{2,4},{3,5},{4,6},{5,7},{6,0},{7,1},{8,10},{9,11},{10,... | collective-permute-start | bytes 442376 | tf_op jit(solution)/shard_map/ppermute | solution.py:193
  14.4 3.1 %collective-permute-start.11 = (bf16[32,2304]{1,0:T(8,128)(2,1)S(1)}, bf16[32,2304]{1,0:T(8,128)(2,1)S(1)}, u32[]{:S(2)}, u32[]{:S(2)}) collective-permute-start(bf16[32,2304]{1,0:T(8,128)(2,1)S(1)} %get-tuple-element.37), channel_id=1, source_target_pairs={{0,11},{1,10},{2,13},{3,12},{4,15},{5,14},{6,9},{7,8},{8,3},{9,2},... | collective-permute-start | bytes 442376 | tf_op jit(solution)/shard_map/ppermute | solution.py:193
  17.4 0.0 collective-permute-done.refs_1_
  17.4 0.3 collective-permute-start.12
  17.8 2.1 %collective-permute-start.13 = (bf16[32,2304]{1,0:T(8,128)(2,1)S(1)}, bf16[32,2304]{1,0:T(8,128)(2,1)S(1)}, u32[]{:S(2)}, u32[]{:S(2)}) collective-permute-start(bf16[32,2304]{1,0:T(8,128)(2,1)S(1)} %get-tuple-element.39), channel_id=1, source_target_pairs={{0,15},{1,14},{2,9},{3,8},{4,11},{5,10},{6,13},{7,12},{8,7},{9,6},... | collective-permute-start | bytes 442376 | tf_op jit(solution)/shard_map/ppermute | solution.py:193
  19.9 0.1 collective-permute-start.14
  20.0 0.0 collective-permute-done.10.refs_12_
  20.0 2.0 %collective-permute-start.15 = (bf16[32,2304]{1,0:T(8,128)(2,1)S(1)}, bf16[32,2304]{1,0:T(8,128)(2,1)S(1)}, u32[]{:S(2)}, u32[]{:S(2)}) collective-permute-start(bf16[32,2304]{1,0:T(8,128)(2,1)S(1)} %get-tuple-element.41), channel_id=1, source_target_pairs={{0,12},{1,13},{2,14},{3,15},{4,8},{5,9},{6,10},{7,11},{8,4},{9,5},... | collective-permute-start | bytes 442376 | tf_op jit(solution)/shard_map/ppermute | solution.py:193
  22.0 0.2 collective-permute-done.11.refs_13_
  22.1 5.5 %collective-permute-start.16 = (bf16[32,2304]{1,0:T(8,128)(2,1)S(1)}, bf16[32,2304]{1,0:T(8,128)(2,1)S(1)}, u32[]{:S(2)}, u32[]{:S(2)}) collective-permute-start(bf16[32,2304]{1,0:T(8,128)(2,1)S(1)} %get-tuple-element.42), channel_id=1, source_target_pairs={{0,13},{1,12},{2,15},{3,14},{4,9},{5,8},{6,11},{7,10},{8,5},{9,4},... | collective-permute-start | bytes 442376 | tf_op jit(solution)/shard_map/ppermute | solution.py:193
  27.6 0.0 collective-permute-done.12.refs_14_
  27.6 0.0 collective-permute-start.17
  27.6 0.0 collective-permute-done.13.refs_15_
  27.7 0.8 collective-permute-start.3
  28.5 2.5 %collective-permute-start.4 = (bf16[32,2304]{1,0:T(8,128)(2,1)S(1)}, bf16[32,2304]{1,0:T(8,128)(2,1)S(1)}, u32[]{:S(2)}, u32[]{:S(2)}) collective-permute-start(bf16[32,2304]{1,0:T(8,128)(2,1)S(1)} %get-tuple-element.30), channel_id=1, source_target_pairs={{0,4},{1,5},{2,6},{3,7},{4,0},{5,1},{6,2},{7,3},{8,12},{9,13},{10,... | collective-permute-start | bytes 442376 | tf_op jit(solution)/shard_map/ppermute | solution.py:193
  30.9 0.0 collective-permute-done.15.refs_17_
  30.9 1.6 %collective-permute-start.5 = (bf16[32,2304]{1,0:T(8,128)(2,1)S(1)}, bf16[32,2304]{1,0:T(8,128)(2,1)S(1)}, u32[]{:S(2)}, u32[]{:S(2)}) collective-permute-start(bf16[32,2304]{1,0:T(8,128)(2,1)S(1)} %get-tuple-element.31), channel_id=1, source_target_pairs={{0,9},{1,8},{2,11},{3,10},{4,13},{5,12},{6,15},{7,14},{8,1},{9,0},... | collective-permute-start | bytes 442376 | tf_op jit(solution)/shard_map/ppermute | solution.py:193
  32.5 0.3 collective-permute-done.16.refs_18_
  32.9 2.9 %collective-permute-start.6 = (bf16[32,2304]{1,0:T(8,128)(2,1)S(1)}, bf16[32,2304]{1,0:T(8,128)(2,1)S(1)}, u32[]{:S(2)}, u32[]{:S(2)}) collective-permute-start(bf16[32,2304]{1,0:T(8,128)(2,1)S(1)} %get-tuple-element.32), channel_id=1, source_target_pairs={{0,5},{1,4},{2,7},{3,6},{4,1},{5,0},{6,3},{7,2},{8,13},{9,12},{10,... | collective-permute-start | bytes 442376 | tf_op jit(solution)/shard_map/ppermute | solution.py:193
  35.8 0.0 collective-permute-done.17.refs_19_
  35.8 1.2 %collective-permute-start.7 = (bf16[32,2304]{1,0:T(8,128)(2,1)S(1)}, bf16[32,2304]{1,0:T(8,128)(2,1)S(1)}, u32[]{:S(2)}, u32[]{:S(2)}) collective-permute-start(bf16[32,2304]{1,0:T(8,128)(2,1)S(1)} %get-tuple-element.33), channel_id=1, source_target_pairs={{0,10},{1,11},{2,12},{3,13},{4,14},{5,15},{6,8},{7,9},{8,2},{9,3},... | collective-permute-start | bytes 442376 | tf_op jit(solution)/shard_map/ppermute | solution.py:193
  37.0 0.0 collective-permute-done.3.refs_5_
  37.0 1.9 %collective-permute-start.8 = (bf16[32,2304]{1,0:T(8,128)(2,1)S(1)}, bf16[32,2304]{1,0:T(8,128)(2,1)S(1)}, u32[]{:S(2)}, u32[]{:S(2)}) collective-permute-start(bf16[32,2304]{1,0:T(8,128)(2,1)S(1)} %get-tuple-element.34), channel_id=1, source_target_pairs={{0,6},{1,7},{2,0},{3,1},{4,2},{5,3},{6,4},{7,5},{8,14},{9,15},{10,... | collective-permute-start | bytes 442376 | tf_op jit(solution)/shard_map/ppermute | solution.py:193
  38.9 1.3 %collective-permute-start.9 = (bf16[32,2304]{1,0:T(8,128)(2,1)S(1)}, bf16[32,2304]{1,0:T(8,128)(2,1)S(1)}, u32[]{:S(2)}, u32[]{:S(2)}) collective-permute-start(bf16[32,2304]{1,0:T(8,128)(2,1)S(1)} %get-tuple-element.35), channel_id=1, source_target_pairs={{0,14},{1,15},{2,8},{3,9},{4,10},{5,11},{6,12},{7,13},{8,6},{9,7},... | collective-permute-start | bytes 442376 | tf_op jit(solution)/shard_map/ppermute | solution.py:193
  40.2 0.7 collective-permute-done.5.refs_7_
  40.9 1.3 %collective-permute-done.7.refs_9_ = bf16[32,2304]{1,0:T(8,128)(2,1)S(1)} collective-permute-done((bf16[32,2304]{1,0:T(8,128)(2,1)S(1)}, bf16[32,2304]{1,0:T(8,128)(2,1)S(1)}, u32[]{:S(2)}, u32[]{:S(2)}) %collective-permute-start.7) | collective-permute-done | bytes 147488 | tf_op jit(solution)/shard_map/ppermute | solution.py:193
  42.2 0.7 collective-permute-done.8.refs_10_
  42.9 2.8 %collective-permute-done.9.refs_11_ = bf16[32,2304]{1,0:T(8,128)(2,1)S(1)} collective-permute-done((bf16[32,2304]{1,0:T(8,128)(2,1)S(1)}, bf16[32,2304]{1,0:T(8,128)(2,1)S(1)}, u32[]{:S(2)}, u32[]{:S(2)}) %collective-permute-start.9) | collective-permute-done | bytes 147488 | tf_op jit(solution)/shard_map/ppermute | solution.py:193
  45.7 3.0 %shard_map.59 = (bf16[512,512]{1,0:T(8,128)(2,1)}, f32[1,448]{1,0:T(1,128)S(1)}, f32[1,448]{1,0:T(1,128)S(1)}, f32[1,448]{1,0:T(1,128)S(1)}, f32[1,448]{1,0:T(1,128)S(1)}, /*index=5*/bf16[512,512]{1,0:T(8,128)(2,1)S(1)}) custom-call(f32[1,448]{1,0:T(1,128)S(1)} %copy-done.2, f32[1,448]{1,0:T(1,128)S(1)} %collective-permute-done.refs_1_, ...), custom_call_target="tpu_custom_call" | custom-call | flops 1600000000 | bytes 2097152 | tf_op jit(solution)/shard_map/pallas_call | solution.py:221
  48.6 6.9 %all-to-all-start = ((bf16[16,32,512]{2,1,0:T(8,128)(2,1)}), bf16[16,32,512]{2,1,0:T(8,128)(2,1)S(1)}, u32[]{:S(2)}, u32[]{:S(2)}) async-start(bf16[16,32,512]{2,1,0:T(8,128)(2,1)} %bitcast), calls=%async_computation | async-start | bytes 1048576 | tf_op jit(solution)/shard_map/all_to_all | solution.py:181
  55.5 2.5 %collective-permute-start.18 = (f32[1,448]{1,0:T(1,128)S(1)}, f32[1,448]{1,0:T(1,128)S(1)}, u32[]{:S(2)}, u32[]{:S(2)}) collective-permute-start(f32[1,448]{1,0:T(1,128)S(1)} %get-tuple-element.46), channel_id=1, source_target_pairs={{0,16},{16,0},{32,48},{48,32},{1,17},{17,1},{33,49},{49,33},{2,18}... | collective-permute-start | bytes 5384 | tf_op jit(solution)/shard_map/ppermute | solution.py:185
  58.0 3.6 %collective-permute-start.19 = (f32[1,448]{1,0:T(1,128)S(1)}, f32[1,448]{1,0:T(1,128)S(1)}, u32[]{:S(2)}, u32[]{:S(2)}) collective-permute-start(f32[1,448]{1,0:T(1,128)S(1)} %get-tuple-element.47), channel_id=1, source_target_pairs={{0,32},{16,48},{32,0},{48,16},{1,33},{17,49},{33,1},{49,17},{2,34}... | collective-permute-start | bytes 5384 | tf_op jit(solution)/shard_map/ppermute | solution.py:185
  61.6 0.0 collective-permute-start.20
  61.6 0.2 collective-permute-done.18.sum1
  61.8 5.3 %collective-permute-done.19.sum2 = f32[1,448]{1,0:T(1,128)S(1)} collective-permute-done((f32[1,448]{1,0:T(1,128)S(1)}, f32[1,448]{1,0:T(1,128)S(1)}, u32[]{:S(2)}, u32[]{:S(2)}) %collective-permute-start.19) | collective-permute-done | bytes 1824 | tf_op jit(solution)/shard_map/ppermute | solution.py:185
  67.2 0.9 %shard_map.60 = (f32[32,512]{1,0:T(8,128)S(1)}, f32[1,448]{1,0:T(1,128)S(1)}, f32[64,1,128]{2,1,0:T(1,128)}) custom-call(bf16[16,32,512]{2,1,0:T(8,128)(2,1)S(1)} %all-to-all-done.parts, f32[1,448]{1,0:T(1,128)S(1)} %get-tuple-element.45.sum0, f32[1,448]{1,0:T(1,128)S(1)} %collective-permute-done.18.sum1, f32[1,448]{1,0:T(1,128)S(1)} %collective-permute-done.19.sum2, ...), custom_call_target="tpu_custom_call" | custom-call | flops 2000000 | bytes 2097152 | tf_op jit(solution)/shard_map/pallas_call | solution.py:230
  68.1 7.8 %all-to-all-start.1 = ((f32[64,1,128]{2,1,0:T(1,128)}), f32[64,1,128]{2,1,0:T(1,128)S(1)}, u32[]{:S(2)}, u32[]{:S(2)}) async-start(f32[64,1,128]{2,1,0:T(1,128)} %get-tuple-element.49), calls=%async_computation.1 | async-start | bytes 65536 | tf_op jit(solution)/shard_map/all_to_all | solution.py:181
  75.9 1.4 %collective-permute-start.21 = (f32[1,128]{1,0:T(1,128)S(1)}, f32[1,128]{1,0:T(1,128)S(1)}, u32[]{:S(2)}, u32[]{:S(2)}) collective-permute-start(f32[1,128]{1,0:T(1,128)S(1)} %get-tuple-element.53.token0), channel_id=1, source_target_pairs={{0,64},{64,0},{128,192},{192,128},{1,65},{65,1},{129,193},{193,129... | collective-permute-start | bytes 1544 | tf_op jit(solution)/shard_map/ppermute | solution.py:185
  77.3 2.6 %collective-permute-start.22 = (f32[1,128]{1,0:T(1,128)S(1)}, f32[1,128]{1,0:T(1,128)S(1)}, u32[]{:S(2)}, u32[]{:S(2)}) collective-permute-start(f32[1,128]{1,0:T(1,128)S(1)} %get-tuple-element.53.token0), channel_id=1, source_target_pairs={{0,128},{64,192},{128,0},{192,64},{1,129},{65,193},{129,1},{193,65... | collective-permute-start | bytes 1544 | tf_op jit(solution)/shard_map/ppermute | solution.py:185
  79.9 1.3 %collective-permute-done.22.token2 = f32[1,128]{1,0:T(1,128)S(1)} collective-permute-done((f32[1,128]{1,0:T(1,128)S(1)}, f32[1,128]{1,0:T(1,128)S(1)}, u32[]{:S(2)}, u32[]{:S(2)}) %collective-permute-start.22) | collective-permute-done | bytes 544 | tf_op jit(solution)/shard_map/ppermute | solution.py:185
  81.2 2.3 %collective-permute-done.23.token3 = f32[1,128]{1,0:T(1,128)S(1)} collective-permute-done((f32[1,128]{1,0:T(1,128)S(1)}, f32[1,128]{1,0:T(1,128)S(1)}, u32[]{:S(2)}, u32[]{:S(2)}) %collective-permute-start.23) | collective-permute-done | bytes 544 | tf_op jit(solution)/shard_map/ppermute | solution.py:185
  83.6 1.7 %all-to-all-done.1.levels = f32[64,1,128]{2,1,0:T(1,128)S(1)} async-done(((f32[64,1,128]{2,1,0:T(1,128)}), f32[64,1,128]{2,1,0:T(1,128)S(1)}, u32[]{:S(2)}, u32[]{:S(2)}) %all-to-all-start.1) | async-done | bytes 32800 | tf_op jit(solution)/shard_map/all_to_all | solution.py:181
  85.3 1.0 %shard_map.61 = (f32[1,32,512]{2,1,0:T(8,128)}, f32[1,448]{1,0:T(1,128)}) custom-call(f32[64,1,128]{2,1,0:T(1,128)S(1)} %all-to-all-done.1.levels, f32[32,512]{1,0:T(8,128)S(1)} %get-tuple-element.50.upper, bf16[512,512]{1,0:T(8,128)(2,1)S(1)} %get-tuple-element.51.narrow, f32[1,32,512]{2,1,0:T(8,128)S(1)} %copy-done.1, ...), custom_call_target="tpu_custom_call" | custom-call | flops 17000000 | bytes 2097152 | tf_op jit(solution)/shard_map/pallas_call | solution.py:234
  (14 shorter events, 0.0 us)
Async XLA Ops:
  0.6 16.8 %collective-permute-start = (f32[1,448]{1,0:T(1,128)}, f32[1,448]{1,0:T(1,128)S(1)}, u32[]{:S(2)}, u32[]{:S(2)}) collective-permute-start(f32[1,448]{1,0:T(1,128)} %right.1), channel_id=1, source_target_pairs={{0,16},{16,0},{32,48},{48,32},{1,17},{17,1},{33,49},{49,33},{2,18}... | collective-permute-start | bytes 5384 | tf_op jit(solution)/shard_map/ppermute | solution.py:185
  4.5 13.2 %collective-permute-start.1 = (f32[1,448]{1,0:T(1,128)}, f32[1,448]{1,0:T(1,128)S(1)}, u32[]{:S(2)}, u32[]{:S(2)}) collective-permute-start(f32[1,448]{1,0:T(1,128)} %right.1), channel_id=1, source_target_pairs={{0,32},{16,48},{32,0},{48,16},{1,33},{17,49},{33,1},{49,17},{2,34}... | collective-permute-start | bytes 5384 | tf_op jit(solution)/shard_map/ppermute | solution.py:185
  9.6 10.2 %collective-permute-start.2 = (f32[1,448]{1,0:T(1,128)}, f32[1,448]{1,0:T(1,128)S(1)}, u32[]{:S(2)}, u32[]{:S(2)}) collective-permute-start(f32[1,448]{1,0:T(1,128)} %right.1), channel_id=1, source_target_pairs={{0,48},{16,32},{32,16},{48,0},{1,49},{17,33},{33,17},{49,1},{2,50}... | collective-permute-start | bytes 5384 | tf_op jit(solution)/shard_map/ppermute | solution.py:185
  10.3 0.8 copy-start
  11.1 34.5 %copy-start.2 = (f32[1,448]{1,0:T(1,128)S(1)}, f32[1,448]{1,0:T(1,128)}, u32[]{:S(2)}) copy-start(f32[1,448]{1,0:T(1,128)} %right.1) | copy-start | bytes 5380
  13.1 6.9 %collective-permute-start.10 = (bf16[32,2304]{1,0:T(8,128)(2,1)S(1)}, bf16[32,2304]{1,0:T(8,128)(2,1)S(1)}, u32[]{:S(2)}, u32[]{:S(2)}) collective-permute-start(bf16[32,2304]{1,0:T(8,128)(2,1)S(1)} %get-tuple-element.36), channel_id=1, source_target_pairs={{0,2},{1,3},{2,4},{3,5},{4,6},{5,7},{6,0},{7,1},{8,10},{9,11},{10,... | collective-permute-start | bytes 442376 | tf_op jit(solution)/shard_map/ppermute | solution.py:193
  14.4 7.8 %collective-permute-start.11 = (bf16[32,2304]{1,0:T(8,128)(2,1)S(1)}, bf16[32,2304]{1,0:T(8,128)(2,1)S(1)}, u32[]{:S(2)}, u32[]{:S(2)}) collective-permute-start(bf16[32,2304]{1,0:T(8,128)(2,1)S(1)} %get-tuple-element.37), channel_id=1, source_target_pairs={{0,11},{1,10},{2,13},{3,12},{4,15},{5,14},{6,9},{7,8},{8,3},{9,2},... | collective-permute-start | bytes 442376 | tf_op jit(solution)/shard_map/ppermute | solution.py:193
  17.4 10.2 %collective-permute-start.12 = (bf16[32,2304]{1,0:T(8,128)(2,1)S(1)}, bf16[32,2304]{1,0:T(8,128)(2,1)S(1)}, u32[]{:S(2)}, u32[]{:S(2)}) collective-permute-start(bf16[32,2304]{1,0:T(8,128)(2,1)S(1)} %get-tuple-element.38), channel_id=1, source_target_pairs={{0,7},{1,6},{2,1},{3,0},{4,3},{5,2},{6,5},{7,4},{8,15},{9,14},{10,... | collective-permute-start | bytes 442376 | tf_op jit(solution)/shard_map/ppermute | solution.py:193
  17.8 9.9 %collective-permute-start.13 = (bf16[32,2304]{1,0:T(8,128)(2,1)S(1)}, bf16[32,2304]{1,0:T(8,128)(2,1)S(1)}, u32[]{:S(2)}, u32[]{:S(2)}) collective-permute-start(bf16[32,2304]{1,0:T(8,128)(2,1)S(1)} %get-tuple-element.39), channel_id=1, source_target_pairs={{0,15},{1,14},{2,9},{3,8},{4,11},{5,10},{6,13},{7,12},{8,7},{9,6},... | collective-permute-start | bytes 442376 | tf_op jit(solution)/shard_map/ppermute | solution.py:193
  19.9 8.6 %collective-permute-start.14 = (bf16[32,2304]{1,0:T(8,128)(2,1)S(1)}, bf16[32,2304]{1,0:T(8,128)(2,1)S(1)}, u32[]{:S(2)}, u32[]{:S(2)}) collective-permute-start(bf16[32,2304]{1,0:T(8,128)(2,1)S(1)} %get-tuple-element.40), channel_id=1, source_target_pairs={{0,3},{1,2},{2,5},{3,4},{4,7},{5,6},{6,1},{7,0},{8,11},{9,10},{10,... | collective-permute-start | bytes 442376 | tf_op jit(solution)/shard_map/ppermute | solution.py:193
  20.0 11.0 %collective-permute-start.15 = (bf16[32,2304]{1,0:T(8,128)(2,1)S(1)}, bf16[32,2304]{1,0:T(8,128)(2,1)S(1)}, u32[]{:S(2)}, u32[]{:S(2)}) collective-permute-start(bf16[32,2304]{1,0:T(8,128)(2,1)S(1)} %get-tuple-element.41), channel_id=1, source_target_pairs={{0,12},{1,13},{2,14},{3,15},{4,8},{5,9},{6,10},{7,11},{8,4},{9,5},... | collective-permute-start | bytes 442376 | tf_op jit(solution)/shard_map/ppermute | solution.py:193
  22.1 10.7 %collective-permute-start.16 = (bf16[32,2304]{1,0:T(8,128)(2,1)S(1)}, bf16[32,2304]{1,0:T(8,128)(2,1)S(1)}, u32[]{:S(2)}, u32[]{:S(2)}) collective-permute-start(bf16[32,2304]{1,0:T(8,128)(2,1)S(1)} %get-tuple-element.42), channel_id=1, source_target_pairs={{0,13},{1,12},{2,15},{3,14},{4,9},{5,8},{6,11},{7,10},{8,5},{9,4},... | collective-permute-start | bytes 442376 | tf_op jit(solution)/shard_map/ppermute | solution.py:193
  27.6 8.1 %collective-permute-start.17 = (bf16[32,2304]{1,0:T(8,128)(2,1)S(1)}, bf16[32,2304]{1,0:T(8,128)(2,1)S(1)}, u32[]{:S(2)}, u32[]{:S(2)}) collective-permute-start(bf16[32,2304]{1,0:T(8,128)(2,1)S(1)} %get-tuple-element.43), channel_id=1, source_target_pairs={{0,1},{1,0},{2,3},{3,2},{4,5},{5,4},{6,7},{7,6},{8,9},{9,8},{10,11... | collective-permute-start | bytes 442376 | tf_op jit(solution)/shard_map/ppermute | solution.py:193
  27.7 9.4 %collective-permute-start.3 = (bf16[32,2304]{1,0:T(8,128)(2,1)S(1)}, bf16[32,2304]{1,0:T(8,128)(2,1)S(1)}, u32[]{:S(2)}, u32[]{:S(2)}) collective-permute-start(bf16[32,2304]{1,0:T(8,128)(2,1)S(1)} %get-tuple-element.29), channel_id=1, source_target_pairs={{0,8},{1,9},{2,10},{3,11},{4,12},{5,13},{6,14},{7,15},{8,0},{9,1},... | collective-permute-start | bytes 442376 | tf_op jit(solution)/shard_map/ppermute | solution.py:193
  28.5 10.4 %collective-permute-start.4 = (bf16[32,2304]{1,0:T(8,128)(2,1)S(1)}, bf16[32,2304]{1,0:T(8,128)(2,1)S(1)}, u32[]{:S(2)}, u32[]{:S(2)}) collective-permute-start(bf16[32,2304]{1,0:T(8,128)(2,1)S(1)} %get-tuple-element.30), channel_id=1, source_target_pairs={{0,4},{1,5},{2,6},{3,7},{4,0},{5,1},{6,2},{7,3},{8,12},{9,13},{10,... | collective-permute-start | bytes 442376 | tf_op jit(solution)/shard_map/ppermute | solution.py:193
  30.9 10.0 %collective-permute-start.5 = (bf16[32,2304]{1,0:T(8,128)(2,1)S(1)}, bf16[32,2304]{1,0:T(8,128)(2,1)S(1)}, u32[]{:S(2)}, u32[]{:S(2)}) collective-permute-start(bf16[32,2304]{1,0:T(8,128)(2,1)S(1)} %get-tuple-element.31), channel_id=1, source_target_pairs={{0,9},{1,8},{2,11},{3,10},{4,13},{5,12},{6,15},{7,14},{8,1},{9,0},... | collective-permute-start | bytes 442376 | tf_op jit(solution)/shard_map/ppermute | solution.py:193
  32.9 8.1 %collective-permute-start.6 = (bf16[32,2304]{1,0:T(8,128)(2,1)S(1)}, bf16[32,2304]{1,0:T(8,128)(2,1)S(1)}, u32[]{:S(2)}, u32[]{:S(2)}) collective-permute-start(bf16[32,2304]{1,0:T(8,128)(2,1)S(1)} %get-tuple-element.32), channel_id=1, source_target_pairs={{0,5},{1,4},{2,7},{3,6},{4,1},{5,0},{6,3},{7,2},{8,13},{9,12},{10,... | collective-permute-start | bytes 442376 | tf_op jit(solution)/shard_map/ppermute | solution.py:193
  35.8 6.4 %collective-permute-start.7 = (bf16[32,2304]{1,0:T(8,128)(2,1)S(1)}, bf16[32,2304]{1,0:T(8,128)(2,1)S(1)}, u32[]{:S(2)}, u32[]{:S(2)}) collective-permute-start(bf16[32,2304]{1,0:T(8,128)(2,1)S(1)} %get-tuple-element.33), channel_id=1, source_target_pairs={{0,10},{1,11},{2,12},{3,13},{4,14},{5,15},{6,8},{7,9},{8,2},{9,3},... | collective-permute-start | bytes 442376 | tf_op jit(solution)/shard_map/ppermute | solution.py:193
  37.0 5.9 %collective-permute-start.8 = (bf16[32,2304]{1,0:T(8,128)(2,1)S(1)}, bf16[32,2304]{1,0:T(8,128)(2,1)S(1)}, u32[]{:S(2)}, u32[]{:S(2)}) collective-permute-start(bf16[32,2304]{1,0:T(8,128)(2,1)S(1)} %get-tuple-element.34), channel_id=1, source_target_pairs={{0,6},{1,7},{2,0},{3,1},{4,2},{5,3},{6,4},{7,5},{8,14},{9,15},{10,... | collective-permute-start | bytes 442376 | tf_op jit(solution)/shard_map/ppermute | solution.py:193
  38.9 6.7 %collective-permute-start.9 = (bf16[32,2304]{1,0:T(8,128)(2,1)S(1)}, bf16[32,2304]{1,0:T(8,128)(2,1)S(1)}, u32[]{:S(2)}, u32[]{:S(2)}) collective-permute-start(bf16[32,2304]{1,0:T(8,128)(2,1)S(1)} %get-tuple-element.35), channel_id=1, source_target_pairs={{0,14},{1,15},{2,8},{3,9},{4,10},{5,11},{6,12},{7,13},{8,6},{9,7},... | collective-permute-start | bytes 442376 | tf_op jit(solution)/shard_map/ppermute | solution.py:193
  45.7 39.6 %copy-start.1 = (f32[1,32,512]{2,1,0:T(8,128)S(1)}, f32[1,32,512]{2,1,0:T(8,128)}, u32[]{:S(2)}) copy-start(f32[1,32,512]{2,1,0:T(8,128)} %factor.3) | copy-start | bytes 196612
  48.6 18.5 %all-to-all-start = ((bf16[16,32,512]{2,1,0:T(8,128)(2,1)}), bf16[16,32,512]{2,1,0:T(8,128)(2,1)S(1)}, u32[]{:S(2)}, u32[]{:S(2)}) async-start(bf16[16,32,512]{2,1,0:T(8,128)(2,1)} %bitcast), calls=%async_computation | async-start | bytes 1048576 | tf_op jit(solution)/shard_map/all_to_all | solution.py:181
  55.5 6.3 %collective-permute-start.18 = (f32[1,448]{1,0:T(1,128)S(1)}, f32[1,448]{1,0:T(1,128)S(1)}, u32[]{:S(2)}, u32[]{:S(2)}) collective-permute-start(f32[1,448]{1,0:T(1,128)S(1)} %get-tuple-element.46), channel_id=1, source_target_pairs={{0,16},{16,0},{32,48},{48,32},{1,17},{17,1},{33,49},{49,33},{2,18}... | collective-permute-start | bytes 5384 | tf_op jit(solution)/shard_map/ppermute | solution.py:185
  58.0 9.2 %collective-permute-start.19 = (f32[1,448]{1,0:T(1,128)S(1)}, f32[1,448]{1,0:T(1,128)S(1)}, u32[]{:S(2)}, u32[]{:S(2)}) collective-permute-start(f32[1,448]{1,0:T(1,128)S(1)} %get-tuple-element.47), channel_id=1, source_target_pairs={{0,32},{16,48},{32,0},{48,16},{1,33},{17,49},{33,1},{49,17},{2,34}... | collective-permute-start | bytes 5384 | tf_op jit(solution)/shard_map/ppermute | solution.py:185
  61.6 5.6 %collective-permute-start.20 = (f32[1,448]{1,0:T(1,128)S(1)}, f32[1,448]{1,0:T(1,128)S(1)}, u32[]{:S(2)}, u32[]{:S(2)}) collective-permute-start(f32[1,448]{1,0:T(1,128)S(1)} %get-tuple-element.48), channel_id=1, source_target_pairs={{0,48},{16,32},{32,16},{48,0},{1,49},{17,33},{33,17},{49,1},{2,50}... | collective-permute-start | bytes 5384 | tf_op jit(solution)/shard_map/ppermute | solution.py:185
  68.1 17.2 %all-to-all-start.1 = ((f32[64,1,128]{2,1,0:T(1,128)}), f32[64,1,128]{2,1,0:T(1,128)S(1)}, u32[]{:S(2)}, u32[]{:S(2)}) async-start(f32[64,1,128]{2,1,0:T(1,128)} %get-tuple-element.49), calls=%async_computation.1 | async-start | bytes 65536 | tf_op jit(solution)/shard_map/all_to_all | solution.py:181
  75.9 4.0 %collective-permute-start.21 = (f32[1,128]{1,0:T(1,128)S(1)}, f32[1,128]{1,0:T(1,128)S(1)}, u32[]{:S(2)}, u32[]{:S(2)}) collective-permute-start(f32[1,128]{1,0:T(1,128)S(1)} %get-tuple-element.53.token0), channel_id=1, source_target_pairs={{0,64},{64,0},{128,192},{192,128},{1,65},{65,1},{129,193},{193,129... | collective-permute-start | bytes 1544 | tf_op jit(solution)/shard_map/ppermute | solution.py:185
  77.3 3.9 %collective-permute-start.22 = (f32[1,128]{1,0:T(1,128)S(1)}, f32[1,128]{1,0:T(1,128)S(1)}, u32[]{:S(2)}, u32[]{:S(2)}) collective-permute-start(f32[1,128]{1,0:T(1,128)S(1)} %get-tuple-element.53.token0), channel_id=1, source_target_pairs={{0,128},{64,192},{128,0},{192,64},{1,129},{65,193},{129,1},{193,65... | collective-permute-start | bytes 1544 | tf_op jit(solution)/shard_map/ppermute | solution.py:185
  79.9 3.6 %collective-permute-start.23 = (f32[1,128]{1,0:T(1,128)S(1)}, f32[1,128]{1,0:T(1,128)S(1)}, u32[]{:S(2)}, u32[]{:S(2)}) collective-permute-start(f32[1,128]{1,0:T(1,128)S(1)} %get-tuple-element.53.token0), channel_id=1, source_target_pairs={{0,192},{64,128},{128,64},{192,0},{1,193},{65,129},{129,65},{193,1... | collective-permute-start | bytes 1544 | tf_op jit(solution)/shard_map/ppermute | solution.py:185

commit v5 on v4

--- a/solution.py
+++ b/solution.py
@@ -18,8 +18,8 @@
 SPAN = 16 * OWN
 HALF = 8 * OWN
 OFFSETS = (
-    (1, 0, 0), (0, 2, 0), (1, 0, 1), (0, 2, 1), (1, 1, 0), (0, 3, 0), (1, 3, 0), (0, 1, 0),
-    (1, 1, 1), (0, 3, 1), (1, 3, 1), (0, 1, 1), (1, 2, 0), (1, 2, 1), (0, 0, 1), (0, 0, 0),
+    (1, 0, 0), (0, 2, 0), (1, 0, 1), (0, 3, 0), (1, 1, 0), (0, 2, 1), (1, 3, 0), (0, 3, 1),
+    (1, 1, 1), (0, 1, 0), (1, 3, 1), (0, 1, 1), (1, 2, 0), (1, 2, 1), (0, 0, 1), (0, 0, 0),
 )
 PEERS = len(OFFSETS)
 WIDE = 1792
@@ -99,15 +99,16 @@
     last = (((1,), (1,)), ((), ()))
     high = lax.dot_general(image[0:256, :], image[...], last, preferred_element_type=jnp.float32)
     low = lax.dot_general(image[256:512, :], image[256:512, :], last, preferred_element_type=jnp.float32)
-    places = [[lax.broadcasted_iota(jnp.int32, half.shape, k) for k in range(2)] for half in (high, low)]
-    least = [jnp.min(jnp.where(row == col, half, jnp.inf)) for half, (row, col) in zip((high, low), places)]
+    row = lax.broadcasted_iota(jnp.int32, (256, 256), 0)
+    col = lax.broadcasted_iota(jnp.int32, (256, 256), 1)
+    on = row == col
+    slot = jnp.logical_and(row % ROWS == ROWS - 1, col == row - (ROWS - 1))
+    corners = (high[:, 0:256], low)
+    least = [jnp.min(jnp.where(on, corner, jnp.inf)) for corner in corners]
     share = jnp.full((8, 128), jnp.minimum(*least), jnp.float32).astype(part.dtype).astype(jnp.float32)[0:1, 0:1]
-    shared = []
-    for half, (row, col) in zip((high, low), places):
-        half = jnp.where(row == col, half - share, half)
-        slot = jnp.logical_and(row % ROWS == ROWS - 1, col == row - (ROWS - 1))
-        shared.append(jnp.where(slot, share, half).astype(part.dtype))
-    part[0:256, :], part[256:512, 256:512] = shared
+    shared = [jnp.where(slot, share, jnp.where(on, corner - share, corner)).astype(part.dtype) for corner in corners]
+    part[0:256, 0:256], part[256:512, 256:512] = shared
+    part[0:256, 256:512] = high[:, 256:512].astype(part.dtype)
     part[256:512, 0:256] = jnp.zeros((256, 256), part.dtype)
 
 
@@ -228,7 +229,10 @@
     parts = exchange(part.reshape(16, ROWS, BLOCK), GROUP)
     sums = [sums[0]] + [across(sums[d], d) for d in (1, 2, 3)]
     upper, term, levels = call(
-        peaks_kernel, [VMEM] * 5, [shape((ROWS, BLOCK)), shape((1, OWN)), shape((64, 1, 128))], 2000000
+        peaks_kernel,
+        [VMEM] * 5,
+        [shape((ROWS, BLOCK)), shape((1, OWN)), shape((64, 1, 128))],
+        2000000,
     )(parts, *sums)
     levels = exchange(levels, SHARD)
     new_factor, new_right = call(

time: 86.6 us -> 89.3 us (1.031)
  waiting for transfers between devices: 16.8 us -> 29.1 us
  starting transfers between devices: 60.5 us -> 50.9 us
    ppermute x15, waiting for transfers between devices: 5.92 us -> 18.2 us  [to_peer(): return lax.ppermute(value, GROUP, pairs)]
    ppermute x15, starting transfers between devices: 26.6 us -> 19.3 us  [to_peer(): return lax.ppermute(value, GROUP, pairs)]
    all_to_all x2, starting transfers between devices: 14.7 us -> 12.6 us  [exchange(): return lax.all_to_all(value, axes, 0, 0, tiled=True)]
  transfers between devices with their start and end apart: 26 -> 26, of which waited for: 11 -> 10; matrix products, arithmetic and copies ran while one was open for 0% -> 0% of each run, Pallas kernels for 2% -> 2%
where the time goes in v5:
time: 89.3 us; the launch traced here: 89 us
  starting transfers between devices  50.9 us (57%)
  waiting for transfers between devices  29.1 us (33%)
  Pallas kernels  6.79 us (8%)
  between operations  1.34 us (2%)
    ppermute x15, starting transfers between devices, to_peer(): return lax.ppermute(value, GROUP, pairs)  19.3 us
    ppermute x9, starting transfers between devices, across(): return lax.ppermute(value, axis, [(k, k ^ turn) for k in range(4)])  19 us
    ppermute x15, waiting for transfers between devices, to_peer(): return lax.ppermute(value, GROUP, pairs)  18.2 us
    all_to_all x2, starting transfers between devices, exchange(): return lax.all_to_all(value, axes, 0, 0, tiled=True)  12.6 us
    ppermute x9, waiting for transfers between devices, across(): return lax.ppermute(value, axis, [(k, k ^ turn) for k in range(4)])  9.24 us
    pallas_call x1, Pallas kernels, inner(): call(gram_kernel, [VMEM] * (PEERS + 4), [shape((BLOCK, BLOCK), half)] + [...  2.99 us
    pallas_call x1, Pallas kernels, pack(): pl.pallas_call(pack_kernel, out_shape=outs + [shape((1, 128))], in_specs=...  1.92 us
  transfers between devices with their start and end apart: 26, of which 10 were waited for; matrix products, arithmetic and copies ran while one was open for 0% of the time, Pallas kernels for 2%

profile of v5, /device:TPU:1, one launch (start us, length us, event | category | flops | bytes accessed | tf_op | source)
XLA Modules:
  0.0 89.0 jit_solution(7931671632388587535)
XLA Ops:
  0.6 3.9 %collective-permute-start = (f32[1,448]{1,0:T(1,128)}, f32[1,448]{1,0:T(1,128)S(1)}, u32[]{:S(2)}, u32[]{:S(2)}) collective-permute-start(f32[1,448]{1,0:T(1,128)} %right.1), channel_id=1, source_target_pairs={{0,16},{16,0},{32,48},{48,32},{1,17},{17,1},{33,49},{49,33},{2,18}... | collective-permute-start | bytes 5384 | tf_op jit(solution)/shard_map/ppermute | solution.py:186
  4.5 5.1 %collective-permute-start.1 = (f32[1,448]{1,0:T(1,128)}, f32[1,448]{1,0:T(1,128)S(1)}, u32[]{:S(2)}, u32[]{:S(2)}) collective-permute-start(f32[1,448]{1,0:T(1,128)} %right.1), channel_id=1, source_target_pairs={{0,32},{16,48},{32,0},{48,16},{1,33},{17,49},{33,1},{49,17},{2,34}... | collective-permute-start | bytes 5384 | tf_op jit(solution)/shard_map/ppermute | solution.py:186
  10.3 0.0 copy-start
  10.3 0.8 copy-done
  11.1 1.9 %pack.1 = (bf16[32,2304]{1,0:T(8,128)(2,1)S(1)}, bf16[32,2304]{1,0:T(8,128)(2,1)S(1)}, bf16[32,2304]{1,0:T(8,128)(2,1)S(1)}, bf16[32,2304]{1,0:T(8,128)(2,1)S(1)...) custom-call(bf16[1,32,28672]{2,1,0:T(8,128)(2,1)} %gradient.1, ...), custom_call_target="tpu_custom_call" | custom-call | flops 2000000 | bytes 4194304 | tf_op jit(solution)/shard_map/pack/pallas_call | solution.py:200
  13.1 3.7 %collective-permute-start.10 = (bf16[32,2304]{1,0:T(8,128)(2,1)S(1)}, bf16[32,2304]{1,0:T(8,128)(2,1)S(1)}, u32[]{:S(2)}, u32[]{:S(2)}) collective-permute-start(bf16[32,2304]{1,0:T(8,128)(2,1)S(1)} %get-tuple-element.36), channel_id=1, source_target_pairs={{0,7},{1,6},{2,1},{3,0},{4,3},{5,2},{6,5},{7,4},{8,15},{9,14},{10,... | collective-permute-start | bytes 442376 | tf_op jit(solution)/shard_map/ppermute | solution.py:194
  16.7 0.0 collective-permute-start.11
  16.7 0.5 collective-permute-start.12
  17.2 3.4 %collective-permute-start.13 = (bf16[32,2304]{1,0:T(8,128)(2,1)S(1)}, bf16[32,2304]{1,0:T(8,128)(2,1)S(1)}, u32[]{:S(2)}, u32[]{:S(2)}) collective-permute-start(bf16[32,2304]{1,0:T(8,128)(2,1)S(1)} %get-tuple-element.39), channel_id=1, source_target_pairs={{0,15},{1,14},{2,9},{3,8},{4,11},{5,10},{6,13},{7,12},{8,7},{9,6},... | collective-permute-start | bytes 442376 | tf_op jit(solution)/shard_map/ppermute | solution.py:194
  20.7 0.0 collective-permute-done.2.refs_3_
  20.7 0.0 collective-permute-start.14
  20.7 0.0 collective-permute-done.10.refs_12_
  20.7 2.2 %collective-permute-start.15 = (bf16[32,2304]{1,0:T(8,128)(2,1)S(1)}, bf16[32,2304]{1,0:T(8,128)(2,1)S(1)}, u32[]{:S(2)}, u32[]{:S(2)}) collective-permute-start(bf16[32,2304]{1,0:T(8,128)(2,1)S(1)} %get-tuple-element.41), channel_id=1, source_target_pairs={{0,12},{1,13},{2,14},{3,15},{4,8},{5,9},{6,10},{7,11},{8,4},{9,5},... | collective-permute-start | bytes 442376 | tf_op jit(solution)/shard_map/ppermute | solution.py:194
  22.9 0.8 collective-permute-done.11.refs_13_
  23.7 0.8 collective-permute-start.16
  24.5 8.6 %collective-permute-done.12.refs_14_ = bf16[32,2304]{1,0:T(8,128)(2,1)S(1)} collective-permute-done((bf16[32,2304]{1,0:T(8,128)(2,1)S(1)}, bf16[32,2304]{1,0:T(8,128)(2,1)S(1)}, u32[]{:S(2)}, u32[]{:S(2)}) %collective-permute-start.12) | collective-permute-done | bytes 147488 | tf_op jit(solution)/shard_map/ppermute | solution.py:194
  33.2 0.7 collective-permute-start.17
  33.9 0.0 collective-permute-done.13.refs_15_
  33.9 0.7 collective-permute-start.3
  34.6 1.7 %collective-permute-done.14.refs_16_ = bf16[32,2304]{1,0:T(8,128)(2,1)S(1)} collective-permute-done((bf16[32,2304]{1,0:T(8,128)(2,1)S(1)}, bf16[32,2304]{1,0:T(8,128)(2,1)S(1)}, u32[]{:S(2)}, u32[]{:S(2)}) %collective-permute-start.14) | collective-permute-done | bytes 147488 | tf_op jit(solution)/shard_map/ppermute | solution.py:194
  36.3 0.1 collective-permute-start.4
  36.4 0.0 collective-permute-done.15.refs_17_
  36.4 1.3 %collective-permute-start.5 = (bf16[32,2304]{1,0:T(8,128)(2,1)S(1)}, bf16[32,2304]{1,0:T(8,128)(2,1)S(1)}, u32[]{:S(2)}, u32[]{:S(2)}) collective-permute-start(bf16[32,2304]{1,0:T(8,128)(2,1)S(1)} %get-tuple-element.31), channel_id=1, source_target_pairs={{0,9},{1,8},{2,11},{3,10},{4,13},{5,12},{6,15},{7,14},{8,1},{9,0},... | collective-permute-start | bytes 442376 | tf_op jit(solution)/shard_map/ppermute | solution.py:194
  37.7 0.0 collective-permute-done.16.refs_18_
  37.7 1.6 %collective-permute-start.6 = (bf16[32,2304]{1,0:T(8,128)(2,1)S(1)}, bf16[32,2304]{1,0:T(8,128)(2,1)S(1)}, u32[]{:S(2)}, u32[]{:S(2)}) collective-permute-start(bf16[32,2304]{1,0:T(8,128)(2,1)S(1)} %get-tuple-element.32), channel_id=1, source_target_pairs={{0,6},{1,7},{2,0},{3,1},{4,2},{5,3},{6,4},{7,5},{8,14},{9,15},{10,... | collective-permute-start | bytes 442376 | tf_op jit(solution)/shard_map/ppermute | solution.py:194
  39.3 0.0 collective-permute-done.17.refs_19_
  39.3 0.3 collective-permute-start.7
  39.6 0.0 collective-permute-done.3.refs_5_
  39.6 3.2 %collective-permute-start.8 = (bf16[32,2304]{1,0:T(8,128)(2,1)S(1)}, bf16[32,2304]{1,0:T(8,128)(2,1)S(1)}, u32[]{:S(2)}, u32[]{:S(2)}) collective-permute-start(bf16[32,2304]{1,0:T(8,128)(2,1)S(1)} %get-tuple-element.34), channel_id=1, source_target_pairs={{0,5},{1,4},{2,7},{3,6},{4,1},{5,0},{6,3},{7,2},{8,13},{9,12},{10,... | collective-permute-start | bytes 442376 | tf_op jit(solution)/shard_map/ppermute | solution.py:194
  42.8 0.0 collective-permute-done.4.refs_6_
  42.8 0.8 collective-permute-start.9
  43.7 4.2 %collective-permute-done.7.refs_9_ = bf16[32,2304]{1,0:T(8,128)(2,1)S(1)} collective-permute-done((bf16[32,2304]{1,0:T(8,128)(2,1)S(1)}, bf16[32,2304]{1,0:T(8,128)(2,1)S(1)}, u32[]{:S(2)}, u32[]{:S(2)}) %collective-permute-start.7) | collective-permute-done | bytes 147488 | tf_op jit(solution)/shard_map/ppermute | solution.py:194
  47.9 2.7 %collective-permute-done.8.refs_10_ = bf16[32,2304]{1,0:T(8,128)(2,1)S(1)} collective-permute-done((bf16[32,2304]{1,0:T(8,128)(2,1)S(1)}, bf16[32,2304]{1,0:T(8,128)(2,1)S(1)}, u32[]{:S(2)}, u32[]{:S(2)}) %collective-permute-start.8) | collective-permute-done | bytes 147488 | tf_op jit(solution)/shard_map/ppermute | solution.py:194
  50.6 0.0 collective-permute-done.9.refs_11_
  50.6 3.0 %shard_map.59 = (bf16[512,512]{1,0:T(8,128)(2,1)}, f32[1,448]{1,0:T(1,128)S(1)}, f32[1,448]{1,0:T(1,128)S(1)}, f32[1,448]{1,0:T(1,128)S(1)}, f32[1,448]{1,0:T(1,128)S(1)}, /*index=5*/bf16[512,512]{1,0:T(8,128)(2,1)S(1)}) custom-call(f32[1,448]{1,0:T(1,128)S(1)} %copy-done.2, f32[1,448]{1,0:T(1,128)S(1)} %collective-permute-done.refs_1_, ...), custom_call_target="tpu_custom_call" | custom-call | flops 1600000000 | bytes 2097152 | tf_op jit(solution)/shard_map/pallas_call | solution.py:222
  53.6 4.8 %all-to-all-start = ((bf16[16,32,512]{2,1,0:T(8,128)(2,1)}), bf16[16,32,512]{2,1,0:T(8,128)(2,1)S(1)}, u32[]{:S(2)}, u32[]{:S(2)}) async-start(bf16[16,32,512]{2,1,0:T(8,128)(2,1)} %bitcast), calls=%async_computation | async-start | bytes 1048576 | tf_op jit(solution)/shard_map/all_to_all | solution.py:182
  58.4 1.4 %collective-permute-start.18 = (f32[1,448]{1,0:T(1,128)S(1)}, f32[1,448]{1,0:T(1,128)S(1)}, u32[]{:S(2)}, u32[]{:S(2)}) collective-permute-start(f32[1,448]{1,0:T(1,128)S(1)} %get-tuple-element.46), channel_id=1, source_target_pairs={{0,16},{16,0},{32,48},{48,32},{1,17},{17,1},{33,49},{49,33},{2,18}... | collective-permute-start | bytes 5384 | tf_op jit(solution)/shard_map/ppermute | solution.py:186
  59.8 4.5 %collective-permute-start.19 = (f32[1,448]{1,0:T(1,128)S(1)}, f32[1,448]{1,0:T(1,128)S(1)}, u32[]{:S(2)}, u32[]{:S(2)}) collective-permute-start(f32[1,448]{1,0:T(1,128)S(1)} %get-tuple-element.47), channel_id=1, source_target_pairs={{0,32},{16,48},{32,0},{48,16},{1,33},{17,49},{33,1},{49,17},{2,34}... | collective-permute-start | bytes 5384 | tf_op jit(solution)/shard_map/ppermute | solution.py:186
  64.3 0.4 collective-permute-done.18.sum1
  64.7 5.2 %collective-permute-done.19.sum2 = f32[1,448]{1,0:T(1,128)S(1)} collective-permute-done((f32[1,448]{1,0:T(1,128)S(1)}, f32[1,448]{1,0:T(1,128)S(1)}, u32[]{:S(2)}, u32[]{:S(2)}) %collective-permute-start.19) | collective-permute-done | bytes 1824 | tf_op jit(solution)/shard_map/ppermute | solution.py:186
  69.9 0.9 %shard_map.60 = (f32[32,512]{1,0:T(8,128)S(1)}, f32[1,448]{1,0:T(1,128)S(1)}, f32[64,1,128]{2,1,0:T(1,128)}) custom-call(bf16[16,32,512]{2,1,0:T(8,128)(2,1)S(1)} %all-to-all-done.parts, f32[1,448]{1,0:T(1,128)S(1)} %get-tuple-element.45.sum0, f32[1,448]{1,0:T(1,128)S(1)} %collective-permute-done.18.sum1, f32[1,448]{1,0:T(1,128)S(1)} %collective-permute-done.19.sum2, ...), custom_call_target="tpu_custom_call" | custom-call | flops 2000000 | bytes 2097152 | tf_op jit(solution)/shard_map/pallas_call | solution.py:231
  70.9 7.8 %all-to-all-start.1 = ((f32[64,1,128]{2,1,0:T(1,128)}), f32[64,1,128]{2,1,0:T(1,128)S(1)}, u32[]{:S(2)}, u32[]{:S(2)}) async-start(f32[64,1,128]{2,1,0:T(1,128)} %get-tuple-element.49), calls=%async_computation.1 | async-start | bytes 65536 | tf_op jit(solution)/shard_map/all_to_all | solution.py:182
  78.7 1.4 %collective-permute-start.21 = (f32[1,128]{1,0:T(1,128)S(1)}, f32[1,128]{1,0:T(1,128)S(1)}, u32[]{:S(2)}, u32[]{:S(2)}) collective-permute-start(f32[1,128]{1,0:T(1,128)S(1)} %get-tuple-element.53.token0), channel_id=1, source_target_pairs={{0,64},{64,0},{128,192},{192,128},{1,65},{65,1},{129,193},{193,129... | collective-permute-start | bytes 1544 | tf_op jit(solution)/shard_map/ppermute | solution.py:186
  80.0 2.6 %collective-permute-start.22 = (f32[1,128]{1,0:T(1,128)S(1)}, f32[1,128]{1,0:T(1,128)S(1)}, u32[]{:S(2)}, u32[]{:S(2)}) collective-permute-start(f32[1,128]{1,0:T(1,128)S(1)} %get-tuple-element.53.token0), channel_id=1, source_target_pairs={{0,128},{64,192},{128,0},{192,64},{1,129},{65,193},{129,1},{193,65... | collective-permute-start | bytes 1544 | tf_op jit(solution)/shard_map/ppermute | solution.py:186
  82.7 1.3 %collective-permute-done.22.token2 = f32[1,128]{1,0:T(1,128)S(1)} collective-permute-done((f32[1,128]{1,0:T(1,128)S(1)}, f32[1,128]{1,0:T(1,128)S(1)}, u32[]{:S(2)}, u32[]{:S(2)}) %collective-permute-start.22) | collective-permute-done | bytes 544 | tf_op jit(solution)/shard_map/ppermute | solution.py:186
  84.0 2.3 %collective-permute-done.23.token3 = f32[1,128]{1,0:T(1,128)S(1)} collective-permute-done((f32[1,128]{1,0:T(1,128)S(1)}, f32[1,128]{1,0:T(1,128)S(1)}, u32[]{:S(2)}, u32[]{:S(2)}) %collective-permute-start.23) | collective-permute-done | bytes 544 | tf_op jit(solution)/shard_map/ppermute | solution.py:186
  86.3 1.7 %all-to-all-done.1.levels = f32[64,1,128]{2,1,0:T(1,128)S(1)} async-done(((f32[64,1,128]{2,1,0:T(1,128)}), f32[64,1,128]{2,1,0:T(1,128)S(1)}, u32[]{:S(2)}, u32[]{:S(2)}) %all-to-all-start.1) | async-done | bytes 32800 | tf_op jit(solution)/shard_map/all_to_all | solution.py:182
  88.0 1.0 %shard_map.61 = (f32[1,32,512]{2,1,0:T(8,128)}, f32[1,448]{1,0:T(1,128)}) custom-call(f32[64,1,128]{2,1,0:T(1,128)S(1)} %all-to-all-done.1.levels, f32[32,512]{1,0:T(8,128)S(1)} %get-tuple-element.50.upper, bf16[512,512]{1,0:T(8,128)(2,1)S(1)} %get-tuple-element.51.narrow, f32[1,32,512]{2,1,0:T(8,128)S(1)} %copy-done.1, ...), custom_call_target="tpu_custom_call" | custom-call | flops 17000000 | bytes 2097152 | tf_op jit(solution)/shard_map/pallas_call | solution.py:238
  (14 shorter events, 0.0 us)
Async XLA Ops:
  0.6 16.1 %collective-permute-start = (f32[1,448]{1,0:T(1,128)}, f32[1,448]{1,0:T(1,128)S(1)}, u32[]{:S(2)}, u32[]{:S(2)}) collective-permute-start(f32[1,448]{1,0:T(1,128)} %right.1), channel_id=1, source_target_pairs={{0,16},{16,0},{32,48},{48,32},{1,17},{17,1},{33,49},{49,33},{2,18}... | collective-permute-start | bytes 5384 | tf_op jit(solution)/shard_map/ppermute | solution.py:186
  4.5 12.7 %collective-permute-start.1 = (f32[1,448]{1,0:T(1,128)}, f32[1,448]{1,0:T(1,128)S(1)}, u32[]{:S(2)}, u32[]{:S(2)}) collective-permute-start(f32[1,448]{1,0:T(1,128)} %right.1), channel_id=1, source_target_pairs={{0,32},{16,48},{32,0},{48,16},{1,33},{17,49},{33,1},{49,17},{2,34}... | collective-permute-start | bytes 5384 | tf_op jit(solution)/shard_map/ppermute | solution.py:186
  9.6 11.1 %collective-permute-start.2 = (f32[1,448]{1,0:T(1,128)}, f32[1,448]{1,0:T(1,128)S(1)}, u32[]{:S(2)}, u32[]{:S(2)}) collective-permute-start(f32[1,448]{1,0:T(1,128)} %right.1), channel_id=1, source_target_pairs={{0,48},{16,32},{32,16},{48,0},{1,49},{17,33},{33,17},{49,1},{2,50}... | collective-permute-start | bytes 5384 | tf_op jit(solution)/shard_map/ppermute | solution.py:186
  10.3 0.8 copy-start
  11.1 39.5 %copy-start.2 = (f32[1,448]{1,0:T(1,128)S(1)}, f32[1,448]{1,0:T(1,128)}, u32[]{:S(2)}) copy-start(f32[1,448]{1,0:T(1,128)} %right.1) | copy-start | bytes 5380
  13.1 7.6 %collective-permute-start.10 = (bf16[32,2304]{1,0:T(8,128)(2,1)S(1)}, bf16[32,2304]{1,0:T(8,128)(2,1)S(1)}, u32[]{:S(2)}, u32[]{:S(2)}) collective-permute-start(bf16[32,2304]{1,0:T(8,128)(2,1)S(1)} %get-tuple-element.36), channel_id=1, source_target_pairs={{0,7},{1,6},{2,1},{3,0},{4,3},{5,2},{6,5},{7,4},{8,15},{9,14},{10,... | collective-permute-start | bytes 442376 | tf_op jit(solution)/shard_map/ppermute | solution.py:194
  16.7 6.9 %collective-permute-start.11 = (bf16[32,2304]{1,0:T(8,128)(2,1)S(1)}, bf16[32,2304]{1,0:T(8,128)(2,1)S(1)}, u32[]{:S(2)}, u32[]{:S(2)}) collective-permute-start(bf16[32,2304]{1,0:T(8,128)(2,1)S(1)} %get-tuple-element.37), channel_id=1, source_target_pairs={{0,11},{1,10},{2,13},{3,12},{4,15},{5,14},{6,9},{7,8},{8,3},{9,2},... | collective-permute-start | bytes 442376 | tf_op jit(solution)/shard_map/ppermute | solution.py:194
  16.7 16.4 %collective-permute-start.12 = (bf16[32,2304]{1,0:T(8,128)(2,1)S(1)}, bf16[32,2304]{1,0:T(8,128)(2,1)S(1)}, u32[]{:S(2)}, u32[]{:S(2)}) collective-permute-start(bf16[32,2304]{1,0:T(8,128)(2,1)S(1)} %get-tuple-element.38), channel_id=1, source_target_pairs={{0,2},{1,3},{2,4},{3,5},{4,6},{5,7},{6,0},{7,1},{8,10},{9,11},{10,... | collective-permute-start | bytes 442376 | tf_op jit(solution)/shard_map/ppermute | solution.py:194
  17.2 16.6 %collective-permute-start.13 = (bf16[32,2304]{1,0:T(8,128)(2,1)S(1)}, bf16[32,2304]{1,0:T(8,128)(2,1)S(1)}, u32[]{:S(2)}, u32[]{:S(2)}) collective-permute-start(bf16[32,2304]{1,0:T(8,128)(2,1)S(1)} %get-tuple-element.39), channel_id=1, source_target_pairs={{0,15},{1,14},{2,9},{3,8},{4,11},{5,10},{6,13},{7,12},{8,7},{9,6},... | collective-permute-start | bytes 442376 | tf_op jit(solution)/shard_map/ppermute | solution.py:194
  20.7 15.6 %collective-permute-start.14 = (bf16[32,2304]{1,0:T(8,128)(2,1)S(1)}, bf16[32,2304]{1,0:T(8,128)(2,1)S(1)}, u32[]{:S(2)}, u32[]{:S(2)}) collective-permute-start(bf16[32,2304]{1,0:T(8,128)(2,1)S(1)} %get-tuple-element.40), channel_id=1, source_target_pairs={{0,3},{1,2},{2,5},{3,4},{4,7},{5,6},{6,1},{7,0},{8,11},{9,10},{10,... | collective-permute-start | bytes 442376 | tf_op jit(solution)/shard_map/ppermute | solution.py:194
  20.7 15.7 %collective-permute-start.15 = (bf16[32,2304]{1,0:T(8,128)(2,1)S(1)}, bf16[32,2304]{1,0:T(8,128)(2,1)S(1)}, u32[]{:S(2)}, u32[]{:S(2)}) collective-permute-start(bf16[32,2304]{1,0:T(8,128)(2,1)S(1)} %get-tuple-element.41), channel_id=1, source_target_pairs={{0,12},{1,13},{2,14},{3,15},{4,8},{5,9},{6,10},{7,11},{8,4},{9,5},... | collective-permute-start | bytes 442376 | tf_op jit(solution)/shard_map/ppermute | solution.py:194
  23.7 14.0 %collective-permute-start.16 = (bf16[32,2304]{1,0:T(8,128)(2,1)S(1)}, bf16[32,2304]{1,0:T(8,128)(2,1)S(1)}, u32[]{:S(2)}, u32[]{:S(2)}) collective-permute-start(bf16[32,2304]{1,0:T(8,128)(2,1)S(1)} %get-tuple-element.42), channel_id=1, source_target_pairs={{0,13},{1,12},{2,15},{3,14},{4,9},{5,8},{6,11},{7,10},{8,5},{9,4},... | collective-permute-start | bytes 442376 | tf_op jit(solution)/shard_map/ppermute | solution.py:194
  33.2 6.1 %collective-permute-start.17 = (bf16[32,2304]{1,0:T(8,128)(2,1)S(1)}, bf16[32,2304]{1,0:T(8,128)(2,1)S(1)}, u32[]{:S(2)}, u32[]{:S(2)}) collective-permute-start(bf16[32,2304]{1,0:T(8,128)(2,1)S(1)} %get-tuple-element.43), channel_id=1, source_target_pairs={{0,1},{1,0},{2,3},{3,2},{4,5},{5,4},{6,7},{7,6},{8,9},{9,8},{10,11... | collective-permute-start | bytes 442376 | tf_op jit(solution)/shard_map/ppermute | solution.py:194
  33.9 5.8 %collective-permute-start.3 = (bf16[32,2304]{1,0:T(8,128)(2,1)S(1)}, bf16[32,2304]{1,0:T(8,128)(2,1)S(1)}, u32[]{:S(2)}, u32[]{:S(2)}) collective-permute-start(bf16[32,2304]{1,0:T(8,128)(2,1)S(1)} %get-tuple-element.29), channel_id=1, source_target_pairs={{0,8},{1,9},{2,10},{3,11},{4,12},{5,13},{6,14},{7,15},{8,0},{9,1},... | collective-permute-start | bytes 442376 | tf_op jit(solution)/shard_map/ppermute | solution.py:194
  36.3 6.5 %collective-permute-start.4 = (bf16[32,2304]{1,0:T(8,128)(2,1)S(1)}, bf16[32,2304]{1,0:T(8,128)(2,1)S(1)}, u32[]{:S(2)}, u32[]{:S(2)}) collective-permute-start(bf16[32,2304]{1,0:T(8,128)(2,1)S(1)} %get-tuple-element.30), channel_id=1, source_target_pairs={{0,4},{1,5},{2,6},{3,7},{4,0},{5,1},{6,2},{7,3},{8,12},{9,13},{10,... | collective-permute-start | bytes 442376 | tf_op jit(solution)/shard_map/ppermute | solution.py:194
  36.4 7.2 %collective-permute-start.5 = (bf16[32,2304]{1,0:T(8,128)(2,1)S(1)}, bf16[32,2304]{1,0:T(8,128)(2,1)S(1)}, u32[]{:S(2)}, u32[]{:S(2)}) collective-permute-start(bf16[32,2304]{1,0:T(8,128)(2,1)S(1)} %get-tuple-element.31), channel_id=1, source_target_pairs={{0,9},{1,8},{2,11},{3,10},{4,13},{5,12},{6,15},{7,14},{8,1},{9,0},... | collective-permute-start | bytes 442376 | tf_op jit(solution)/shard_map/ppermute | solution.py:194
  37.7 6.0 %collective-permute-start.6 = (bf16[32,2304]{1,0:T(8,128)(2,1)S(1)}, bf16[32,2304]{1,0:T(8,128)(2,1)S(1)}, u32[]{:S(2)}, u32[]{:S(2)}) collective-permute-start(bf16[32,2304]{1,0:T(8,128)(2,1)S(1)} %get-tuple-element.32), channel_id=1, source_target_pairs={{0,6},{1,7},{2,0},{3,1},{4,2},{5,3},{6,4},{7,5},{8,14},{9,15},{10,... | collective-permute-start | bytes 442376 | tf_op jit(solution)/shard_map/ppermute | solution.py:194
  39.3 8.6 %collective-permute-start.7 = (bf16[32,2304]{1,0:T(8,128)(2,1)S(1)}, bf16[32,2304]{1,0:T(8,128)(2,1)S(1)}, u32[]{:S(2)}, u32[]{:S(2)}) collective-permute-start(bf16[32,2304]{1,0:T(8,128)(2,1)S(1)} %get-tuple-element.33), channel_id=1, source_target_pairs={{0,10},{1,11},{2,12},{3,13},{4,14},{5,15},{6,8},{7,9},{8,2},{9,3},... | collective-permute-start | bytes 442376 | tf_op jit(solution)/shard_map/ppermute | solution.py:194
  39.6 11.0 %collective-permute-start.8 = (bf16[32,2304]{1,0:T(8,128)(2,1)S(1)}, bf16[32,2304]{1,0:T(8,128)(2,1)S(1)}, u32[]{:S(2)}, u32[]{:S(2)}) collective-permute-start(bf16[32,2304]{1,0:T(8,128)(2,1)S(1)} %get-tuple-element.34), channel_id=1, source_target_pairs={{0,5},{1,4},{2,7},{3,6},{4,1},{5,0},{6,3},{7,2},{8,13},{9,12},{10,... | collective-permute-start | bytes 442376 | tf_op jit(solution)/shard_map/ppermute | solution.py:194
  42.8 7.8 %collective-permute-start.9 = (bf16[32,2304]{1,0:T(8,128)(2,1)S(1)}, bf16[32,2304]{1,0:T(8,128)(2,1)S(1)}, u32[]{:S(2)}, u32[]{:S(2)}) collective-permute-start(bf16[32,2304]{1,0:T(8,128)(2,1)S(1)} %get-tuple-element.35), channel_id=1, source_target_pairs={{0,14},{1,15},{2,8},{3,9},{4,10},{5,11},{6,12},{7,13},{8,6},{9,7},... | collective-permute-start | bytes 442376 | tf_op jit(solution)/shard_map/ppermute | solution.py:194
  50.6 37.4 %copy-start.1 = (f32[1,32,512]{2,1,0:T(8,128)S(1)}, f32[1,32,512]{2,1,0:T(8,128)}, u32[]{:S(2)}) copy-start(f32[1,32,512]{2,1,0:T(8,128)} %factor.3) | copy-start | bytes 196612
  53.6 16.3 %all-to-all-start = ((bf16[16,32,512]{2,1,0:T(8,128)(2,1)}), bf16[16,32,512]{2,1,0:T(8,128)(2,1)S(1)}, u32[]{:S(2)}, u32[]{:S(2)}) async-start(bf16[16,32,512]{2,1,0:T(8,128)(2,1)} %bitcast), calls=%async_computation | async-start | bytes 1048576 | tf_op jit(solution)/shard_map/all_to_all | solution.py:182
  58.4 6.3 %collective-permute-start.18 = (f32[1,448]{1,0:T(1,128)S(1)}, f32[1,448]{1,0:T(1,128)S(1)}, u32[]{:S(2)}, u32[]{:S(2)}) collective-permute-start(f32[1,448]{1,0:T(1,128)S(1)} %get-tuple-element.46), channel_id=1, source_target_pairs={{0,16},{16,0},{32,48},{48,32},{1,17},{17,1},{33,49},{49,33},{2,18}... | collective-permute-start | bytes 5384 | tf_op jit(solution)/shard_map/ppermute | solution.py:186
  59.8 10.1 %collective-permute-start.19 = (f32[1,448]{1,0:T(1,128)S(1)}, f32[1,448]{1,0:T(1,128)S(1)}, u32[]{:S(2)}, u32[]{:S(2)}) collective-permute-start(f32[1,448]{1,0:T(1,128)S(1)} %get-tuple-element.47), channel_id=1, source_target_pairs={{0,32},{16,48},{32,0},{48,16},{1,33},{17,49},{33,1},{49,17},{2,34}... | collective-permute-start | bytes 5384 | tf_op jit(solution)/shard_map/ppermute | solution.py:186
  64.3 5.6 %collective-permute-start.20 = (f32[1,448]{1,0:T(1,128)S(1)}, f32[1,448]{1,0:T(1,128)S(1)}, u32[]{:S(2)}, u32[]{:S(2)}) collective-permute-start(f32[1,448]{1,0:T(1,128)S(1)} %get-tuple-element.48), channel_id=1, source_target_pairs={{0,48},{16,32},{32,16},{48,0},{1,49},{17,33},{33,17},{49,1},{2,50}... | collective-permute-start | bytes 5384 | tf_op jit(solution)/shard_map/ppermute | solution.py:186
  70.9 17.1 %all-to-all-start.1 = ((f32[64,1,128]{2,1,0:T(1,128)}), f32[64,1,128]{2,1,0:T(1,128)S(1)}, u32[]{:S(2)}, u32[]{:S(2)}) async-start(f32[64,1,128]{2,1,0:T(1,128)} %get-tuple-element.49), calls=%async_computation.1 | async-start | bytes 65536 | tf_op jit(solution)/shard_map/all_to_all | solution.py:182
  78.7 4.0 %collective-permute-start.21 = (f32[1,128]{1,0:T(1,128)S(1)}, f32[1,128]{1,0:T(1,128)S(1)}, u32[]{:S(2)}, u32[]{:S(2)}) collective-permute-start(f32[1,128]{1,0:T(1,128)S(1)} %get-tuple-element.53.token0), channel_id=1, source_target_pairs={{0,64},{64,0},{128,192},{192,128},{1,65},{65,1},{129,193},{193,129... | collective-permute-start | bytes 1544 | tf_op jit(solution)/shard_map/ppermute | solution.py:186
  80.0 3.9 %collective-permute-start.22 = (f32[1,128]{1,0:T(1,128)S(1)}, f32[1,128]{1,0:T(1,128)S(1)}, u32[]{:S(2)}, u32[]{:S(2)}) collective-permute-start(f32[1,128]{1,0:T(1,128)S(1)} %get-tuple-element.53.token0), channel_id=1, source_target_pairs={{0,128},{64,192},{128,0},{192,64},{1,129},{65,193},{129,1},{193,65... | collective-permute-start | bytes 1544 | tf_op jit(solution)/shard_map/ppermute | solution.py:186
  82.7 3.6 %collective-permute-start.23 = (f32[1,128]{1,0:T(1,128)S(1)}, f32[1,128]{1,0:T(1,128)S(1)}, u32[]{:S(2)}, u32[]{:S(2)}) collective-permute-start(f32[1,128]{1,0:T(1,128)S(1)} %get-tuple-element.53.token0), channel_id=1, source_target_pairs={{0,192},{64,128},{128,64},{192,0},{1,193},{65,129},{129,65},{193,1... | collective-permute-start | bytes 1544 | tf_op jit(solution)/shard_map/ppermute | solution.py:186
